TPU v7x, 256 devices: a whole 4x4x8 slice. The times are simulated.
256 devices in a mesh: tm: 32 (over z_lo, y, core), space: 8 (over x, z_hi).
Axes of the slice: x: 4, y: 4, z: 8 (z_hi: 2, z_lo: 4; z = z_hi * 4 + z_lo), core: 2. Of those that a mesh axis runs over, the one named last changes fastest.
Arguments:
- iterate: float32 [32, 4, 128, 64, 128], P('tm', None, 'space'), may hold values from -6 to 6
- right_side: float32 [32, 4, 128, 64, 128], P('tm', None, 'space'), may hold values from -6 to 6
- diffusivity: float32 [128, 64, 128], P('space'), may hold values from 0.5 to 2
- velocity: float32 [3], replicated, may hold values from -2 to 2
Outputs:
- next_iterate: float32 [32, 4, 128, 64, 128], P('tm', None, 'space')
All inputs are finite; a program needn't handle non-finite values.
Results may differ from a plain program's by a relative error of at most 0.0003.
Values sent between devices are 32-bit elements; how exact they have to be, the bound alone decides.
A program may use at most 128 MiB of HBM per device.

v0:
```python
import math

import jax
import jax.numpy as jnp
from jax import lax
from jax.sharding import PartitionSpec as P

NX = 128
NY = 128
NZ = 64


diffusion_number = 16.0
circulant_alpha = 0.1


def padded_2(block, sides, width):
    for axis, dim in sides:
        count = lax.axis_size(axis)
        forward = [(i, i + 1) for i in range(count - 1)]
        forward.append((count - 1, 0))
        backward = [(target, source) for source, target in forward]
        low = lax.ppermute(
            lax.slice_in_dim(block, block.shape[dim] - width, None, axis=dim), axis, forward
        )
        high = lax.ppermute(lax.slice_in_dim(block, 0, width, axis=dim), axis, backward)
        block = jnp.concatenate([low, block, high], axis=dim)
    return block


def passed_along(value, axis, steps):
    count = lax.axis_size(axis)
    leading, last = (max(0, -steps), min(count, count - steps))
    return lax.ppermute(value, axis, [(source, source + steps) for source in range(leading, last)])


def items_in_groups(array, axis, split_dim, concat_dim, work, item_dim, out_dim):
    items = jax.tree.leaves(array)[0].shape[item_dim]
    count = 2 if items % 2 == 0 else 1
    finished = []
    for k in range(count):
        group = jax.tree.map(
            lambda a: lax.slice_in_dim(
                a, k * (items // count), (k + 1) * (items // count), axis=item_dim
            ),
            array,
        )
        finished.append(
            work(
                lax.all_to_all(
                    group, axis, split_axis=split_dim, concat_axis=concat_dim, tiled=True
                )
            )
        )
    return jax.tree.map(lambda *parts: jnp.concatenate(parts, axis=out_dim), *finished)


def collocation_matrix():
    radau_nodes = [0.08858795951270394, 0.4094668644407347, 0.7876594617608471, 1.0]
    matrix = [[0.0] * 4 for row_index in range(4)]
    for column_index in range(4):
        coefficients = [1.0]
        for other_index in range(4):
            if other_index != column_index:
                scale_value = 1.0 / (radau_nodes[column_index] - radau_nodes[other_index])
                shifted = [0.0] + [value * scale_value for value in coefficients]
                lowered = [
                    -radau_nodes[other_index] * scale_value * value for value in coefficients
                ] + [0.0]
                coefficients = [
                    left_value + right_value for left_value, right_value in zip(shifted, lowered)
                ]
        for row_index in range(4):
            total = 0.0
            for power_index in range(len(coefficients)):
                total = total + coefficients[power_index] * radau_nodes[row_index] ** (
                    power_index + 1
                ) / (power_index + 1)
            matrix[row_index][column_index] = total
    return matrix


def solve_system(matrix, target):
    count = len(target)
    rows_list = [list(matrix[row_index]) + [target[row_index]] for row_index in range(count)]
    for column in range(count):
        best_row = column
        for candidate in range(column + 1, count):
            if abs(rows_list[candidate][column]) > abs(rows_list[best_row][column]):
                best_row = candidate
        saved_row = rows_list[column]
        rows_list[column] = rows_list[best_row]
        rows_list[best_row] = saved_row
        leader = rows_list[column][column]
        for other_row in range(count):
            if other_row != column:
                factor = rows_list[other_row][column] / leader
                rows_list[other_row] = [
                    left_value - factor * right_value
                    for left_value, right_value in zip(rows_list[other_row], rows_list[column])
                ]
    return [
        rows_list[row_index][count] / rows_list[row_index][row_index] for row_index in range(count)
    ]


def node_basis():
    matrix = collocation_matrix()
    helper = [[0.0] * 4 for row_index in range(4)]
    coefficients = [0.0, 0.0, 0.0, 0.0, 1.0]
    for order in range(1, 5):
        product = [
            [
                sum((matrix[row_index][inner] * helper[inner][column] for inner in range(4)))
                for column in range(4)
            ]
            for row_index in range(4)
        ]
        for row_index in range(4):
            product[row_index][row_index] = product[row_index][row_index] + coefficients[5 - order]
        helper = product
        trace_value = sum(
            (
                sum((matrix[row_index][inner] * helper[inner][row_index] for inner in range(4)))
                for row_index in range(4)
            )
        )
        coefficients[4 - order] = -trace_value / order
    roots_list = [(0.4 + 0.9j) ** power_index for power_index in range(4)]
    for sweep in range(400):
        for root_index in range(4):
            current = roots_list[root_index]
            numer = 0.0
            for power_index in range(4, -1, -1):
                numer = numer * current + coefficients[power_index]
            denom = 1.0
            for other_index in range(4):
                if other_index != root_index:
                    denom = denom * (current - roots_list[other_index])
            roots_list[root_index] = current - numer / denom
    vectors = [[0.0] * 4 for row_index in range(4)]
    for root_index in range(4):
        shifted = [
            [
                matrix[row_index][column] - (roots_list[root_index] if row_index == column else 0.0)
                for column in range(3)
            ]
            for row_index in range(3)
        ]
        target = [-matrix[row_index][3] for row_index in range(3)]
        parts = solve_system(shifted, target) + [1.0 + 0j]
        for row_index in range(4):
            vectors[row_index][root_index] = parts[row_index]
    inverse = [[0.0] * 4 for row_index in range(4)]
    for column in range(4):
        unit = [1.0 if row_index == column else 0.0 for row_index in range(4)]
        parts = solve_system(vectors, unit)
        for row_index in range(4):
            inverse[row_index][column] = parts[row_index]
    weights = [sum((inverse[row_index][column] for column in range(4))) for row_index in range(4)]
    return (roots_list, vectors, inverse, weights)


def dft_tables(length):
    indices = jnp.arange(length, dtype=jnp.int32)
    phases = indices[:, None] * indices[None, :] % length
    angles = phases.astype(jnp.float32) * (2.0 * math.pi / length)
    return (jnp.cos(angles), jnp.sin(angles))


def half_tables(length):
    rows_index = jnp.arange(length // 2, dtype=jnp.int32)
    cells_index = jnp.arange(length, dtype=jnp.int32)
    phases = rows_index[:, None] * cells_index[None, :] % length
    angles = phases.astype(jnp.float32) * (2.0 * math.pi / length)
    return (jnp.cos(angles), jnp.sin(angles))


def alternating(length):
    return 1.0 - 2.0 * (jnp.arange(length, dtype=jnp.int32) % 2).astype(jnp.float32)


def contract(table_values, values, position):
    letters = "abcde"
    source = letters[: values.ndim]
    target = source[:position] + "k" + source[position + 1 :]
    return jnp.einsum(
        "k" + source[position] + "," + source + "->" + target,
        table_values,
        values,
        precision=lax.Precision.HIGHEST,
    )


def complex_dft(pieces, position, inverse):
    length = pieces[0].shape[position]
    cosine, sine_table = dft_tables(length)
    real_cos = contract(cosine, pieces[0], position)
    real_sin = contract(sine_table, pieces[0], position)
    imag_cos = contract(cosine, pieces[1], position)
    imag_sin = contract(sine_table, pieces[1], position)
    if inverse:
        return ((real_cos - imag_sin) / length, (imag_cos + real_sin) / length)
    return (real_cos + imag_sin, imag_cos - real_sin)


def transform(stacked, position, inverse):
    real_out, imag_out = complex_dft((stacked[0], stacked[1]), position, inverse)
    return jnp.stack((real_out, imag_out))


def half_forward(values):
    length = values.shape[4]
    cosine, sine_table = half_tables(length)
    nyquist = jnp.sum(values * alternating(length), axis=4, keepdims=True)
    real_part = jnp.concatenate([contract(cosine, values, 4), nyquist], axis=4)
    imag_part = jnp.concatenate([-contract(sine_table, values, 4), jnp.zeros_like(nyquist)], axis=4)
    return jnp.stack((real_part, imag_part))


def real_part_inverse(pieces, position):
    length = pieces[0].shape[position]
    cosine, sine_table = dft_tables(length)
    return (
        contract(cosine, pieces[0], position) - contract(sine_table, pieces[1], position)
    ) / length


def half_inverse(pieces):
    main_real = pieces[0][..., :-1]
    main_imag = pieces[1][..., :-1]
    nyquist = pieces[0][..., -1:]
    length = 2 * main_real.shape[4]
    cosine, sine_table = half_tables(length)
    doubling = jnp.where(jnp.arange(length // 2, dtype=jnp.int32) == 0, 1.0, 2.0).astype(
        jnp.float32
    )[:, None]
    total = contract(jnp.transpose(doubling * cosine), main_real, 4) - contract(
        jnp.transpose(doubling * sine_table), main_imag, 4
    )
    return (total + nyquist * alternating(length)) / length


def spatial_operator(padded, diffusivity, velocity):
    center = padded[:, :, 1:-1]
    upper_x = padded[:, :, 2:]
    lower_x = padded[:, :, :-2]
    upper_z = jnp.roll(center, -1, axis=3)
    lower_z = jnp.roll(center, 1, axis=3)
    upper_y = jnp.roll(center, -1, axis=4)
    lower_y = jnp.roll(center, 1, axis=4)
    laplace = upper_x + lower_x + (upper_z + lower_z) + (upper_y + lower_y) - 6.0 * center
    transport = (
        velocity[0] * (upper_x - lower_x)
        + velocity[1] * (upper_y - lower_y)
        + velocity[2] * (upper_z - lower_z)
    )
    return diffusion_number * diffusivity * laplace - 0.5 * transport


def mode_symbol(wave_x, wave_z, wave_y, velocity):
    theta_x = wave_x.astype(jnp.float32) * (2.0 * math.pi / NX)
    theta_z = wave_z.astype(jnp.float32) * (2.0 * math.pi / NZ)
    theta_y = wave_y.astype(jnp.float32) * (2.0 * math.pi / NY)
    symbol_real = diffusion_number * (
        2.0 * jnp.cos(theta_x)[:, None, None]
        - 2.0
        + (2.0 * jnp.cos(theta_z)[None, :, None] - 2.0)
        + (2.0 * jnp.cos(theta_y)[None, None, :] - 2.0)
    )
    symbol_imag = -(
        velocity[0] * jnp.sin(theta_x)[:, None, None]
        + velocity[1] * jnp.sin(theta_y)[None, None, :]
        + velocity[2] * jnp.sin(theta_z)[None, :, None]
    )
    return (symbol_real, symbol_imag)


def solve_modes(pieces, frequency, wave_x, wave_z, wave_y, velocity, gamma_base, step_count):
    symbol_real, symbol_imag = mode_symbol(wave_x, wave_z, wave_y, velocity)
    values, vectors, inverse, weights = node_basis()
    damp_real = []
    damp_imag = []
    for node_index in range(4):
        eigen_real = float(complex(values[node_index]).real)
        eigen_imag = float(complex(values[node_index]).imag)
        denom_real = 1.0 - (symbol_real * eigen_real - symbol_imag * eigen_imag)
        denom_imag = -(symbol_real * eigen_imag + symbol_imag * eigen_real)
        magnitude = denom_real * denom_real + denom_imag * denom_imag
        damp_real.append(denom_real / magnitude)
        damp_imag.append(-denom_imag / magnitude)
    inner_real = []
    inner_imag = []
    for node_index in range(4):
        total_real = jnp.zeros_like(pieces[0][:, 0])
        total_imag = jnp.zeros_like(pieces[0][:, 0])
        for other_index in range(4):
            coef_real = float(complex(inverse[node_index][other_index]).real)
            coef_imag = float(complex(inverse[node_index][other_index]).imag)
            total_real = total_real + (
                coef_real * pieces[0][:, other_index] - coef_imag * pieces[1][:, other_index]
            )
            total_imag = total_imag + (
                coef_real * pieces[1][:, other_index] + coef_imag * pieces[0][:, other_index]
            )
        inner_real.append(total_real * damp_real[node_index] - total_imag * damp_imag[node_index])
        inner_imag.append(total_real * damp_imag[node_index] + total_imag * damp_real[node_index])
    image_real = []
    image_imag = []
    ones_real = []
    ones_imag = []
    for row_index in range(4):
        total_real = jnp.zeros_like(inner_real[0])
        total_imag = jnp.zeros_like(inner_real[0])
        unit_real = jnp.zeros_like(damp_real[0])
        unit_imag = jnp.zeros_like(damp_real[0])
        for node_index in range(4):
            coef_real = float(complex(vectors[row_index][node_index]).real)
            coef_imag = float(complex(vectors[row_index][node_index]).imag)
            total_real = total_real + (
                coef_real * inner_real[node_index] - coef_imag * inner_imag[node_index]
            )
            total_imag = total_imag + (
                coef_real * inner_imag[node_index] + coef_imag * inner_real[node_index]
            )
            joint = complex(vectors[row_index][node_index]) * complex(weights[node_index])
            joint_real = float(joint.real)
            joint_imag = float(joint.imag)
            unit_real = unit_real + (
                joint_real * damp_real[node_index] - joint_imag * damp_imag[node_index]
            )
            unit_imag = unit_imag + (
                joint_real * damp_imag[node_index] + joint_imag * damp_real[node_index]
            )
        image_real.append(total_real)
        image_imag.append(total_imag)
        ones_real.append(unit_real)
        ones_imag.append(unit_imag)
    phase = frequency.astype(jnp.float32) * (2.0 * math.pi / step_count)
    shift_real = (gamma_base * jnp.cos(phase))[:, None, None, None]
    shift_imag = (-gamma_base * jnp.sin(phase))[:, None, None, None]
    numer_real = shift_real * image_real[3] - shift_imag * image_imag[3]
    numer_imag = shift_real * image_imag[3] + shift_imag * image_real[3]
    lower_real = 1.0 - (shift_real * ones_real[3] - shift_imag * ones_imag[3])
    lower_imag = -(shift_real * ones_imag[3] + shift_imag * ones_real[3])
    lower_size = lower_real * lower_real + lower_imag * lower_imag
    factor_real = (numer_real * lower_real + numer_imag * lower_imag) / lower_size
    factor_imag = (numer_imag * lower_real - numer_real * lower_imag) / lower_size
    solved_real = []
    solved_imag = []
    for row_index in range(4):
        solved_real.append(
            image_real[row_index]
            + ones_real[row_index] * factor_real
            - ones_imag[row_index] * factor_imag
        )
        solved_imag.append(
            image_imag[row_index]
            + ones_real[row_index] * factor_imag
            + ones_imag[row_index] * factor_real
        )
    return jnp.stack((jnp.stack(solved_real, axis=1), jnp.stack(solved_imag, axis=1)))


def solve_every(stacked, frequency, wave_x, wave_z, velocity, gamma_base, step_count):
    wave_y = jnp.arange(stacked.shape[5], dtype=jnp.int32)
    return solve_modes(
        (stacked[0], stacked[1]),
        frequency,
        wave_x,
        wave_z,
        wave_y,
        velocity,
        gamma_base,
        step_count,
    )


def along_x(stacked):
    return transform(stacked, 2, False)


def along_steps(stacked):
    return transform(stacked, 0, False)


def inverse_x(stacked):
    return transform(stacked, 2, True)


def to_grid(stacked):
    pieces = complex_dft((stacked[0], stacked[1]), 3, True)
    if pieces[0].shape[4] == NY:
        return real_part_inverse(pieces, 4)
    return half_inverse(pieces)


def shards(iterate, right_side, diffusivity, velocity):
    padded = padded_2(iterate, (("space", 2),), 1)
    previous = passed_along(iterate[:, 3], "tm", 1)
    applied = spatial_operator(padded, diffusivity, velocity)
    collocation = jnp.asarray(collocation_matrix(), jnp.float32)
    coupled = jnp.einsum("mn,snxzy->smxzy", collocation, applied, precision=lax.Precision.HIGHEST)
    residual = right_side - iterate + coupled + previous[:, None]
    step_count = lax.axis_size("tm")
    gamma_base = circulant_alpha ** (1.0 / step_count)
    step_power = lax.axis_index("tm").astype(jnp.float32)
    step_scale = jnp.power(jnp.float32(gamma_base), step_power)
    stacked = half_forward(residual * step_scale)
    stacked = transform(stacked, 3, False)
    stacked = items_in_groups(stacked, "space", 4, 3, along_x, 2, 2)
    stacked = items_in_groups(stacked, "tm", 3, 1, along_steps, 2, 2)
    x_count = stacked.shape[3]
    z_count = stacked.shape[4]
    frequency = jnp.arange(step_count, dtype=jnp.int32)
    wave_x = lax.axis_index("tm") * x_count + jnp.arange(x_count, dtype=jnp.int32)
    wave_z = lax.axis_index("space") * z_count + jnp.arange(z_count, dtype=jnp.int32)
    solved = solve_every(stacked, frequency, wave_x, wave_z, velocity, gamma_base, step_count)
    solved = transform(solved, 0, True)
    solved = items_in_groups(solved, "tm", 1, 3, inverse_x, 2, 2)
    correction = items_in_groups(solved, "space", 3, 4, to_grid, 2, 1)
    unscale = jnp.power(jnp.float32(gamma_base), -step_power)
    return iterate + correction * unscale


def solution(mesh):
    placed = (
        P("tm", None, "space", None, None),
        P("tm", None, "space", None, None),
        P("space", None, None),
        P(),
    )
    return jax.shard_map(
        shards,
        mesh=mesh,
        in_specs=placed,
        out_specs=P("tm", None, "space", None, None),
        check_vma=False,
    )
```

profile of v0, /device:TPU:64, one launch (start us, length us, event | category | flops | bytes accessed | tf_op | source)
XLA Modules:
  0.0 568.5 jit_solution(2019130616099487964)
XLA Ops:
  0.0 1.7 fusion.451
  1.7 7.6 %collective-permute-start = (f32[1,4,1,64,128]{4,3,2,1,0:T(8,128)}, f32[1,4,1,64,128]{4,3,2,1,0:T(8,128)S(1)}, u32[]{:S(2)}, u32[]{:S(2)}) collective-permute-start(f32[1,4,1,64,128]{4,3,2,1,0:T(8,128)} %get-tuple-element.52), channel_id=1, source_target_pairs={{1,0},{2,1},{3,2},{4,3},{5,4},{6,5},{7,6},{0,7},{9,8},{10,9},{11,1... | collective-permute-start | bytes 393224 | tf_op jit(solution)/shard_map/ppermute | solution.py:26
  9.3 1.9 slice_bitcast_fusion.22
  11.2 2.0 collective-permute-start.2
  13.2 5.1 fusion.452
  18.3 2.9 fusion.454
  21.1 2.9 fusion.455
  24.9 7.9 %subtract_bitcast_fusion.1 = f32[4,16,64,128]{3,2,1,0:T(8,128)S(1)} fusion(f32[1,4,16,64,128]{4,3,2,1,0:T(8,128)S(1)} %copy-done, f32[1,4,16,64,127]{4,3,2,1,0:T(8,128)} %get-tuple-element.58, f32[1,4,16,64,1]{4,3,2,1,0:T(8,128)} %get-tuple-element.60, f32[1,4,16,64,1]{4,3,2,1,0:T(8,128)} %get-tuple-element.59, f32[1,4,16,64,127]{4,3,2,1,0:T(8,128)} %get-tuple-element.57, ...), kind=kLoop, calls=%fused_computation.42 | loop fusion | flops 12582912 | bytes 13369356 | tf_op jit(solution)/shard_map/reshape.1
  32.8 7.7 %multiply_reduce_fusion = (f32[4,16,64]{0,2,1:T(8,128)S(1)}, f32[1,4,16,64,128]{4,1,3,2,0:T(4,128)S(1)}) fusion(f32[128]{0:T(128)S(1)} %fusion.251, f32[]{:T(128)S(6)} %pow.6, f32[16,64,128]{2,1,0:T(8,128)S(1)} %bitcast.381, f32[1,4,16,64,128]{4,3,2,1,0:T(8,128)S(1)} %copy-done, f32[1,4,16,64,128]{4,3,2,1,0:T(8,128)S(1)} %copy-done.9, ...), kind=kOutput, calls=%fused_computation.41 | convolution fusion | flops 28307456 | bytes 8929860 | tf_op jit(solution)/shard_map/mn,snxzy->smxzy/dot_general | solution.py:403
  40.5 3.3 fusion.17
  43.7 3.3 negate_bitcast_fusion
  47.0 8.6 %copy.64 = f32[1,4,16,64,1]{4,3,2,1,0:T(8,128)} copy(f32[1,4,16,64,1]{1,3,2,4,0:T(8,128)S(1)} %bitcast.380) | data formatting | bytes 32768 | tf_op jit(solution)/shard_map/broadcast_in_dim | solution.py:215
  55.6 4.8 fusion.84
  60.4 2.5 fusion.85
  62.9 2.5 subtract_bitcast_fusion
  65.5 2.2 add_bitcast_fusion
  67.7 2.0 fusion.1
  69.7 2.5 copy.66
  72.2 9.3 %all-to-all-start = ((f32[2,1,2,16,64,65]{5,3,2,1,0,4:T(8,128)}), f32[2,1,2,16,64,65]{5,3,2,1,0,4:T(8,128)}, u32[]{:S(2)}, u32[]{:S(2)}) async-start(f32[2,1,2,16,64,65]{5,3,2,1,0,4:T(8,128)} %copy.66), calls=%async_computation | async-start | bytes 4194304 | tf_op jit(solution)/shard_map/all_to_all | solution.py:50
  81.6 4.1 copy.75
  85.7 50.5 %all-to-all-done = f32[2,1,2,16,64,65]{5,3,2,1,0,4:T(8,128)} async-done(((f32[2,1,2,16,64,65]{5,3,2,1,0,4:T(8,128)}), f32[2,1,2,16,64,65]{5,3,2,1,0,4:T(8,128)}, u32[]{:S(2)}, u32[]{:S(2)}) %all-to-all-start) | async-done | bytes 1064992 | tf_op jit(solution)/shard_map/all_to_all | solution.py:50
  136.2 4.6 all-to-all-start.2
  140.9 2.8 copy.180
  146.8 1.6 copy.69
  151.9 2.1 copy.72
  154.0 18.8 %all-to-all-done.2 = f32[2,1,2,16,64,65]{5,3,2,1,0,4:T(8,128)} async-done(((f32[2,1,2,16,64,65]{5,3,2,1,0,4:T(8,128)}), f32[2,1,2,16,64,65]{5,3,2,1,0,4:T(8,128)}, u32[]{:S(2)}, u32[]{:S(2)}) %all-to-all-start.2) | async-done | bytes 1064992 | tf_op jit(solution)/shard_map/all_to_all | solution.py:50
  172.8 25.9 %all-to-all-start.1 = ((f32[2,1,2,128,8,65]{5,4,2,1,0,3:T(8,128)}), f32[2,1,2,128,8,65]{5,4,2,1,0,3:T(8,128)}, u32[]{:S(2)}, u32[]{:S(2)}) async-start(f32[2,1,2,128,8,65]{5,4,2,1,0,3:T(8,128)} %copy.72), calls=%async_computation.1 | async-start | bytes 4194304 | tf_op jit(solution)/shard_map/all_to_all | solution.py:50
  198.7 2.8 copy.179
  204.6 1.6 copy.78
  209.8 1.9 copy.81
  211.7 34.5 %all-to-all-done.1 = f32[2,1,2,128,8,65]{5,4,2,1,0,3:T(8,128)} async-done(((f32[2,1,2,128,8,65]{5,4,2,1,0,3:T(8,128)}), f32[2,1,2,128,8,65]{5,4,2,1,0,3:T(8,128)}, u32[]{:S(2)}, u32[]{:S(2)}) %all-to-all-start.1) | async-done | bytes 1064992 | tf_op jit(solution)/shard_map/all_to_all | solution.py:50
  246.3 7.0 %all-to-all-start.3 = ((f32[2,1,2,128,8,65]{5,4,2,1,0,3:T(8,128)}), f32[2,1,2,128,8,65]{5,4,2,1,0,3:T(8,128)}, u32[]{:S(2)}, u32[]{:S(2)}) async-start(f32[2,1,2,128,8,65]{5,4,2,1,0,3:T(8,128)} %copy.81), calls=%async_computation.3 | async-start | bytes 4194304 | tf_op jit(solution)/shard_map/all_to_all | solution.py:50
  255.6 2.8 copy.178
  258.5 2.1 fusion.72
  261.7 39.1 %all-to-all-done.3 = f32[2,1,2,128,8,65]{5,4,2,1,0,3:T(8,128)} async-done(((f32[2,1,2,128,8,65]{5,4,2,1,0,3:T(8,128)}), f32[2,1,2,128,8,65]{5,4,2,1,0,3:T(8,128)}, u32[]{:S(2)}, u32[]{:S(2)}) %all-to-all-start.3) | async-done | bytes 1064992 | tf_op jit(solution)/shard_map/all_to_all | solution.py:50
  300.8 2.8 copy.177
  314.1 1.6 multiply_subtract_fusion.3
  315.8 2.7 multiply_subtract_fusion.2
  318.5 2.0 fusion.56
  320.4 2.0 fusion.57
  322.4 2.1 multiply_bitcast_fusion
  324.6 2.1 multiply_bitcast_fusion.1
  326.7 2.1 fusion
  328.8 2.5 copy.84
  331.3 6.8 %all-to-all-start.4 = ((f32[2,32,2,4,8,65]{5,4,3,2,0,1:T(8,128)}), f32[2,32,2,4,8,65]{5,4,3,2,0,1:T(8,128)}, u32[]{:S(2)}, u32[]{:S(2)}) async-start(f32[2,32,2,4,8,65]{5,4,3,2,0,1:T(8,128)} %copy.84), calls=%async_computation.4 | async-start | bytes 4194304 | tf_op jit(solution)/shard_map/all_to_all | solution.py:50
  338.1 4.1 copy.95
  342.2 43.6 %all-to-all-done.4 = f32[2,32,2,4,8,65]{5,4,3,2,0,1:T(8,128)} async-done(((f32[2,32,2,4,8,65]{5,4,3,2,0,1:T(8,128)}), f32[2,32,2,4,8,65]{5,4,3,2,0,1:T(8,128)}, u32[]{:S(2)}, u32[]{:S(2)}) %all-to-all-start.4) | async-done | bytes 1064992 | tf_op jit(solution)/shard_map/all_to_all | solution.py:50
  385.8 6.8 %all-to-all-start.6 = ((f32[2,32,2,4,8,65]{5,4,3,2,0,1:T(8,128)}), f32[2,32,2,4,8,65]{5,4,3,2,0,1:T(8,128)}, u32[]{:S(2)}, u32[]{:S(2)}) async-start(f32[2,32,2,4,8,65]{5,4,3,2,0,1:T(8,128)} %copy.95), calls=%async_computation.6 | async-start | bytes 4194304 | tf_op jit(solution)/shard_map/all_to_all | solution.py:50
  392.6 2.8 fusion.446
  398.1 2.3 copy.87
  405.6 2.1 copy.91
  407.6 32.7 %all-to-all-done.6 = f32[2,32,2,4,8,65]{5,4,3,2,0,1:T(8,128)} async-done(((f32[2,32,2,4,8,65]{5,4,3,2,0,1:T(8,128)}), f32[2,32,2,4,8,65]{5,4,3,2,0,1:T(8,128)}, u32[]{:S(2)}, u32[]{:S(2)}) %all-to-all-start.6) | async-done | bytes 1064992 | tf_op jit(solution)/shard_map/all_to_all | solution.py:50
  440.3 4.4 all-to-all-start.5
  444.7 2.8 fusion.448
  450.2 2.3 copy.98
  457.7 1.9 copy.102
  459.6 39.0 %all-to-all-done.5 = f32[2,1,2,128,8,65]{5,4,2,1,0,3:T(8,128)} async-done(((f32[2,1,2,128,8,65]{5,4,2,1,0,3:T(8,128)}), f32[2,1,2,128,8,65]{5,4,2,1,0,3:T(8,128)}, u32[]{:S(2)}, u32[]{:S(2)}) %all-to-all-start.5) | async-done | bytes 1064992 | tf_op jit(solution)/shard_map/all_to_all | solution.py:50
  498.6 25.6 %all-to-all-start.7 = ((f32[2,1,2,128,8,65]{5,4,2,1,0,3:T(8,128)}), f32[2,1,2,128,8,65]{5,4,2,1,0,3:T(8,128)}, u32[]{:S(2)}, u32[]{:S(2)}) async-start(f32[2,1,2,128,8,65]{5,4,2,1,0,3:T(8,128)} %copy.102), calls=%async_computation.7 | async-start | bytes 4194304 | tf_op jit(solution)/shard_map/all_to_all | solution.py:50
  524.3 1.7 copy.92
  529.2 2.1 fusion.66
  531.4 2.1 fusion.59
  533.4 20.7 %all-to-all-done.7 = f32[2,1,2,128,8,65]{5,4,2,1,0,3:T(8,128)} async-done(((f32[2,1,2,128,8,65]{5,4,2,1,0,3:T(8,128)}), f32[2,1,2,128,8,65]{5,4,2,1,0,3:T(8,128)}, u32[]{:S(2)}, u32[]{:S(2)}) %all-to-all-start.7) | async-done | bytes 1064992 | tf_op jit(solution)/shard_map/all_to_all | solution.py:50
  554.2 1.7 copy.103
  566.5 1.8 fusion.2
  (100 shorter events, 57.2 us)
Async XLA Ops:
  1.7 23.1 %collective-permute-start = (f32[1,4,1,64,128]{4,3,2,1,0:T(8,128)}, f32[1,4,1,64,128]{4,3,2,1,0:T(8,128)S(1)}, u32[]{:S(2)}, u32[]{:S(2)}) collective-permute-start(f32[1,4,1,64,128]{4,3,2,1,0:T(8,128)} %get-tuple-element.52), channel_id=1, source_target_pairs={{1,0},{2,1},{3,2},{4,3},{5,4},{6,5},{7,6},{0,7},{9,8},{10,9},{11,1... | collective-permute-start | bytes 393224 | tf_op jit(solution)/shard_map/ppermute | solution.py:26
  9.3 15.6 %collective-permute-start.1 = (f32[1,4,1,64,128]{4,3,2,1,0:T(8,128)}, f32[1,4,1,64,128]{4,3,2,1,0:T(8,128)S(1)}, u32[]{:S(2)}, u32[]{:S(2)}) collective-permute-start(f32[1,4,1,64,128]{4,3,2,1,0:T(8,128)} %get-tuple-element.51), channel_id=1, source_target_pairs={{0,1},{1,2},{2,3},{3,4},{4,5},{5,6},{6,7},{7,0},{8,9},{9,10},{10,1... | collective-permute-start | bytes 393224 | tf_op jit(solution)/shard_map/ppermute | solution.py:23
  11.2 7.1 %copy-start = (f32[1,4,16,64,128]{4,3,2,1,0:T(8,128)S(1)}, f32[1,4,16,64,128]{4,3,2,1,0:T(8,128)}, u32[]{:S(2)}) copy-start(f32[1,4,16,64,128]{4,3,2,1,0:T(8,128)} %param.5) | copy-start | bytes 6291460
  11.2 21.6 %collective-permute-start.2 = (f32[1,16,64,128]{3,2,1,0:T(8,128)}, f32[1,16,64,128]{3,2,1,0:T(8,128)S(1)}, u32[]{:S(2)}, u32[]{:S(2)}) collective-permute-start(f32[1,16,64,128]{3,2,1,0:T(8,128)} %slice_bitcast_fusion.22), channel_id=1, source_target_pairs={{0,8},{8,16},{16,24},{24,32},{32,40},{40,48},{48,56},{56,64},{64,7... | collective-permute-start | bytes 1572872 | tf_op jit(solution)/shard_map/ppermute | solution.py:34
  21.1 2.9 copy-start.10
  21.1 3.1 copy-start.11
  24.8 7.9 %copy-start.9 = (f32[1,4,16,64,128]{4,3,2,1,0:T(8,128)S(1)}, f32[1,4,16,64,128]{4,3,2,1,0:T(8,128)}, u32[]{:S(2)}) copy-start(f32[1,4,16,64,128]{4,3,2,1,0:T(8,128)} %param.6) | copy-start | bytes 6291460
  24.8 7.9 %copy-start.12 = (f32[4,4,1,1]{1,0,3,2:T(4,128)S(1)}, f32[4,4,1,1]{1,0,3,2:T(4,128)}, u32[]{:S(2)}) copy-start(f32[4,4,1,1]{1,0,3,2:T(4,128)} %constant.337) | copy-start | bytes 196
  55.6 4.9 copy-start.1
  55.6 4.9 copy-start.3
  60.4 2.5 copy-start.2
  72.2 64.0 %all-to-all-start = ((f32[2,1,2,16,64,65]{5,3,2,1,0,4:T(8,128)}), f32[2,1,2,16,64,65]{5,3,2,1,0,4:T(8,128)}, u32[]{:S(2)}, u32[]{:S(2)}) async-start(f32[2,1,2,16,64,65]{5,3,2,1,0,4:T(8,128)} %copy.66), calls=%async_computation | async-start | bytes 4194304 | tf_op jit(solution)/shard_map/all_to_all | solution.py:50
  136.2 36.5 %all-to-all-start.2 = ((f32[2,1,2,16,64,65]{5,3,2,1,0,4:T(8,128)}), f32[2,1,2,16,64,65]{5,3,2,1,0,4:T(8,128)}, u32[]{:S(2)}, u32[]{:S(2)}) async-start(f32[2,1,2,16,64,65]{5,3,2,1,0,4:T(8,128)} %copy.75), calls=%async_computation.2 | async-start | bytes 4194304 | tf_op jit(solution)/shard_map/all_to_all | solution.py:50
  172.8 73.5 %all-to-all-start.1 = ((f32[2,1,2,128,8,65]{5,4,2,1,0,3:T(8,128)}), f32[2,1,2,128,8,65]{5,4,2,1,0,3:T(8,128)}, u32[]{:S(2)}, u32[]{:S(2)}) async-start(f32[2,1,2,128,8,65]{5,4,2,1,0,3:T(8,128)} %copy.72), calls=%async_computation.1 | async-start | bytes 4194304 | tf_op jit(solution)/shard_map/all_to_all | solution.py:50
  246.3 54.5 %all-to-all-start.3 = ((f32[2,1,2,128,8,65]{5,4,2,1,0,3:T(8,128)}), f32[2,1,2,128,8,65]{5,4,2,1,0,3:T(8,128)}, u32[]{:S(2)}, u32[]{:S(2)}) async-start(f32[2,1,2,128,8,65]{5,4,2,1,0,3:T(8,128)} %copy.81), calls=%async_computation.3 | async-start | bytes 4194304 | tf_op jit(solution)/shard_map/all_to_all | solution.py:50
  258.5 2.1 copy-start.4
  303.6 2.2 copy-start.5
  303.6 2.2 copy-start.7
  331.3 54.5 %all-to-all-start.4 = ((f32[2,32,2,4,8,65]{5,4,3,2,0,1:T(8,128)}), f32[2,32,2,4,8,65]{5,4,3,2,0,1:T(8,128)}, u32[]{:S(2)}, u32[]{:S(2)}) async-start(f32[2,32,2,4,8,65]{5,4,3,2,0,1:T(8,128)} %copy.84), calls=%async_computation.4 | async-start | bytes 4194304 | tf_op jit(solution)/shard_map/all_to_all | solution.py:50
  385.8 54.5 %all-to-all-start.6 = ((f32[2,32,2,4,8,65]{5,4,3,2,0,1:T(8,128)}), f32[2,32,2,4,8,65]{5,4,3,2,0,1:T(8,128)}, u32[]{:S(2)}, u32[]{:S(2)}) async-start(f32[2,32,2,4,8,65]{5,4,3,2,0,1:T(8,128)} %copy.95), calls=%async_computation.6 | async-start | bytes 4194304 | tf_op jit(solution)/shard_map/all_to_all | solution.py:50
  440.3 58.3 %all-to-all-start.5 = ((f32[2,1,2,128,8,65]{5,4,2,1,0,3:T(8,128)}), f32[2,1,2,128,8,65]{5,4,2,1,0,3:T(8,128)}, u32[]{:S(2)}, u32[]{:S(2)}) async-start(f32[2,1,2,128,8,65]{5,4,2,1,0,3:T(8,128)} %copy.91), calls=%async_computation.5 | async-start | bytes 4194304 | tf_op jit(solution)/shard_map/all_to_all | solution.py:50
  498.6 55.5 %all-to-all-start.7 = ((f32[2,1,2,128,8,65]{5,4,2,1,0,3:T(8,128)}), f32[2,1,2,128,8,65]{5,4,2,1,0,3:T(8,128)}, u32[]{:S(2)}, u32[]{:S(2)}) async-start(f32[2,1,2,128,8,65]{5,4,2,1,0,3:T(8,128)} %copy.102), calls=%async_computation.7 | async-start | bytes 4194304 | tf_op jit(solution)/shard_map/all_to_all | solution.py:50
  559.6 1.8 copy-start.6
  562.9 1.2 copy-start.8
where the time goes:
time: 576 us; the launch traced here: 569 us
  waiting for transfers between devices  279 us (48%)
  starting transfers between devices  99.9 us (17%)
  local copies, waits for them, and re-layouts  90 us (16%)
  matrix products  74.3 us (13%)
  other arithmetic  24.1 us (4%)
    all_to_all x8, waiting for transfers between devices, items_in_groups(): lax.all_to_all(group, axis, split_axis=split_dim, concat_axis=concat_dim,...  279 us
    all_to_all x8, starting transfers between devices, items_in_groups(): lax.all_to_all(group, axis, split_axis=split_dim, concat_axis=concat_dim,...  90.3 us
    dot_general x46, matrix products, contract(): jnp.einsum('k' + source[position] + ',' + source + '->' + target, table_v...  66.6 us
    all_to_all x6, local copies, waits for them, and re-layouts, items_in_groups(): lax.all_to_all(group, axis, split_axis=split_dim, concat_axis=concat_dim,...  14.7 us
    slice x4, local copies, waits for them, and re-layouts, items_in_groups(): lax.slice_in_dim(a, k * (items // count), (k + 1) * (items // count), axi...  13.4 us
    another operation x8, local copies, waits for them, and re-layouts  12.7 us
  transfers between devices with their start and end apart: 11, of which 8 were waited for; matrix products, arithmetic and copies ran while one was open for 18% of the time, Pallas kernels for 0%

commit v1 on v0

v1 whole, which is shorter than its diff:
```python
import functools
import math

import jax
import jax.numpy as jnp
import numpy as np
from jax import lax
from jax.experimental import pallas as pl
from jax.experimental.pallas import tpu as pltpu
from jax.sharding import PartitionSpec as P

NX, NY, NZ, STEPS = 128, 128, 64, 32
SLABS, WIDE = 8, 16
OWNERS = 64
ROWS = 24
MESH = pl.DeviceIdType.MESH
f32, bf16 = jnp.float32, jnp.bfloat16

diffusion_number = 16.0
circulant_alpha = 0.1


def collocation_matrix():
    radau_nodes = [0.08858795951270394, 0.4094668644407347, 0.7876594617608471, 1.0]
    matrix = [[0.0] * 4 for row_index in range(4)]
    for column_index in range(4):
        coefficients = [1.0]
        for other_index in range(4):
            if other_index != column_index:
                scale_value = 1.0 / (radau_nodes[column_index] - radau_nodes[other_index])
                shifted = [0.0] + [value * scale_value for value in coefficients]
                lowered = [
                    -radau_nodes[other_index] * scale_value * value for value in coefficients
                ] + [0.0]
                coefficients = [
                    left_value + right_value for left_value, right_value in zip(shifted, lowered)
                ]
        for row_index in range(4):
            total = 0.0
            for power_index in range(len(coefficients)):
                total = total + coefficients[power_index] * radau_nodes[row_index] ** (
                    power_index + 1
                ) / (power_index + 1)
            matrix[row_index][column_index] = total
    return matrix


def solve_system(matrix, target):
    count = len(target)
    rows_list = [list(matrix[row_index]) + [target[row_index]] for row_index in range(count)]
    for column in range(count):
        best_row = column
        for candidate in range(column + 1, count):
            if abs(rows_list[candidate][column]) > abs(rows_list[best_row][column]):
                best_row = candidate
        saved_row = rows_list[column]
        rows_list[column] = rows_list[best_row]
        rows_list[best_row] = saved_row
        leader = rows_list[column][column]
        for other_row in range(count):
            if other_row != column:
                factor = rows_list[other_row][column] / leader
                rows_list[other_row] = [
                    left_value - factor * right_value
                    for left_value, right_value in zip(rows_list[other_row], rows_list[column])
                ]
    return [
        rows_list[row_index][count] / rows_list[row_index][row_index] for row_index in range(count)
    ]


def node_basis():
    matrix = collocation_matrix()
    helper = [[0.0] * 4 for row_index in range(4)]
    coefficients = [0.0, 0.0, 0.0, 0.0, 1.0]
    for order in range(1, 5):
        product = [
            [
                sum((matrix[row_index][inner] * helper[inner][column] for inner in range(4)))
                for column in range(4)
            ]
            for row_index in range(4)
        ]
        for row_index in range(4):
            product[row_index][row_index] = product[row_index][row_index] + coefficients[5 - order]
        helper = product
        trace_value = sum(
            (
                sum((matrix[row_index][inner] * helper[inner][row_index] for inner in range(4)))
                for row_index in range(4)
            )
        )
        coefficients[4 - order] = -trace_value / order
    roots_list = [(0.4 + 0.9j) ** power_index for power_index in range(4)]
    for sweep in range(400):
        for root_index in range(4):
            current = roots_list[root_index]
            numer = 0.0
            for power_index in range(4, -1, -1):
                numer = numer * current + coefficients[power_index]
            denom = 1.0
            for other_index in range(4):
                if other_index != root_index:
                    denom = denom * (current - roots_list[other_index])
            roots_list[root_index] = current - numer / denom
    vectors = [[0.0] * 4 for row_index in range(4)]
    for root_index in range(4):
        shifted = [
            [
                matrix[row_index][column] - (roots_list[root_index] if row_index == column else 0.0)
                for column in range(3)
            ]
            for row_index in range(3)
        ]
        target = [-matrix[row_index][3] for row_index in range(3)]
        parts = solve_system(shifted, target) + [1.0 + 0j]
        for row_index in range(4):
            vectors[row_index][root_index] = parts[row_index]
    inverse = [[0.0] * 4 for row_index in range(4)]
    for column in range(4):
        unit = [1.0 if row_index == column else 0.0 for row_index in range(4)]
        parts = solve_system(vectors, unit)
        for row_index in range(4):
            inverse[row_index][column] = parts[row_index]
    weights = [sum((inverse[row_index][column] for column in range(4))) for row_index in range(4)]
    return (roots_list, vectors, inverse, weights)


VALUES, VECTORS, INVERSE, WEIGHTS = node_basis()
PAIRS = [m for m in range(4) if complex(VALUES[m]).imag > 0]
MU = [complex(VALUES[m]) for m in PAIRS]
COLUMN = [[complex(VECTORS[n][m]) for n in range(4)] for m in PAIRS]
ROW = [[complex(INVERSE[m][n]) for n in range(4)] for m in PAIRS]
EPS = [complex(WEIGHTS[m]) for m in PAIRS]


def wave_order(n):
    index = np.arange(n)
    return np.where(index <= n // 2, index, n + n // 2 - index)


def split(values):
    values = np.asarray(values, np.float64)
    high = values.astype(np.float32).astype(bf16)
    low = (values - high.astype(np.float64)).astype(np.float32).astype(bf16)
    return high, low


def side_table(values):
    high, low = split(values)
    return np.concatenate([high, high, low], axis=1)


def halves(x):
    high = x.astype(bf16)
    return high, (x - high.astype(f32)).astype(bf16)


def left_dot(table, x):
    high, low = halves(x)
    return jnp.dot(table, jnp.concatenate([high, low, high], axis=0), preferred_element_type=f32)


def right_dot(high, low, table_high, table_low):
    return (
        jnp.dot(high, table_high, preferred_element_type=f32)
        + jnp.dot(low, table_high, preferred_element_type=f32)
        + jnp.dot(high, table_low, preferred_element_type=f32)
    )


def complex_block(matrix):
    return np.block([[matrix.real, -matrix.imag], [matrix.imag, matrix.real]])


def make_tables():
    ky, kz = wave_order(NY), wave_order(NZ)
    kx, x = np.arange(NX), np.arange(NX)
    to_y = np.exp(-2j * np.pi * np.outer(ky, np.arange(NY)) / NY)
    to_z = np.exp(-2j * np.pi * np.outer(kz, np.arange(NZ)) / NZ)
    tables = {}
    tables["ty"] = np.stack(split(complex_block(to_y).T))
    tables["tz"] = side_table(complex_block(to_z))
    tables["uy"] = np.stack(split(complex_block(np.conj(to_y.T) / NY).T))
    tables["uz"] = side_table(complex_block(np.conj(to_z.T) / NZ))
    cells = (np.arange(SLABS)[:, None] * WIDE + np.arange(8)[None, :]).reshape(-1)
    theta = 2 * np.pi * kx / NX
    at = np.exp(-1j * np.outer(theta, cells))
    shifted = np.exp(-8j * theta)[:, None]
    from_own = at * (1 - 1j * shifted) / 2
    from_partner = at * (1 + 1j * shifted) / 2
    own = complex_block(from_own)
    partner = complex_block(from_partner) * np.concatenate([np.ones(64), -np.ones(64)])[None, :]
    tables["tg"] = side_table(np.concatenate([own, partner], axis=1))
    firsts = np.arange(SLABS) * WIDE
    start = np.exp(-1j * np.outer(theta, firsts))
    before = np.exp(-1j * np.outer(theta, firsts - 1))
    tables["td"] = side_table(np.concatenate([complex_block(start), complex_block(before)], axis=1))
    back = np.exp(1j * np.outer(cells, theta)) * (1 + 1j * np.exp(8j * theta))[None, :] / NX
    tables["tw"] = side_table(complex_block(back))
    ends = [complex_block(np.exp(1j * np.outer(firsts + k, theta)) / NX) for k in (0, 1, 15)]
    tables["tb"] = side_table(np.concatenate(ends, axis=0))
    trig_y = 2 * np.pi * ky / NY
    trig_z = 2 * np.pi * kz / NZ
    tables["lane"] = np.stack([np.cos(trig_y), np.sin(trig_y)]).astype(np.float32)
    tables["row"] = np.stack(
        [np.broadcast_to(v[:, None], (NZ, NY)) for v in (np.cos(trig_z), np.sin(trig_z))]
    ).astype(np.float32)
    tables["wave_x"] = np.stack(
        [np.broadcast_to(v[:, None], (NX, 128)) for v in (np.cos(theta), np.sin(theta))]
    ).astype(np.float32)
    lane = np.arange(128)
    second = (lane % 64) >= 32
    own_lane, own_row = [], []
    for owner in range(OWNERS):
        half, pair = owner // 32, owner % 32
        own_lane.append(trig_y[lane - 32 * second + 32 * half])
        own_row.append(trig_z[pair + 32 * second])
    own_lane, own_row = np.stack(own_lane), np.stack(own_row)
    tables["own"] = np.stack(
        [np.cos(own_lane), np.sin(own_lane), np.cos(own_row), np.sin(own_row)], axis=1
    ).astype(np.float32)
    return tables


TABLES = make_tables()


def times(a, b):
    return (a[0] * b[0] - a[1] * b[1], a[0] * b[1] + a[1] * b[0])


def plus(a, b):
    return (a[0] + b[0], a[1] + b[1])


def minus(a, b):
    return (a[0] - b[0], a[1] - b[1])


def scaled(number, a):
    return (number.real * a[0] - number.imag * a[1], number.real * a[1] + number.imag * a[0])


def inverse_of(a):
    size = 1.0 / (a[0] * a[0] + a[1] * a[1])
    return (a[0] * size, -a[1] * size)


def root_of(a):
    size = jnp.sqrt(a[0] * a[0] + a[1] * a[1])
    main = jnp.sqrt(0.5 * (size + jnp.abs(a[0])))
    other = a[1] / (2.0 * main)
    positive = a[0] >= 0.0
    return (
        jnp.where(positive, main, jnp.abs(other)),
        jnp.where(positive, other, jnp.where(a[1] >= 0.0, main, -main)),
    )


def cross_symbol(cos_y, sin_y, cos_z, sin_z, v1, v2):
    return (
        diffusion_number * ((2.0 * cos_y - 2.0) + (2.0 * cos_z - 2.0)),
        -(v1 * sin_y + v2 * sin_z),
    )


def factors(mu, cross, v0):
    c_up = -mu.real * (diffusion_number - 0.5 * v0), -mu.imag * (diffusion_number - 0.5 * v0)
    c_down = -mu.real * (diffusion_number + 0.5 * v0), -mu.imag * (diffusion_number + 0.5 * v0)
    moved = scaled(mu, cross)
    c_mid = (1.0 + 2.0 * diffusion_number * mu.real - moved[0], 2.0 * diffusion_number * mu.imag - moved[1])
    product = times(c_up, c_down)
    square = times(c_mid, c_mid)
    root = root_of((square[0] - 4.0 * product[0], square[1] - 4.0 * product[1]))
    same = c_mid[0] * root[0] + c_mid[1] * root[1] >= 0.0
    kappa = (
        0.5 * (c_mid[0] + jnp.where(same, root[0], -root[0])),
        0.5 * (c_mid[1] + jnp.where(same, root[1], -root[1])),
    )
    inv = inverse_of(kappa)
    p = times(inv, c_down)
    q = times(inv, c_up)
    return (-p[0], -p[1]), (-q[0], -q[1]), kappa, inv


def plane_partner(low, high, lane, first_row):
    ends = (lane == 0) | (lane == 64)

    def turned(v):
        return jnp.where(ends, v, pltpu.roll(v, 64, 1))

    low_turned, high_turned = [turned(v) for v in low], [turned(v) for v in high]
    to_low = [jnp.where(first_row, a, b) for a, b in zip(low_turned, high_turned)]
    to_high = [jnp.where(first_row, b, a) for a, b in zip(low_turned, high_turned)]
    return (to_low[0], -to_low[1]), (to_high[0], -to_high[1])


def chunk_factors(t, lane_ref, row_ref, velocity_ref, mu):
    cos_y, sin_y = lane_ref[0:1, :], lane_ref[1:2, :]
    found = []
    for base in (0, 32):
        rows = pl.ds(pl.multiple_of(base + 8 * t, 8), 8)
        cross = cross_symbol(
            cos_y, sin_y, row_ref[0, rows, :], row_ref[1, rows, :], velocity_ref[1], velocity_ref[2]
        )
        found.append([factors(number, cross, velocity_ref[0]) for number in mu])
    return found


def forward_kernel(
    velocity_ref, step_ref, iterate_ref, right_ref, kappa_ref, below_ref, above_ref,
    ty_ref, tz_ref, lane_ref, row_ref,
    u_ref, send_ref,
    high_ref, low_ref, spec_ref,
):
    v0, v1, v2 = velocity_ref[0], velocity_ref[1], velocity_ref[2]

    def put(at, real, imag):
        rows = pl.ds(pl.multiple_of(at * 64, 64), 64)
        for k, part in enumerate((real, imag)):
            high, low = halves(part)
            high_ref[rows, k * 128 : (k + 1) * 128] = high
            low_ref[rows, k * 128 : (k + 1) * 128] = low

    def combine(plain, applied, plane):
        for m in range(2):
            real = imag = None
            for n in range(4):
                c = ROW[m][n]
                d = MU[m] * c
                terms = [(d, applied[n])]
                if plain is not None:
                    terms.append((c, plain[n]))
                for factor, value in terms:
                    a, b = factor.real * value, factor.imag * value
                    real = a if real is None else real + a
                    imag = b if imag is None else imag + b
            put(m * 18 + plane, real, imag)

    def inner(x, below, above):
        plain, applied = [], []
        kappa = kappa_ref[x]
        for n in range(4):
            f = iterate_ref[n, x]
            up_z, down_z = pltpu.roll(f, NZ - 1, 0), pltpu.roll(f, 1, 0)
            up_y, down_y = pltpu.roll(f, NY - 1, 1), pltpu.roll(f, 1, 1)
            total = (up_z + down_z) + (up_y + down_y) - 6.0 * f
            moved = v1 * (up_y - down_y) + v2 * (up_z - down_z)
            if above:
                up_x = iterate_ref[n, x + 1]
                total, moved = total + up_x, moved + v0 * up_x
            if below:
                down_x = iterate_ref[n, x - 1]
                total, moved = total + down_x, moved - v0 * down_x
            applied.append((diffusion_number * kappa) * total - 0.5 * moved)
            plain.append(right_ref[n, x] - f)
        combine(plain, applied, x + 1)

    outer = diffusion_number * below_ref[...] - 0.5 * v0
    combine(None, [outer * iterate_ref[n, 0] for n in range(4)], 0)
    outer = diffusion_number * above_ref[...] + 0.5 * v0
    combine(None, [outer * iterate_ref[n, WIDE - 1] for n in range(4)], 17)
    inner(0, False, True)
    inner(WIDE - 1, True, False)

    @pl.loop(1, WIDE - 1)
    def _(x):
        inner(x, True, True)

    keep = jnp.where(step_ref[0] < STEPS - 1, 1.0, 0.0).astype(f32)

    @pl.loop(0, 8)
    def _(x):
        put(36 + x, keep * iterate_ref[3, x], keep * iterate_ref[3, x + 8])

    @pl.loop(0, 11)
    def _(block):
        rows = pl.ds(pl.multiple_of(block * 256, 256), 256)
        mid = right_dot(high_ref[rows, :], low_ref[rows, :], ty_ref[0], ty_ref[1])
        stacked = jnp.concatenate(
            [
                jnp.concatenate([mid[64 * k : 64 * k + 64, :128], mid[64 * k : 64 * k + 64, 128:]], axis=0)
                for k in range(4)
            ],
            axis=1,
        )
        out = left_dot(tz_ref[...], stacked)
        for k in range(4):
            spec_ref[block * 4 + k] = out[:, 128 * k : 128 * k + 128]

    lane = lax.broadcasted_iota(jnp.int32, (8, 128), 1)
    sub = lax.broadcasted_iota(jnp.int32, (8, 128), 0)
    narrow = (lane % 64) < 32

    @pl.loop(0, 4)
    def _(t):
        first_row = (sub + t) == 0
        found = chunk_factors(t, lane_ref, row_ref, velocity_ref, MU)
        bases = [pl.multiple_of(base + 8 * t, 8) for base in (0, 32)]

        def plane(at, base):
            return spec_ref[at, pl.ds(base, 8), :], spec_ref[at, pl.ds(base + 64, 8), :]

        def send(value, low, high):
            start = 8 * t * ROWS + value
            send_ref[pl.ds(start, 8, stride=ROWS), :] = jnp.where(narrow, low, pltpu.roll(high, 32, 1))
            send_ref[pl.ds(start + 32 * ROWS, 8, stride=ROWS), :] = jnp.where(
                narrow, pltpu.roll(low, 96, 1), high
            )

        sums = [[None, None] for x in range(WIDE)]
        for m in range(2):
            carries = []
            for half in range(2):
                base = bases[half]
                p, q, kappa, inv = found[half][m]
                under, over = plane(m * 18, base), plane(m * 18 + 17, base)
                u = plus(plane(m * 18 + 1, base), times(p, under))
                us = [u]
                for x in range(1, WIDE):
                    u = plus(plane(m * 18 + 1 + x, base), times(p, u))
                    us.append(u)
                for x in range(WIDE):
                    u_ref[m * 16 + x, pl.ds(base, 8), :] = us[x][0]
                    u_ref[m * 16 + x, pl.ds(base + 64, 8), :] = us[x][1]
                outflow = plus(times(p, us[-1]), over)
                y = us[-1]
                for x in range(WIDE - 1, -1, -1):
                    if x < WIDE - 1:
                        y = plus(us[x], times(q, y))
                    z = times(inv, y)
                    sums[x][half] = z if m == 0 else plus(sums[x][half], z)
                carries.append((outflow, plus(times(q, y), under)))
            for k in range(2):
                for part in range(2):
                    send(16 + m * 4 + k * 2 + part, carries[0][k][part], carries[1][k][part])
        for x in range(8):
            own, other = [], []
            for half in range(2):
                first, second = sums[x][half], sums[x + 8][half]
                own.append((first[0] - second[1], first[1] + second[0]))
                other.append((first[0] + second[1], first[1] - second[0]))
            partners = plane_partner(other[0], other[1], lane, first_row)
            packed = [
                plus(plus(own[half], partners[half]), plane(36 + x, bases[half])) for half in range(2)
            ]
            for part in range(2):
                send(part * 8 + x, packed[0][part], packed[1][part])


def backward_kernel(
    velocity_ref, iterate_ref, u_ref, got_ref, uy_ref, uz_ref, lane_ref, row_ref,
    out_ref,
    spec_ref,
):
    lane = lax.broadcasted_iota(jnp.int32, (8, 128), 1)
    sub = lax.broadcasted_iota(jnp.int32, (8, 128), 0)
    narrow = (lane % 64) < 32

    @pl.loop(0, 4)
    def _(t):
        first_row = (sub + t) == 0
        found = chunk_factors(t, lane_ref, row_ref, velocity_ref, MU)
        bases = [pl.multiple_of(base + 8 * t, 8) for base in (0, 32)]

        def take(value):
            start = 8 * t * ROWS + value
            a = got_ref[pl.ds(start, 8, stride=ROWS), :]
            b = got_ref[pl.ds(start + 32 * ROWS, 8, stride=ROWS), :]
            return jnp.where(narrow, a, pltpu.roll(b, 32, 1)), jnp.where(narrow, pltpu.roll(a, 96, 1), b)

        last = [[None, None] for x in range(WIDE)]
        for x in range(8):
            real, imag = take(x), take(8 + x)
            packed = [(real[half], imag[half]) for half in range(2)]
            partners = plane_partner(packed[0], packed[1], lane, first_row)
            for half in range(2):
                both, apart = plus(packed[half], partners[half]), minus(packed[half], partners[half])
                last[x][half] = (0.5 * both[0], 0.5 * both[1])
                last[x + 8][half] = (0.5 * apart[1], -0.5 * apart[0])
        for m in range(2):
            carried = [take(16 + m * 4 + k) for k in range(4)]
            for half in range(2):
                base = bases[half]
                p, q, kappa, inv = found[half][m]

                def old(x):
                    return (
                        u_ref[m * 16 + x, pl.ds(base, 8), :],
                        u_ref[m * 16 + x, pl.ds(base + 64, 8), :],
                    )

                u = (carried[0][half], carried[1][half])
                totals = [plus(u, old(0))]
                for x in range(1, WIDE - 1):
                    u = plus(scaled(EPS[m], last[x][half]), times(p, u))
                    totals.append(plus(u, old(x)))
                y = plus(times(inv, old(WIDE - 1)), (carried[2][half], carried[3][half]))
                for x in range(WIDE - 1, -1, -1):
                    if x < WIDE - 1:
                        y = plus(times(inv, totals[x]), times(q, y))
                    spec_ref[m * 16 + x, pl.ds(base, 8), :] = y[0]
                    spec_ref[m * 16 + x, pl.ds(base + 64, 8), :] = y[1]

    @pl.loop(0, 8)
    def _(block):
        planes = [2 * block, 2 * block + 1, 16 + 2 * block, 17 + 2 * block]
        stacked = jnp.concatenate([spec_ref[at] for at in planes], axis=1)
        mid = left_dot(uz_ref[...], stacked)
        rows = jnp.concatenate(
            [
                jnp.concatenate([mid[:64, 128 * k : 128 * k + 128], mid[64:, 128 * k : 128 * k + 128]], axis=1)
                for k in range(4)
            ],
            axis=0,
        )
        high, low = halves(rows)
        out = right_dot(high, low, uy_ref[0], uy_ref[1])
        for k in range(2):
            x = 2 * block + k
            parts = []
            for m in range(2):
                piece = out[(2 * m + k) * 64 : (2 * m + k) * 64 + 64]
                parts.append((piece[:, :128], piece[:, 128:]))
            for n in range(4):
                total = iterate_ref[n, x]
                for m in range(2):
                    c = COLUMN[m][n]
                    total = total + (2.0 * c.real) * parts[m][0] - (2.0 * c.imag) * parts[m][1]
                out_ref[n, x] = total


def mode_kernel(
    velocity_ref, place_ref, got_ref, own_ref, wave_ref, tg_ref, td_ref, tw_ref, tb_ref,
    back_ref,
    damp_ref, ratio_ref, last_ref, drive_ref, kept_ref,
):
    v0, v1, v2 = velocity_ref[0], velocity_ref[1], velocity_ref[2]
    half, pair = place_ref[0], place_ref[1]
    own = [jnp.broadcast_to(own_ref[k : k + 1, :], (8, 128)) for k in range(4)]
    cross = cross_symbol(own[0], own[1], own[2], own[3], v1, v2)
    mu = [MU[0], MU[0].conjugate(), MU[1], MU[1].conjugate()]
    eps = [EPS[0], EPS[0].conjugate(), EPS[1], EPS[1].conjugate()]
    found = [factors(number, cross, v0) for number in mu]

    @pl.loop(0, 16)
    def _(at):
        rows = pl.ds(pl.multiple_of(at * 8, 8), 8)
        lower = pl.ds(pl.multiple_of(at * 8 + 128, 8), 8)
        symbol = (
            diffusion_number * (2.0 * wave_ref[0, rows, :] - 2.0) + cross[0],
            cross[1] - v0 * wave_ref[1, rows, :],
        )
        total = None
        for m in range(4):
            moved = scaled(mu[m], symbol)
            damp = inverse_of((1.0 - moved[0], -moved[1]))
            damp_ref[m, rows, :] = damp[0]
            damp_ref[m, lower, :] = damp[1]
            term = scaled(eps[m], damp)
            total = term if total is None else plus(total, term)
        ratio_ref[rows, :] = total[0]
        ratio_ref[lower, :] = total[1]
        last_ref[rows, :] = jnp.zeros((8, 128), f32)
        last_ref[lower, :] = jnp.zeros((8, 128), f32)

    lane = lax.broadcasted_iota(jnp.int32, (8, 128), 1)
    narrow = (lane % 64) < 32
    special = ((lane % 32) == 0) & (half == 0)
    plain_pair = pair > 0
    take_own = special & jnp.logical_not(plain_pair)
    take_64 = jnp.logical_not(plain_pair)
    take_32 = narrow ^ special

    def partner(v):
        swapped = jnp.where(take_32, pltpu.roll(v, 32, 1), pltpu.roll(v, 96, 1))
        return jnp.where(take_own, v, jnp.where(take_64, pltpu.roll(v, 64, 1), swapped))

    @pl.loop(0, STEPS)
    def _(s):
        top = pl.multiple_of(s * (SLABS * ROWS), 8)
        pieces = [got_ref[pl.ds(pl.multiple_of(top + x * ROWS, 8), 8), :] for x in range(SLABS)]
        pieces += [got_ref[pl.ds(pl.multiple_of(top + x * ROWS + 8, 8), 8), :] for x in range(SLABS)]
        stacked = jnp.concatenate(pieces + [partner(v) for v in pieces], axis=0)
        drive = left_dot(tg_ref[...], stacked)
        fields = []
        for m in range(2):
            plain = [got_ref[pl.ds(top + 16 + m * 4 + k, SLABS, stride=ROWS), :] for k in range(4)]
            turned = [partner(v) for v in plain]
            fields.append(plain)
            fields.append([turned[0], -turned[1], turned[2], -turned[3]])
        sources = []
        for m in range(4):
            a, b = (fields[m][0], fields[m][1]), (fields[m][2], fields[m][3])
            a = tuple(pltpu.roll(v, 1, 0) for v in a)
            first = minus(a, times(found[m][0], b))
            sources.append(jnp.concatenate([first[0], first[1], b[0], b[1]], axis=0))
        point = left_dot(td_ref[...], jnp.concatenate(sources, axis=1))
        total = (drive[:128], drive[128:])
        for m in range(4):
            d = (point[:128, 128 * m : 128 * m + 128], point[128:, 128 * m : 128 * m + 128])
            y = times((damp_ref[m, :128, :], damp_ref[m, 128:, :]), d)
            if m % 2 == 0:
                kept_ref[s, m // 2, :128, :] = y[0]
                kept_ref[s, m // 2, 128:, :] = y[1]
            total = plus(total, y)
        drive_ref[s, :128, :] = total[0]
        drive_ref[s, 128:, :] = total[1]
        ratio = (ratio_ref[:128, :], ratio_ref[128:, :])
        summed = plus(total, times(ratio, (last_ref[:128, :], last_ref[128:, :])))
        last_ref[:128, :] = summed[0]
        last_ref[128:, :] = summed[1]

    @pl.loop(0, 16)
    def _(at):
        rows = pl.ds(pl.multiple_of(at * 8, 8), 8)
        lower = pl.ds(pl.multiple_of(at * 8 + 128, 8), 8)
        power = (ratio_ref[rows, :], ratio_ref[lower, :])
        for k in range(5):
            power = times(power, power)
        closing = inverse_of((1.0 - circulant_alpha * power[0], -circulant_alpha * power[1]))
        first = times(closing, (last_ref[rows, :], last_ref[lower, :]))
        last_ref[rows, :] = circulant_alpha * first[0]
        last_ref[lower, :] = circulant_alpha * first[1]
        for m in (0, 2):
            weighted = scaled(eps[m], (damp_ref[m, rows, :], damp_ref[m, lower, :]))
            damp_ref[m, rows, :] = weighted[0]
            damp_ref[m, lower, :] = weighted[1]

    @pl.loop(0, STEPS)
    def _(s):
        top = pl.multiple_of(s * (SLABS * ROWS), 8)
        last = (last_ref[:128, :], last_ref[128:, :])
        packed = left_dot(tw_ref[...], last_ref[...])
        for x in range(SLABS):
            back_ref[pl.ds(pl.multiple_of(top + x * ROWS, 8), 8), :] = packed[8 * x : 8 * x + 8]
            back_ref[pl.ds(pl.multiple_of(top + x * ROWS + 8, 8), 8), :] = packed[64 + 8 * x : 72 + 8 * x]
        lines = []
        for m in range(2):
            y = times((damp_ref[2 * m, :128, :], damp_ref[2 * m, 128:, :]), last)
            y = plus(y, (kept_ref[s, m, :128, :], kept_ref[s, m, 128:, :]))
            lines.append(jnp.concatenate([y[0], y[1]], axis=0))
        ends = left_dot(tb_ref[...], jnp.concatenate(lines, axis=1))
        for m in range(2):
            part = [ends[8 * k : 8 * k + 8, 128 * m : 128 * m + 128] for k in range(6)]
            p, q, kappa, inv = found[2 * m]
            u = times(kappa, minus((part[0], part[1]), times(q, (part[2], part[3]))))
            for k, value in enumerate((u[0], u[1], part[4], part[5])):
                back_ref[pl.ds(top + 16 + m * 4 + k, SLABS, stride=ROWS), :] = value
        ratio = (ratio_ref[:128, :], ratio_ref[128:, :])
        following = plus((drive_ref[s, :128, :], drive_ref[s, 128:, :]), times(ratio, last))
        last_ref[:128, :] = following[0]
        last_ref[128:, :] = following[1]


def owner_place(owner):
    x, y, z_pair = owner // 16, (owner // 4) % 4, owner % 4
    z = 2 * z_pair + (x + y) % 2
    return ((z % 4) * 4 + y) * 2 + 1, x * 2 + z // 4


def owner_of(tm, space):
    y, z, x = (tm // 2) % 4, (tm // 8) + 4 * (space % 2), space // 2
    owner = x * 16 + y * 4 + z // 2
    return owner, ((tm % 2) == 1) & ((x + y + z) % 2 == 0)


def gather_kernel(send_ref, got_ref, send_sem, recv_sem, own_sem):
    tm, space = lax.axis_index("tm"), lax.axis_index("space")
    owner, is_owner = owner_of(tm, space)
    here = (tm * SLABS + space) * ROWS

    def copy(target):
        to_tm, to_space = owner_place(target)
        return pltpu.make_async_remote_copy(
            src_ref=send_ref.at[pl.ds(pl.multiple_of(target * ROWS, 8), ROWS), :],
            dst_ref=got_ref.at[pl.ds(pl.multiple_of(here, 8), ROWS), :],
            send_sem=send_sem,
            recv_sem=recv_sem,
            device_id=(to_tm, to_space),
            device_id_type=MESH,
        )

    def kept():
        return pltpu.make_async_copy(
            send_ref.at[pl.ds(pl.multiple_of(owner * ROWS, 8), ROWS), :],
            got_ref.at[pl.ds(pl.multiple_of(here, 8), ROWS), :],
            own_sem,
        )

    @pl.when(is_owner)
    def _():
        kept().start()

    @pl.loop(0, OWNERS)
    def _(k):
        target = (owner + k) % OWNERS

        @pl.when(jnp.logical_not(is_owner) | (k > 0))
        def _():
            copy(target).start()

    def waiter(rows_sent, rows_got):
        return pltpu.make_async_remote_copy(
            src_ref=send_ref.at[pl.ds(0, rows_sent), :],
            dst_ref=got_ref.at[pl.ds(0, rows_got), :],
            send_sem=send_sem,
            recv_sem=recv_sem,
            device_id=(tm, space),
            device_id_type=MESH,
        )

    @pl.when(is_owner)
    def _():
        kept().wait()
        both = waiter((OWNERS - 1) * ROWS, (STEPS * SLABS - 1) * ROWS)
        both.wait_send()
        both.wait_recv()

    @pl.when(jnp.logical_not(is_owner))
    def _():
        waiter(OWNERS * ROWS, OWNERS * ROWS).wait_send()


def scatter_kernel(back_ref, got_ref, send_sem, recv_sem, own_sem):
    tm, space = lax.axis_index("tm"), lax.axis_index("space")
    owner, is_owner = owner_of(tm, space)
    me = tm * SLABS + space
    count = STEPS * SLABS

    def copy(target):
        return pltpu.make_async_remote_copy(
            src_ref=back_ref.at[pl.ds(pl.multiple_of(target * ROWS, 8), ROWS), :],
            dst_ref=got_ref.at[pl.ds(pl.multiple_of(owner * ROWS, 8), ROWS), :],
            send_sem=send_sem,
            recv_sem=recv_sem,
            device_id=(target // SLABS, target % SLABS),
            device_id_type=MESH,
        )

    def kept():
        return pltpu.make_async_copy(
            back_ref.at[pl.ds(pl.multiple_of(me * ROWS, 8), ROWS), :],
            got_ref.at[pl.ds(pl.multiple_of(owner * ROWS, 8), ROWS), :],
            own_sem,
        )

    def waiter(rows_sent, rows_got):
        return pltpu.make_async_remote_copy(
            src_ref=back_ref.at[pl.ds(0, rows_sent), :],
            dst_ref=got_ref.at[pl.ds(0, rows_got), :],
            send_sem=send_sem,
            recv_sem=recv_sem,
            device_id=(tm, space),
            device_id_type=MESH,
        )

    @pl.when(is_owner)
    def _():
        kept().start()

        @pl.loop(1, count)
        def _(k):
            copy((me + k) % count).start()

        kept().wait()
        both = waiter((count - 1) * ROWS, (OWNERS - 1) * ROWS)
        both.wait_send()
        both.wait_recv()

    @pl.when(jnp.logical_not(is_owner))
    def _():
        waiter(OWNERS * ROWS, OWNERS * ROWS).wait_recv()


VMEM, SMEM, ANY = pltpu.VMEM, pltpu.SMEM, pl.ANY


def spec(space):
    return pl.BlockSpec(memory_space=space)


def shape(*dims):
    return jax.ShapeDtypeStruct(dims, f32)


PARAMS = pltpu.CompilerParams(vmem_limit_bytes=60 * 1024 * 1024)


def forward(velocity, step, iterate, right_side, kappa, below, above, interpret=False):
    return pl.pallas_call(
        forward_kernel,
        out_shape=(shape(32, 128, 128), shape(OWNERS * ROWS, 128)),
        in_specs=[spec(SMEM)] * 2 + [spec(VMEM)] * 9,
        out_specs=(spec(VMEM), spec(VMEM)),
        scratch_shapes=[VMEM((2816, 256), bf16), VMEM((2816, 256), bf16), VMEM((44, 128, 128), f32)],
        compiler_params=PARAMS,
        interpret=interpret,
        name="forward",
    )(
        velocity, step, iterate, right_side, kappa, below, above,
        TABLES["ty"], TABLES["tz"], TABLES["lane"], TABLES["row"],
    )


def modes(velocity, place, got, own, interpret=False):
    return pl.pallas_call(
        mode_kernel,
        out_shape=shape(STEPS * SLABS * ROWS, 128),
        in_specs=[spec(SMEM)] * 2 + [spec(VMEM)] * 7,
        out_specs=spec(VMEM),
        scratch_shapes=[
            VMEM((4, 256, 128), f32), VMEM((256, 128), f32), VMEM((256, 128), f32),
            VMEM((STEPS, 256, 128), f32), VMEM((STEPS, 2, 256, 128), f32),
        ],
        compiler_params=PARAMS,
        interpret=interpret,
        name="modes",
    )(
        velocity, place, got, own,
        TABLES["wave_x"], TABLES["tg"], TABLES["td"], TABLES["tw"], TABLES["tb"],
    )


def backward(velocity, iterate, u, got, interpret=False):
    return pl.pallas_call(
        backward_kernel,
        out_shape=shape(4, WIDE, NZ, NY),
        in_specs=[spec(SMEM)] + [spec(VMEM)] * 7,
        out_specs=spec(VMEM),
        scratch_shapes=[VMEM((32, 128, 128), f32)],
        compiler_params=PARAMS,
        interpret=interpret,
        name="backward",
    )(velocity, iterate, u, got, TABLES["uy"], TABLES["uz"], TABLES["lane"], TABLES["row"])


def exchange(kernel, value, rows, name):
    return pl.pallas_call(
        kernel,
        out_shape=shape(rows, 128),
        in_specs=[spec(ANY)],
        out_specs=spec(ANY),
        scratch_shapes=[pltpu.SemaphoreType.DMA] * 3,
        compiler_params=pltpu.CompilerParams(has_side_effects=True),
        name=name,
    )(value)


def shards(iterate, right_side, diffusivity, velocity):
    iterate, right_side = iterate[0], right_side[0]
    tm, space = lax.axis_index("tm"), lax.axis_index("space")
    up = [(i, (i + 1) % SLABS) for i in range(SLABS)]
    down = [(i, (i - 1) % SLABS) for i in range(SLABS)]
    below = lax.ppermute(diffusivity[WIDE - 1], "space", up)
    above = lax.ppermute(diffusivity[0], "space", down)
    step = tm.astype(jnp.int32)[None]
    u, sent = forward(velocity, step, iterate, right_side, diffusivity, below, above)
    got = exchange(gather_kernel, sent, STEPS * SLABS * ROWS, "gather")
    owner, _ = owner_of(tm, space)
    place = jnp.stack([owner // 32, owner % 32]).astype(jnp.int32)
    own = lax.dynamic_index_in_dim(jnp.asarray(TABLES["own"]), owner, 0, keepdims=False)
    back = modes(velocity, place, got, own)
    returned = exchange(scatter_kernel, back, OWNERS * ROWS, "scatter")
    return backward(velocity, iterate, u, returned)[None]


def solution(mesh):
    placed = (
        P("tm", None, "space", None, None),
        P("tm", None, "space", None, None),
        P("space", None, None),
        P(),
    )
    return jax.shard_map(
        shards,
        mesh=mesh,
        in_specs=placed,
        out_specs=P("tm", None, "space", None, None),
        check_vma=False,
    )
```

time: 576 us -> 147 us (0.26)
  the two profiles are of different devices: /device:TPU:64 before, /device:TPU:1 now
where the time goes in v1:
time: 147 us
  Pallas kernels  127 us (86%)
  starting transfers between devices  9.92 us (7%)
  waiting for transfers between devices  7.1 us (5%)
  local copies, waits for them, and re-layouts  2.66 us (2%)
    pallas_call x2, Pallas kernels, exchange(): pl.pallas_call(kernel, out_shape=shape(rows, 128), in_specs=[spec(ANY)],...  72.1 us
    pallas_call x1, Pallas kernels, modes(): pl.pallas_call(mode_kernel, out_shape=shape(STEPS * SLABS * ROWS, 128), i...  29 us
    pallas_call x1, Pallas kernels, forward(): pl.pallas_call(forward_kernel, out_shape=(shape(32, 128, 128), shape(OWNE...  16.1 us
    ppermute x1, starting transfers between devices, shards(): above = lax.ppermute(diffusivity[0], 'space', down)  9.92 us
    pallas_call x1, Pallas kernels, backward(): pl.pallas_call(backward_kernel, out_shape=shape(4, WIDE, NZ, NY), in_spec...  9.55 us
    ppermute x1, waiting for transfers between devices, shards(): below = lax.ppermute(diffusivity[WIDE - 1], 'space', up)  7.09 us
  transfers between devices with their start and end apart: 2, of which 1 were waited for; matrix products, arithmetic and copies ran while one was open for 1% of the time, Pallas kernels for 0%

profile of v1, /device:TPU:1, one launch (start us, length us, event | category | flops | bytes accessed | tf_op | source)
XLA Modules:
  0.0 147.0 jit_solution(15023849559860425216)
XLA Ops:
  0.0 0.8 slice_bitcast_fusion
  0.8 9.9 %collective-permute-start.1 = (f32[64,128]{1,0:T(8,128)S(1)}, f32[64,128]{1,0:T(8,128)S(1)}, u32[]{:S(2)}, u32[]{:S(2)}) collective-permute-start(f32[64,128]{1,0:T(8,128)S(1)} %get-tuple-element.9), channel_id=1, source_target_pairs={{0,7},{1,0},{2,1},{3,2},{4,3},{5,4},{6,5},{7,6},{8,15},{9,8},{10,9... | collective-permute-start | bytes 98312 | tf_op jit(solution)/shard_map/ppermute | solution.py:857
  10.7 0.0 collective-permute-start
  10.7 1.3 dynamic-slice_bitcast_fusion.own_ref
  12.0 0.6 pad_add_fusion.place_ref
  12.6 0.0 collective-permute-done.1.above_ref
  12.6 0.0 copy-start
  12.6 7.1 %collective-permute-done.below_ref = f32[64,128]{1,0:T(8,128)S(1)} collective-permute-done((f32[64,128]{1,0:T(8,128)S(1)}, f32[64,128]{1,0:T(8,128)S(1)}, u32[]{:S(2)}, u32[]{:S(2)}) %collective-permute-start) | collective-permute-done | bytes 32800 | tf_op jit(solution)/shard_map/ppermute | solution.py:856
  19.7 0.0 copy-start.1
  19.7 0.0 copy-done
  19.7 0.6 copy-done.1
  20.3 16.1 %forward.1 = (f32[32,128,128]{2,1,0:T(8,128)}, f32[1536,128]{1,0:T(8,128)}) custom-call(f32[3]{0:T(128)} %velocity_ref.5, s32[1]{0:T(128)} %bitcast.1.step_ref, f32[4,16,64,128]{3,2,1,0:T(8,128)} %bitcast.12, f32[4,16,64,128]{3,2,1,0:T(8,128)} %bitcast.14, f32[16,64,128]{2,1,0:T(8,128)} %kappa_ref.1, f32[64,128]{1,0:T(8,128)} %copy-done.1, ...), custom_call_target="tpu_custom_call" | custom-call | tf_op jit(solution)/shard_map/forward/pallas_call | solution.py:792
  36.4 31.8 %gather.1.got_ref = f32[6144,128]{1,0:T(8,128)} custom-call(f32[1536,128]{1,0:T(8,128)} %get-tuple-element.8.send_ref), custom_call_target="tpu_custom_call" | custom-call | tf_op jit(solution)/shard_map/gather/pallas_call | solution.py:840
  68.2 29.0 %modes.1.back_ref = f32[6144,128]{1,0:T(8,128)} custom-call(f32[3]{0:T(128)} %velocity_ref.5, s32[2]{0:T(128)} %pad_add_fusion.place_ref, f32[6144,128]{1,0:T(8,128)} %gather.1.got_ref, f32[4,128]{1,0:T(4,128)} %dynamic-slice_bitcast_fusion.own_ref, f32[2,128,128]{2,1,0:T(8,128)} %constant.122.clone.wave_ref, bf16[256,768]{1,0:T(8,128)(2,1)} %constant.123.clone.tg_ref, ...), custom_call_target="tpu_custom_call" | custom-call | tf_op jit(solution)/shard_map/modes/pallas_call | solution.py:808
  97.2 40.3 %scatter.1.got_ref = f32[1536,128]{1,0:T(8,128)} custom-call(f32[6144,128]{1,0:T(8,128)} %modes.1.back_ref), custom_call_target="tpu_custom_call" | custom-call | tf_op jit(solution)/shard_map/scatter/pallas_call | solution.py:840
  137.5 9.6 %backward.1 = f32[4,16,64,128]{3,2,1,0:T(8,128)} custom-call(f32[3]{0:T(128)} %velocity_ref.5, f32[4,16,64,128]{3,2,1,0:T(8,128)} %bitcast.13, f32[32,128,128]{2,1,0:T(8,128)} %get-tuple-element.7.u_ref, f32[1536,128]{1,0:T(8,128)} %scatter.1.got_ref, bf16[2,256,256]{2,1,0:T(8,128)(2,1)} %constant.127.clone.uy_ref, bf16[128,384]{1,0:T(8,128)(2,1)} %constant.128.clone.uz_ref, ...), custom_call_target="tpu_custom_call" | custom-call | tf_op jit(solution)/shard_map/backward/pallas_call | solution.py:827
Async XLA Ops:
  0.8 11.8 %collective-permute-start.1 = (f32[64,128]{1,0:T(8,128)S(1)}, f32[64,128]{1,0:T(8,128)S(1)}, u32[]{:S(2)}, u32[]{:S(2)}) collective-permute-start(f32[64,128]{1,0:T(8,128)S(1)} %get-tuple-element.9), channel_id=1, source_target_pairs={{0,7},{1,0},{2,1},{3,2},{4,3},{5,4},{6,5},{7,6},{8,15},{9,8},{10,9... | collective-permute-start | bytes 98312 | tf_op jit(solution)/shard_map/ppermute | solution.py:857
  10.7 9.0 %collective-permute-start = (f32[64,128]{1,0:T(8,128)S(1)}, f32[64,128]{1,0:T(8,128)S(1)}, u32[]{:S(2)}, u32[]{:S(2)}) collective-permute-start(f32[64,128]{1,0:T(8,128)S(1)} %get-tuple-element.10), channel_id=1, source_target_pairs={{0,1},{1,2},{2,3},{3,4},{4,5},{5,6},{6,7},{7,0},{8,9},{9,10},{10,1... | collective-permute-start | bytes 98312 | tf_op jit(solution)/shard_map/ppermute | solution.py:856
  12.6 7.1 %copy-start = (f32[64,128]{1,0:T(8,128)}, f32[64,128]{1,0:T(8,128)S(1)}, u32[]{:S(2)}) copy-start(f32[64,128]{1,0:T(8,128)S(1)} %collective-permute-done.1.above_ref) | copy-start | bytes 98308
  19.7 0.6 copy-start.1

commit v2 on v1

v2 whole, which is shorter than its diff:
```python
import functools
import math

import jax
import jax.numpy as jnp
import numpy as np
from jax import lax
from jax.experimental import pallas as pl
from jax.experimental.pallas import tpu as pltpu
from jax.sharding import PartitionSpec as P

NX, NY, NZ, STEPS = 128, 128, 64, 32
SLABS, WIDE = 8, 16
OWNERS = 128
ROWS = 12
MESH = pl.DeviceIdType.MESH
f32, bf16 = jnp.float32, jnp.bfloat16

diffusion_number = 16.0
circulant_alpha = 0.1


def collocation_matrix():
    radau_nodes = [0.08858795951270394, 0.4094668644407347, 0.7876594617608471, 1.0]
    matrix = [[0.0] * 4 for row_index in range(4)]
    for column_index in range(4):
        coefficients = [1.0]
        for other_index in range(4):
            if other_index != column_index:
                scale_value = 1.0 / (radau_nodes[column_index] - radau_nodes[other_index])
                shifted = [0.0] + [value * scale_value for value in coefficients]
                lowered = [
                    -radau_nodes[other_index] * scale_value * value for value in coefficients
                ] + [0.0]
                coefficients = [
                    left_value + right_value for left_value, right_value in zip(shifted, lowered)
                ]
        for row_index in range(4):
            total = 0.0
            for power_index in range(len(coefficients)):
                total = total + coefficients[power_index] * radau_nodes[row_index] ** (
                    power_index + 1
                ) / (power_index + 1)
            matrix[row_index][column_index] = total
    return matrix


def solve_system(matrix, target):
    count = len(target)
    rows_list = [list(matrix[row_index]) + [target[row_index]] for row_index in range(count)]
    for column in range(count):
        best_row = column
        for candidate in range(column + 1, count):
            if abs(rows_list[candidate][column]) > abs(rows_list[best_row][column]):
                best_row = candidate
        saved_row = rows_list[column]
        rows_list[column] = rows_list[best_row]
        rows_list[best_row] = saved_row
        leader = rows_list[column][column]
        for other_row in range(count):
            if other_row != column:
                factor = rows_list[other_row][column] / leader
                rows_list[other_row] = [
                    left_value - factor * right_value
                    for left_value, right_value in zip(rows_list[other_row], rows_list[column])
                ]
    return [
        rows_list[row_index][count] / rows_list[row_index][row_index] for row_index in range(count)
    ]


def node_basis():
    matrix = collocation_matrix()
    helper = [[0.0] * 4 for row_index in range(4)]
    coefficients = [0.0, 0.0, 0.0, 0.0, 1.0]
    for order in range(1, 5):
        product = [
            [
                sum((matrix[row_index][inner] * helper[inner][column] for inner in range(4)))
                for column in range(4)
            ]
            for row_index in range(4)
        ]
        for row_index in range(4):
            product[row_index][row_index] = product[row_index][row_index] + coefficients[5 - order]
        helper = product
        trace_value = sum(
            (
                sum((matrix[row_index][inner] * helper[inner][row_index] for inner in range(4)))
                for row_index in range(4)
            )
        )
        coefficients[4 - order] = -trace_value / order
    roots_list = [(0.4 + 0.9j) ** power_index for power_index in range(4)]
    for sweep in range(400):
        for root_index in range(4):
            current = roots_list[root_index]
            numer = 0.0
            for power_index in range(4, -1, -1):
                numer = numer * current + coefficients[power_index]
            denom = 1.0
            for other_index in range(4):
                if other_index != root_index:
                    denom = denom * (current - roots_list[other_index])
            roots_list[root_index] = current - numer / denom
    vectors = [[0.0] * 4 for row_index in range(4)]
    for root_index in range(4):
        shifted = [
            [
                matrix[row_index][column] - (roots_list[root_index] if row_index == column else 0.0)
                for column in range(3)
            ]
            for row_index in range(3)
        ]
        target = [-matrix[row_index][3] for row_index in range(3)]
        parts = solve_system(shifted, target) + [1.0 + 0j]
        for row_index in range(4):
            vectors[row_index][root_index] = parts[row_index]
    inverse = [[0.0] * 4 for row_index in range(4)]
    for column in range(4):
        unit = [1.0 if row_index == column else 0.0 for row_index in range(4)]
        parts = solve_system(vectors, unit)
        for row_index in range(4):
            inverse[row_index][column] = parts[row_index]
    weights = [sum((inverse[row_index][column] for column in range(4))) for row_index in range(4)]
    return (roots_list, vectors, inverse, weights)


VALUES, VECTORS, INVERSE, WEIGHTS = node_basis()
PAIRS = [m for m in range(4) if complex(VALUES[m]).imag > 0]
MU = [complex(VALUES[m]) for m in PAIRS]
COLUMN = [[complex(VECTORS[n][m]) for n in range(4)] for m in PAIRS]
ROW = [[complex(INVERSE[m][n]) for n in range(4)] for m in PAIRS]
EPS = [complex(WEIGHTS[m]) for m in PAIRS]


def wave_order_z():
    index = np.arange(NZ)
    return np.where(index <= NZ // 2, index, NZ + NZ // 2 - index)


def wave_order_y():
    lane = np.arange(NY)
    index = 16 * (lane // 32) + lane % 16
    return np.where(lane % 32 < 16, index, np.where(index == 0, NY // 2, NY - index))


def split(values):
    values = np.asarray(values, np.float64)
    high = values.astype(np.float32).astype(bf16)
    low = (values - high.astype(np.float64)).astype(np.float32).astype(bf16)
    return high, low


def side_table(values):
    high, low = split(values)
    return np.concatenate([high, high, low], axis=1)


def halves(x):
    high = x.astype(bf16)
    return high, (x - high.astype(f32)).astype(bf16)


def left_dot(table, x):
    high, low = halves(x)
    return jnp.dot(table, jnp.concatenate([high, low, high], axis=0), preferred_element_type=f32)


def right_dot(high, low, table_high, table_low):
    return (
        jnp.dot(high, table_high, preferred_element_type=f32)
        + jnp.dot(low, table_high, preferred_element_type=f32)
        + jnp.dot(high, table_low, preferred_element_type=f32)
    )


def complex_block(matrix):
    return np.block([[matrix.real, -matrix.imag], [matrix.imag, matrix.real]])


def make_tables():
    ky, kz = wave_order_y(), wave_order_z()
    kx, x = np.arange(NX), np.arange(NX)
    to_y = np.exp(-2j * np.pi * np.outer(ky, np.arange(NY)) / NY)
    to_z = np.exp(-2j * np.pi * np.outer(kz, np.arange(NZ)) / NZ)
    tables = {}
    tables["ty"] = np.stack(split(complex_block(to_y).T))
    tables["tz"] = side_table(complex_block(to_z))
    tables["uy"] = np.stack(split(complex_block(np.conj(to_y.T) / NY).T))
    tables["uz"] = side_table(complex_block(np.conj(to_z.T) / NZ))
    cells = (np.arange(SLABS)[:, None] * WIDE + np.arange(8)[None, :]).reshape(-1)
    theta = 2 * np.pi * kx / NX
    at = np.exp(-1j * np.outer(theta, cells))
    shifted = np.exp(-8j * theta)[:, None]
    from_own = at * (1 - 1j * shifted) / 2
    from_partner = at * (1 + 1j * shifted) / 2
    firsts = np.arange(SLABS) * WIDE

    def lane_block(matrix):
        return np.concatenate([matrix.real, -matrix.imag], axis=1)

    def drive_table(from_x):
        table = np.zeros((NX, SLABS, ROWS), complex)
        table[:, :, :8] = from_x.reshape(NX, SLABS, 8)
        return table

    def point_tables():
        out = []
        for m in range(2):
            table = np.zeros((NX, SLABS, ROWS), complex)
            table[:, :, 8 + 2 * m] = np.exp(-1j * np.outer(theta, firsts + WIDE))
            table[:, :, 9 + 2 * m] = np.exp(-1j * np.outer(theta, firsts - 1))
            out.append(table)
        for m in range(2):
            table = np.zeros((8, SLABS, ROWS), complex)
            table[:, :, 9 + 2 * m] = np.exp(-1j * np.outer(theta[:8], firsts))
            out.append(table)
        return out

    def flat(pieces):
        return lane_block(np.concatenate(pieces, axis=0).reshape(-1, SLABS * ROWS))

    tables["tg"] = np.stack(
        [side_table(flat([drive_table(k)] + point_tables())) for k in (from_own, from_partner)]
    )
    back = np.exp(1j * np.outer(cells, theta)) * (1 + 1j * np.exp(8j * theta))[None, :] / NX
    tables["tw"] = side_table(lane_block(back))
    ends = [np.exp(1j * np.outer(firsts + k, theta)) / NX for k in (0, 1, 15)]
    tables["tb"] = side_table(lane_block(np.concatenate(ends, axis=0)))
    trig_y = 2 * np.pi * ky / NY
    trig_z = 2 * np.pi * kz / NZ
    tables["lane"] = np.stack([np.cos(trig_y), np.sin(trig_y)]).astype(np.float32)
    tables["row"] = np.stack(
        [np.broadcast_to(v[:, None], (NZ, NY)) for v in (np.cos(trig_z), np.sin(trig_z))]
    ).astype(np.float32)
    tables["wave_x"] = np.stack(
        [np.broadcast_to(v[:, None], (NX, 128)) for v in (np.cos(theta), np.sin(theta))]
    ).astype(np.float32)
    lane = np.arange(128)
    own = np.zeros((OWNERS, 8, 128))
    for owner in range(OWNERS):
        part, pair = owner // 32, owner % 32
        piece = (lane // 32 - part) % 4
        at_y, row = (lane - 32 * piece) % 128, piece % 2
        other_y = np.where((at_y == 0) | (at_y == 16), at_y, at_y ^ 16)
        other_row = row if pair == 0 else 1 - row
        other = (other_y + 32 * (2 * (piece // 2) + other_row)) % 128
        y, z = trig_y[at_y], trig_z[pair + 32 * row]
        own[owner] = np.stack(
            [
                np.cos(y), np.sin(y), np.cos(z), np.sin(z),
                other, np.roll(other, -64), np.where(piece < 2, 1.0, -1.0), (lane + 64) % 128,
            ]
        )
    tables["own"] = own.astype(np.float32)
    return tables


TABLES = make_tables()


def times(a, b):
    return (a[0] * b[0] - a[1] * b[1], a[0] * b[1] + a[1] * b[0])


def plus(a, b):
    return (a[0] + b[0], a[1] + b[1])


def minus(a, b):
    return (a[0] - b[0], a[1] - b[1])


def scaled(number, a):
    return (number.real * a[0] - number.imag * a[1], number.real * a[1] + number.imag * a[0])


def inverse_of(a):
    size = 1.0 / (a[0] * a[0] + a[1] * a[1])
    return (a[0] * size, -a[1] * size)


def root_of(a):
    size = jnp.sqrt(a[0] * a[0] + a[1] * a[1])
    main = jnp.sqrt(0.5 * (size + jnp.abs(a[0])))
    other = a[1] / (2.0 * main)
    positive = a[0] >= 0.0
    return (
        jnp.where(positive, main, jnp.abs(other)),
        jnp.where(positive, other, jnp.where(a[1] >= 0.0, main, -main)),
    )


def cross_symbol(cos_y, sin_y, cos_z, sin_z, v1, v2):
    return (
        diffusion_number * ((2.0 * cos_y - 2.0) + (2.0 * cos_z - 2.0)),
        -(v1 * sin_y + v2 * sin_z),
    )


def factors(mu, cross, v0):
    c_up = -mu.real * (diffusion_number - 0.5 * v0), -mu.imag * (diffusion_number - 0.5 * v0)
    c_down = -mu.real * (diffusion_number + 0.5 * v0), -mu.imag * (diffusion_number + 0.5 * v0)
    moved = scaled(mu, cross)
    c_mid = (1.0 + 2.0 * diffusion_number * mu.real - moved[0], 2.0 * diffusion_number * mu.imag - moved[1])
    product = times(c_up, c_down)
    square = times(c_mid, c_mid)
    root = root_of((square[0] - 4.0 * product[0], square[1] - 4.0 * product[1]))
    same = c_mid[0] * root[0] + c_mid[1] * root[1] >= 0.0
    kappa = (
        0.5 * (c_mid[0] + jnp.where(same, root[0], -root[0])),
        0.5 * (c_mid[1] + jnp.where(same, root[1], -root[1])),
    )
    inv = inverse_of(kappa)
    p = times(inv, c_down)
    q = times(inv, c_up)
    return (-p[0], -p[1]), (-q[0], -q[1]), kappa, inv


def plane_partner(low, high, lane, first_row):
    ends = (lane == 0) | (lane == 16)
    first = (lane % 32) < 16

    def turned(v):
        return jnp.where(ends, v, jnp.where(first, pltpu.roll(v, 112, 1), pltpu.roll(v, 16, 1)))

    low_turned, high_turned = [turned(v) for v in low], [turned(v) for v in high]
    to_low = [jnp.where(first_row, a, b) for a, b in zip(low_turned, high_turned)]
    to_high = [jnp.where(first_row, b, a) for a, b in zip(low_turned, high_turned)]
    return (to_low[0], -to_low[1]), (to_high[0], -to_high[1])


def packed_for(low, high, block):
    pieces = [low[0], high[0], low[1], high[1]]
    pieces = [pieces[0]] + [pltpu.roll(pieces[c], 32 * c, 1) for c in (1, 2, 3)]
    out = []
    for h in range(4):
        value = pieces[3]
        for c in (2, 1, 0):
            value = jnp.where(block == (h + c) % 4, pieces[c], value)
        out.append(value)
    return out


def unpacked_from(values, block):
    out = []
    for c in range(4):
        piece = values[(3 - c) % 4]
        for d in (2, 1, 0):
            piece = jnp.where(block == d, values[(d - c) % 4], piece)
        out.append(piece if c == 0 else pltpu.roll(piece, 128 - 32 * c, 1))
    return (out[0], out[2]), (out[1], out[3])


def chunk_factors(t, lane_ref, row_ref, velocity_ref, mu):
    cos_y, sin_y = lane_ref[0:1, :], lane_ref[1:2, :]
    found = []
    for base in (0, 32):
        rows = pl.ds(pl.multiple_of(base + 8 * t, 8), 8)
        cross = cross_symbol(
            cos_y, sin_y, row_ref[0, rows, :], row_ref[1, rows, :], velocity_ref[1], velocity_ref[2]
        )
        found.append([factors(number, cross, velocity_ref[0]) for number in mu])
    return found


def dft_block(high, low, ty_ref, tz_ref):
    mid = right_dot(high, low, ty_ref[0], ty_ref[1])
    stacked = jnp.concatenate(
        [
            jnp.concatenate([mid[64 * k : 64 * k + 64, :128], mid[64 * k : 64 * k + 64, 128:]], axis=0)
            for k in range(4)
        ],
        axis=1,
    )
    return left_dot(tz_ref[...], stacked)


def source_kernel(
    velocity_ref, step_ref, iterate_ref, right_ref, kappa_ref, ty_ref, tz_ref,
    spec_ref, mixed_ref,
    high_ref, low_ref,
):
    v0, v1, v2 = velocity_ref[0], velocity_ref[1], velocity_ref[2]

    def put(at, real, imag):
        rows = pl.ds(pl.multiple_of(at * 64, 64), 64)
        for k, part in enumerate((real, imag)):
            high, low = halves(part)
            high_ref[rows, k * 128 : (k + 1) * 128] = high
            low_ref[rows, k * 128 : (k + 1) * 128] = low

    def mixture(m, groups):
        real = imag = None
        for scale, values in groups:
            for n in range(4):
                factor = scale * ROW[m][n]
                a, b = factor.real * values[n], factor.imag * values[n]
                real = a if real is None else real + a
                imag = b if imag is None else imag + b
        return real, imag

    def inner(x, below, above):
        plain, applied = [], []
        kappa = kappa_ref[x]
        for n in range(4):
            f = iterate_ref[n, x]
            up_z, down_z = pltpu.roll(f, NZ - 1, 0), pltpu.roll(f, 1, 0)
            up_y, down_y = pltpu.roll(f, NY - 1, 1), pltpu.roll(f, 1, 1)
            total = (up_z + down_z) + (up_y + down_y) - 6.0 * f
            moved = v1 * (up_y - down_y) + v2 * (up_z - down_z)
            if above:
                up_x = iterate_ref[n, x + 1]
                total, moved = total + up_x, moved + v0 * up_x
            if below:
                down_x = iterate_ref[n, x - 1]
                total, moved = total + down_x, moved - v0 * down_x
            applied.append((diffusion_number * kappa) * total - 0.5 * moved)
            plain.append(right_ref[n, x] - f)
        for m in range(2):
            real, imag = mixture(m, [(1.0, plain), (MU[m], applied)])
            put(m * 16 + x, real, imag)

    for side, x in enumerate((0, WIDE - 1)):
        for m in range(2):
            real, imag = mixture(m, [(MU[m], [iterate_ref[n, x] for n in range(4)])])
            mixed_ref[side * 4 + m * 2] = real
            mixed_ref[side * 4 + m * 2 + 1] = imag
    inner(0, False, True)
    inner(WIDE - 1, True, False)

    @pl.loop(1, WIDE - 1)
    def _(x):
        inner(x, True, True)

    keep = jnp.where(step_ref[0] < STEPS - 1, 1.0, 0.0).astype(f32)

    @pl.loop(0, 8)
    def _(x):
        put(32 + x, keep * iterate_ref[3, x], keep * iterate_ref[3, x + 8])

    @pl.loop(0, 10)
    def _(block):
        rows = pl.ds(pl.multiple_of(block * 256, 256), 256)
        out = dft_block(high_ref[rows, :], low_ref[rows, :], ty_ref, tz_ref)
        for k in range(4):
            spec_ref[block * 4 + k] = out[:, 128 * k : 128 * k + 128]


def slab_kernel(
    velocity_ref, spec_ref, mixed_ref, below_ref, above_ref, ty_ref, tz_ref, lane_ref, row_ref,
    u_ref, send_ref,
    edge_ref,
):
    v0 = velocity_ref[0]
    outer = [diffusion_number * below_ref[...] - 0.5 * v0, diffusion_number * above_ref[...] + 0.5 * v0]
    edges = [
        jnp.concatenate([outer[side] * mixed_ref[side * 4 + m * 2 + part] for part in range(2)], axis=1)
        for m in range(2)
        for side in range(2)
    ]
    high, low = halves(jnp.concatenate(edges, axis=0))
    out = dft_block(high, low, ty_ref, tz_ref)
    for k in range(4):
        edge_ref[k] = out[:, 128 * k : 128 * k + 128]

    lane = lax.broadcasted_iota(jnp.int32, (8, 128), 1)
    sub = lax.broadcasted_iota(jnp.int32, (8, 128), 0)
    block = lane // 32

    @pl.loop(0, 4)
    def _(t):
        first_row = (sub + t) == 0
        found = chunk_factors(t, lane_ref, row_ref, velocity_ref, MU)
        bases = [pl.multiple_of(base + 8 * t, 8) for base in (0, 32)]

        def plane(at, base, ref=spec_ref):
            return ref[at, pl.ds(base, 8), :], ref[at, pl.ds(base + 64, 8), :]

        def send(value, low, high):
            for h, packed in enumerate(packed_for(low, high, block)):
                send_ref[pl.ds((32 * h + 8 * t) * ROWS + value, 8, stride=ROWS), :] = packed

        sums = [[None, None] for x in range(WIDE)]
        for m in range(2):
            carries = []
            for half in range(2):
                base = bases[half]
                p, q, kappa, inv = found[half][m]
                under, over = plane(m * 2, base, edge_ref), plane(m * 2 + 1, base, edge_ref)
                u = plus(plane(m * 16, base), times(p, under))
                us = [u]
                for x in range(1, WIDE):
                    u = plus(plane(m * 16 + x, base), times(p, u))
                    us.append(u)
                for x in range(WIDE):
                    u_ref[m * 16 + x, pl.ds(base, 8), :] = us[x][0]
                    u_ref[m * 16 + x, pl.ds(base + 64, 8), :] = us[x][1]
                outflow = plus(times(p, us[-1]), over)
                y = us[-1]
                for x in range(WIDE - 1, -1, -1):
                    if x < WIDE - 1:
                        y = plus(us[x], times(q, y))
                    z = times(inv, y)
                    sums[x][half] = z if m == 0 else plus(sums[x][half], z)
                carries.append((outflow, plus(times(q, y), under)))
            for k in range(2):
                send(8 + m * 2 + k, carries[0][k], carries[1][k])
        for x in range(8):
            own, other = [], []
            for half in range(2):
                first, second = sums[x][half], sums[x + 8][half]
                own.append((first[0] - second[1], first[1] + second[0]))
                other.append((first[0] + second[1], first[1] - second[0]))
            partners = plane_partner(other[0], other[1], lane, first_row)
            packed = [
                plus(plus(own[half], partners[half]), plane(32 + x, bases[half])) for half in range(2)
            ]
            send(x, packed[0], packed[1])


def backward_kernel(
    velocity_ref, iterate_ref, u_ref, got_ref, uy_ref, uz_ref, lane_ref, row_ref,
    out_ref,
    spec_ref,
):
    lane = lax.broadcasted_iota(jnp.int32, (8, 128), 1)
    sub = lax.broadcasted_iota(jnp.int32, (8, 128), 0)
    block = lane // 32

    @pl.loop(0, 4)
    def _(t):
        first_row = (sub + t) == 0
        found = chunk_factors(t, lane_ref, row_ref, velocity_ref, MU)
        bases = [pl.multiple_of(base + 8 * t, 8) for base in (0, 32)]

        def take(value):
            values = [
                got_ref[pl.ds((32 * h + 8 * t) * ROWS + value, 8, stride=ROWS), :] for h in range(4)
            ]
            return unpacked_from(values, block)

        last = [[None, None] for x in range(WIDE)]
        for x in range(8):
            packed = take(x)
            partners = plane_partner(packed[0], packed[1], lane, first_row)
            for half in range(2):
                both, apart = plus(packed[half], partners[half]), minus(packed[half], partners[half])
                last[x][half] = (0.5 * both[0], 0.5 * both[1])
                last[x + 8][half] = (0.5 * apart[1], -0.5 * apart[0])
        for m in range(2):
            start, end = take(8 + m * 2), take(9 + m * 2)
            for half in range(2):
                base = bases[half]
                p, q, kappa, inv = found[half][m]

                def old(x):
                    return (
                        u_ref[m * 16 + x, pl.ds(base, 8), :],
                        u_ref[m * 16 + x, pl.ds(base + 64, 8), :],
                    )

                u = start[half]
                totals = [plus(u, old(0))]
                for x in range(1, WIDE - 1):
                    u = plus(scaled(EPS[m], last[x][half]), times(p, u))
                    totals.append(plus(u, old(x)))
                y = plus(times(inv, old(WIDE - 1)), end[half])
                for x in range(WIDE - 1, -1, -1):
                    if x < WIDE - 1:
                        y = plus(times(inv, totals[x]), times(q, y))
                    spec_ref[m * 16 + x, pl.ds(base, 8), :] = y[0]
                    spec_ref[m * 16 + x, pl.ds(base + 64, 8), :] = y[1]

    @pl.loop(0, 8)
    def _(block):
        planes = [2 * block, 2 * block + 1, 16 + 2 * block, 17 + 2 * block]
        stacked = jnp.concatenate([spec_ref[at] for at in planes], axis=1)
        mid = left_dot(uz_ref[...], stacked)
        rows = jnp.concatenate(
            [
                jnp.concatenate([mid[:64, 128 * k : 128 * k + 128], mid[64:, 128 * k : 128 * k + 128]], axis=1)
                for k in range(4)
            ],
            axis=0,
        )
        high, low = halves(rows)
        out = right_dot(high, low, uy_ref[0], uy_ref[1])
        for k in range(2):
            x = 2 * block + k
            parts = []
            for m in range(2):
                piece = out[(2 * m + k) * 64 : (2 * m + k) * 64 + 64]
                parts.append((piece[:, :128], piece[:, 128:]))
            for n in range(4):
                total = iterate_ref[n, x]
                for m in range(2):
                    c = COLUMN[m][n]
                    total = total + (2.0 * c.real) * parts[m][0] - (2.0 * c.imag) * parts[m][1]
                out_ref[n, x] = total


def mode_kernel(
    remote, velocity_ref, own_ref, wave_ref, tg_ref, tw_ref, tb_ref, sent_ref,
    returned_ref,
    got_ref, back_ref, damp_ref, ratio_ref, last_ref, drive_ref, kept_ref, turn_ref,
    gather_sem, arrive_sem, scatter_sem, return_sem, own_sem,
):
    count = STEPS * SLABS
    tm, space = remote.place()
    is_owner = tm % 2 == 1
    owner = (tm // 2) * SLABS + space
    me = tm * SLABS + space

    def rows_of(index, number=1):
        return pl.ds(pl.multiple_of(index * ROWS, 4), number * ROWS)

    @pl.loop(0, OWNERS)
    def _(k):
        pair = (tm // 2 + STEPS // 2 - k // SLABS) % (STEPS // 2)
        to_space = ((space // 2 + (k % SLABS) // 2) % (SLABS // 2)) * 2 + (space + k) % 2
        target = pair * SLABS + to_space

        @pl.when(jnp.logical_not(is_owner) | (k > 0))
        def _():
            remote.start(
                sent_ref.at[rows_of(target), :], got_ref.at[rows_of(me), :],
                gather_sem, arrive_sem.at[tm], (2 * pair + 1, to_space),
            )

    @pl.when(is_owner)
    def _():
        got_ref[rows_of(me), :] = sent_ref[rows_of(owner), :]
        solve_modes(
            remote, owner, tm, me, rows_of,
            velocity_ref, own_ref, wave_ref, tg_ref, tw_ref, tb_ref,
            sent_ref, returned_ref,
            got_ref, back_ref, damp_ref, ratio_ref, last_ref, drive_ref, kept_ref, turn_ref,
            arrive_sem, scatter_sem, return_sem, own_sem,
        )
        remote.wait_sent(sent_ref.at[rows_of(0, OWNERS - 1), :], gather_sem)
        remote.wait_sent(back_ref.at[rows_of(0, count - 1), :], scatter_sem)
        remote.local(back_ref.at[rows_of(me), :], returned_ref.at[rows_of(owner), :], own_sem).wait()
        remote.wait_got(returned_ref.at[rows_of(0, OWNERS - 1), :], return_sem)

    @pl.when(jnp.logical_not(is_owner))
    def _():
        remote.wait_sent(sent_ref.at[rows_of(0, OWNERS), :], gather_sem)
        remote.wait_got(returned_ref.at[rows_of(0, OWNERS), :], return_sem)


def solve_modes(
    remote, owner, tm, me, rows_of,
    velocity_ref, own_ref, wave_ref, tg_ref, tw_ref, tb_ref,
    sent_ref, returned_ref,
    got_ref, back_ref, damp_ref, ratio_ref, last_ref, drive_ref, kept_ref, turn_ref,
    arrive_sem, scatter_sem, return_sem, own_sem,
):
    v0, v1, v2 = velocity_ref[0], velocity_ref[1], velocity_ref[2]
    own = own_ref[owner]
    line = [own[k : k + 1, :] for k in range(8)]
    wide = [jnp.broadcast_to(v, (8, 128)) for v in line]
    sign = wide[6]
    cross = cross_symbol(wide[0], wide[1], wide[2], wide[3], v1, v2)
    mu = [MU[0], MU[1], MU[0].conjugate(), MU[1].conjugate()]
    eps = [EPS[0], EPS[1], EPS[0].conjugate(), EPS[1].conjugate()]
    found = [factors(number, cross, v0) for number in mu]

    def crossed(a):
        return (a[0], -(sign * a[1]))

    def times_lanes(v, table):
        return v * table[0] + pltpu.roll(v, 64, 1) * table[1]

    row = lax.broadcasted_iota(jnp.int32, (128, 128), 0).astype(f32)
    turn_ref[:, 0:128] = jnp.where(row == line[7], line[6], 0.0).astype(bf16)
    turn_ref[:, 128:256] = jnp.where(row == line[4], line[6], 0.0).astype(bf16)
    turn_ref[:, 256:384] = jnp.where(row == line[5], -1.0, 0.0).astype(bf16)

    @pl.loop(0, 16)
    def _(at):
        rows = pl.ds(pl.multiple_of(at * 8, 8), 8)
        symbol = (
            diffusion_number * (2.0 * wave_ref[0, rows, :] - 2.0) + cross[0],
            cross[1] - v0 * wave_ref[1, rows, :],
        )
        total = None
        for m in range(4):
            moved = scaled(mu[m], symbol)
            damp = inverse_of((1.0 - moved[0], -moved[1]))
            for k, value in enumerate(crossed(damp)):
                damp_ref[m, k, rows, :] = value
            term = scaled(eps[m], damp)
            if m < 2:
                for k, value in enumerate(crossed(term)):
                    damp_ref[4 + m, k, rows, :] = value
            total = term if total is None else plus(total, term)
        for k, value in enumerate(crossed(total)):
            ratio_ref[k, rows, :] = value
        power = total
        for k in range(5):
            power = times(power, power)
        closing = inverse_of((1.0 - circulant_alpha * power[0], -circulant_alpha * power[1]))
        for k, value in enumerate(crossed(closing)):
            ratio_ref[2 + k, rows, :] = value
        last_ref[rows, :] = jnp.zeros((8, 128), f32)

    first_step = tm - tm % 2
    roots = [crossed(found[m][0]) for m in range(4)]

    @pl.loop(0, STEPS)
    def _(i):
        s = (first_step + i) % STEPS
        block = pl.ds(pl.multiple_of(s * (SLABS * ROWS), 8), SLABS * ROWS)

        @pl.when(s == tm)
        def _():
            remote.wait_got(got_ref.at[rows_of(0, SLABS - 1), :], arrive_sem.at[s])

        @pl.when(s != tm)
        def _():
            remote.wait_got(got_ref.at[rows_of(0, SLABS), :], arrive_sem.at[s])

        high, low = halves(got_ref[block, :])
        both = jnp.concatenate([high, low], axis=0)
        turned = jnp.dot(both, turn_ref[...], preferred_element_type=f32).astype(bf16)
        cut = SLABS * ROWS
        pieces = [high, turned[:cut, :128], low, turned[cut:, :128], high, turned[:cut, :128]]
        mine = jnp.dot(tg_ref[0], jnp.concatenate(pieces, axis=0), preferred_element_type=f32)
        pieces = [
            turned[:cut, 128:256], turned[:cut, 256:], turned[cut:, 128:256], turned[cut:, 256:],
            turned[:cut, 128:256], turned[:cut, 256:],
        ]
        theirs = jnp.dot(tg_ref[1], jnp.concatenate(pieces, axis=0), preferred_element_type=f32)
        total = mine[:128] + theirs[:128]
        for m in range(4):
            out = mine if m < 2 else theirs
            k = m % 2
            point = times_lanes(out[384 + 8 * k : 392 + 8 * k], roots[m])
            d = out[128 + 128 * k : 256 + 128 * k] - jnp.concatenate([point] * 16, axis=0)
            y = times_lanes(d, (damp_ref[m, 0], damp_ref[m, 1]))
            if m < 2:
                kept_ref[s, m] = y
            total = total + y
        drive_ref[s] = total
        wrap = jnp.where(s == 0, circulant_alpha, 1.0).astype(f32)
        last_ref[...] = total + times_lanes(wrap * last_ref[...], (ratio_ref[0], ratio_ref[1]))

    last_ref[...] = times_lanes(last_ref[...], (ratio_ref[2], ratio_ref[3]))
    kappas = [crossed(found[m][2]) for m in range(2)]
    ups = [crossed(found[m][1]) for m in range(2)]
    flip = jnp.concatenate([sign] * 16, axis=0)

    def both_parts(v):
        return jnp.concatenate([v, flip * pltpu.roll(v, 64, 1)], axis=0)

    def send(s):
        for x in range(SLABS):
            target = s * SLABS + x

            @pl.when(target != me)
            def _():
                remote.start(
                    back_ref.at[rows_of(target), :], returned_ref.at[rows_of(owner), :],
                    scatter_sem, return_sem, (s, x),
                )

            @pl.when(target == me)
            def _():
                remote.local(
                    back_ref.at[rows_of(me), :], returned_ref.at[rows_of(owner), :], own_sem
                ).start()

    @pl.loop(0, STEPS)
    def _(i):
        s = (first_step + i) % STEPS
        top = pl.multiple_of(s * (SLABS * ROWS), 8)
        wrap = jnp.where(s == 0, circulant_alpha, 1.0).astype(f32)
        last = wrap * last_ref[...]
        packed = left_dot(tw_ref[...], both_parts(last))
        for x in range(SLABS):
            back_ref[pl.ds(top + x * ROWS, 8), :] = packed[8 * x : 8 * x + 8]
        lines = []
        for m in range(2):
            y = times_lanes(last, (damp_ref[4 + m, 0], damp_ref[4 + m, 1])) + kept_ref[s, m]
            lines.append(both_parts(y))
        ends = left_dot(tb_ref[...], jnp.concatenate(lines, axis=1))
        for m in range(2):
            part = [ends[8 * k : 8 * k + 8, 128 * m : 128 * m + 128] for k in range(3)]
            u = times_lanes(part[0] - times_lanes(part[1], ups[m]), kappas[m])
            back_ref[pl.ds(top + 8 + m * 2, SLABS, stride=ROWS), :] = u
            back_ref[pl.ds(top + 9 + m * 2, SLABS, stride=ROWS), :] = part[2]
        last_ref[...] = drive_ref[s] + times_lanes(last, (ratio_ref[0], ratio_ref[1]))

        @pl.when(i > 0)
        def _():
            send((s + STEPS - 1) % STEPS)

    send((first_step + STEPS - 1) % STEPS)


class Remote:
    def place(self):
        return lax.axis_index("tm"), lax.axis_index("space")

    def start(self, source, target, send_sem, recv_sem, device):
        pltpu.make_async_remote_copy(
            src_ref=source, dst_ref=target, send_sem=send_sem, recv_sem=recv_sem,
            device_id=device, device_id_type=MESH,
        ).start()

    def local(self, source, target, sem):
        return pltpu.make_async_copy(source, target, sem)

    def bytes_of(self, ref, sem):
        return pltpu.make_async_remote_copy(
            src_ref=ref, dst_ref=ref, send_sem=sem, recv_sem=sem,
            device_id=self.place(), device_id_type=MESH,
        )

    def wait_sent(self, ref, sem):
        self.bytes_of(ref, sem).wait_send()

    def wait_got(self, ref, sem):
        self.bytes_of(ref, sem).wait_recv()


VMEM, SMEM, ANY = pltpu.VMEM, pltpu.SMEM, pl.ANY


def spec(space):
    return pl.BlockSpec(memory_space=space)


def shape(*dims):
    return jax.ShapeDtypeStruct(dims, f32)


PARAMS = pltpu.CompilerParams(vmem_limit_bytes=60 * 1024 * 1024)


def sources(velocity, step, iterate, right_side, kappa, interpret=False):
    return pl.pallas_call(
        source_kernel,
        out_shape=(shape(40, 128, 128), shape(8, 64, 128)),
        in_specs=[spec(SMEM)] * 2 + [spec(VMEM)] * 5,
        out_specs=(spec(VMEM), spec(VMEM)),
        scratch_shapes=[VMEM((2560, 256), bf16), VMEM((2560, 256), bf16)],
        compiler_params=PARAMS,
        cost_estimate=pl.CostEstimate(flops=4_000_000_000, bytes_accessed=8_000_000, transcendentals=0),
        interpret=interpret,
        name="sources",
    )(velocity, step, iterate, right_side, kappa, TABLES["ty"], TABLES["tz"])


def slab(velocity, spectra, mixed, below, above, interpret=False):
    return pl.pallas_call(
        slab_kernel,
        out_shape=(shape(32, 128, 128), shape(OWNERS * ROWS, 128)),
        in_specs=[spec(SMEM)] + [spec(VMEM)] * 8,
        out_specs=(spec(VMEM), spec(VMEM)),
        scratch_shapes=[VMEM((4, 128, 128), f32)],
        compiler_params=PARAMS,
        interpret=interpret,
        name="slab",
    )(
        velocity, spectra, mixed, below, above,
        TABLES["ty"], TABLES["tz"], TABLES["lane"], TABLES["row"],
    )


def modes(velocity, sent, remote=Remote(), interpret=False):
    return pl.pallas_call(
        functools.partial(mode_kernel, remote),
        out_shape=shape(OWNERS * ROWS, 128),
        in_specs=[spec(SMEM)] + [spec(VMEM)] * 6,
        out_specs=spec(ANY),
        scratch_shapes=[
            VMEM((STEPS * SLABS * ROWS, 128), f32), VMEM((STEPS * SLABS * ROWS, 128), f32),
            VMEM((6, 2, 128, 128), f32), VMEM((4, 128, 128), f32), VMEM((128, 128), f32),
            VMEM((STEPS, 128, 128), f32), VMEM((STEPS, 2, 128, 128), f32), VMEM((128, 384), bf16),
            pltpu.SemaphoreType.DMA, pltpu.SemaphoreType.DMA((STEPS,)),
            pltpu.SemaphoreType.DMA, pltpu.SemaphoreType.DMA, pltpu.SemaphoreType.DMA,
        ],
        compiler_params=pltpu.CompilerParams(
            vmem_limit_bytes=60 * 1024 * 1024, has_side_effects=True
        ),
        interpret=interpret,
        name="modes",
    )(velocity, TABLES["own"], TABLES["wave_x"], TABLES["tg"], TABLES["tw"], TABLES["tb"], sent)


def backward(velocity, iterate, u, got, interpret=False):
    return pl.pallas_call(
        backward_kernel,
        out_shape=shape(4, WIDE, NZ, NY),
        in_specs=[spec(SMEM)] + [spec(VMEM)] * 7,
        out_specs=spec(VMEM),
        scratch_shapes=[VMEM((32, 128, 128), f32)],
        compiler_params=PARAMS,
        interpret=interpret,
        name="backward",
    )(velocity, iterate, u, got, TABLES["uy"], TABLES["uz"], TABLES["lane"], TABLES["row"])


def shards(iterate, right_side, diffusivity, velocity):
    iterate, right_side = iterate[0], right_side[0]
    tm = lax.axis_index("tm")
    up = [(i, (i + 1) % SLABS) for i in range(SLABS)]
    down = [(i, (i - 1) % SLABS) for i in range(SLABS)]
    below = lax.ppermute(diffusivity[WIDE - 1], "space", up)
    above = lax.ppermute(diffusivity[0], "space", down)
    step = tm.astype(jnp.int32)[None]
    spectra, mixed = sources(velocity, step, iterate, right_side, diffusivity)
    u, sent = slab(velocity, spectra, mixed, below, above)
    returned = modes(velocity, sent)
    return backward(velocity, iterate, u, returned)[None]


def solution(mesh):
    placed = (
        P("tm", None, "space", None, None),
        P("tm", None, "space", None, None),
        P("space", None, None),
        P(),
    )
    return jax.shard_map(
        shards,
        mesh=mesh,
        in_specs=placed,
        out_specs=P("tm", None, "space", None, None),
        check_vma=False,
    )
```

time: 147 us -> 117 us (0.80)
  Pallas kernels: 127 us -> 105 us
  waiting for transfers between devices: 7.1 us -> 0.01 us
    pallas_call x4 -> x3, Pallas kernels: 117 us -> 95.6 us  [the longest x1 76.7 us: modes(): pl.pallas_call(functools.partial(mode_kernel, remote), out_shape=shape(OW...]
    ppermute x1, waiting for transfers between devices: 7.09 us -> 0.01 us  [shards(): below = lax.ppermute(diffusivity[WIDE - 1], 'space', up)]
  transfers between devices with their start and end apart: 2 -> 2, of which waited for: 1 -> 0; matrix products, arithmetic and copies ran while one was open for 1% -> 0% of each run, Pallas kernels for 0% -> 11%
where the time goes in v2:
time: 117 us
  Pallas kernels  105 us (90%)
  starting transfers between devices  9.92 us (8%)
  local copies, waits for them, and re-layouts  1.4 us (1%)
    pallas_call x1, Pallas kernels, modes(): pl.pallas_call(functools.partial(mode_kernel, remote), out_shape=shape(OW...  76.7 us
    pallas_call x1, Pallas kernels, sources(): pl.pallas_call(source_kernel, out_shape=(shape(40, 128, 128), shape(8, 64...  13.3 us
    ppermute x1, starting transfers between devices, shards(): above = lax.ppermute(diffusivity[0], 'space', down)  9.92 us
    pallas_call x1, Pallas kernels, backward(): pl.pallas_call(backward_kernel, out_shape=shape(4, WIDE, NZ, NY), in_spec...  9.57 us
    pallas_call x1, Pallas kernels, slab(): pl.pallas_call(slab_kernel, out_shape=(shape(32, 128, 128), shape(OWNERS...  5.61 us
  transfers between devices with their start and end apart: 2, of which 0 were waited for; matrix products, arithmetic and copies ran while one was open for 0% of the time, Pallas kernels for 11%

profile of v2, /device:TPU:1, one launch (start us, length us, event | category | flops | bytes accessed | tf_op | source)
XLA Modules:
  0.0 116.5 jit_solution(17961786581502686525)
XLA Ops:
  0.0 0.8 slice_bitcast_fusion
  0.8 9.9 %collective-permute-start.1 = (f32[64,128]{1,0:T(8,128)S(1)}, f32[64,128]{1,0:T(8,128)S(1)}, u32[]{:S(2)}, u32[]{:S(2)}) collective-permute-start(f32[64,128]{1,0:T(8,128)S(1)} %get-tuple-element.13), channel_id=1, source_target_pairs={{0,7},{1,0},{2,1},{3,2},{4,3},{5,4},{6,5},{7,6},{8,15},{9,8},{10,9... | collective-permute-start | bytes 98312 | tf_op jit(solution)/shard_map/ppermute | solution.py:913
  10.7 0.0 collective-permute-start
  10.7 13.3 %sources.1 = (f32[40,128,128]{2,1,0:T(8,128)}, f32[8,64,128]{2,1,0:T(8,128)}) custom-call(f32[3]{0:T(128)} %velocity_ref.7, s32[1]{0:T(128)} %bitcast.1.step_ref, f32[4,16,64,128]{3,2,1,0:T(8,128)} %bitcast.8, f32[4,16,64,128]{3,2,1,0:T(8,128)} %bitcast.10, f32[16,64,128]{2,1,0:T(8,128)} %kappa_ref.1, bf16[2,256,256]{2,1,0:T(8,128)(2,1)} %constant.28.clone.ty_ref, ...), custom_call_target="tpu_custom_call" | custom-call | flops 4000000000 | bytes 8000000 | tf_op jit(solution)/shard_map/sources/pallas_call | solution.py:844
  24.0 0.0 collective-permute-done.1.above_ref
  24.0 0.0 copy-start
  24.0 0.0 collective-permute-done.below_ref
  24.0 0.0 copy-start.1
  24.0 0.6 copy-done
  24.6 0.0 copy-done.1
  24.7 5.6 %slab.1 = (f32[32,128,128]{2,1,0:T(8,128)}, f32[1536,128]{1,0:T(8,128)}) custom-call(f32[3]{0:T(128)} %velocity_ref.7, f32[40,128,128]{2,1,0:T(8,128)} %get-tuple-element.9.spec_ref, f32[8,64,128]{2,1,0:T(8,128)} %get-tuple-element.10.mixed_ref, f32[64,128]{1,0:T(8,128)} %copy-done.1, f32[64,128]{1,0:T(8,128)} %copy-done, ...), custom_call_target="tpu_custom_call" | custom-call | tf_op jit(solution)/shard_map/slab/pallas_call | solution.py:858
  30.3 76.7 %modes.1.got_ref = f32[1536,128]{1,0:T(8,128)} custom-call(f32[3]{0:T(128)} %velocity_ref.7, f32[128,8,128]{2,1,0:T(8,128)} %constant.32.clone.own_ref, f32[2,128,128]{2,1,0:T(8,128)} %constant.33.clone.wave_ref, bf16[2,400,576]{2,1,0:T(8,128)(2,1)} %constant.34.clone.tg_ref, bf16[64,768]{1,0:T(8,128)(2,1)} %constant.35.clone.tw_ref, ...), custom_call_target="tpu_custom_call" | custom-call | tf_op jit(solution)/shard_map/modes/pallas_call | solution.py:874
  107.0 9.6 %backward.1 = f32[4,16,64,128]{3,2,1,0:T(8,128)} custom-call(f32[3]{0:T(128)} %velocity_ref.7, f32[4,16,64,128]{3,2,1,0:T(8,128)} %bitcast.9, f32[32,128,128]{2,1,0:T(8,128)} %get-tuple-element.11.u_ref, f32[1536,128]{1,0:T(8,128)} %modes.1.got_ref, bf16[2,256,256]{2,1,0:T(8,128)(2,1)} %constant.37.clone.uy_ref, bf16[128,384]{1,0:T(8,128)(2,1)} %constant.38.clone.uz_ref, ...), custom_call_target="tpu_custom_call" | custom-call | tf_op jit(solution)/shard_map/backward/pallas_call | solution.py:895
Async XLA Ops:
  0.8 23.2 %collective-permute-start.1 = (f32[64,128]{1,0:T(8,128)S(1)}, f32[64,128]{1,0:T(8,128)S(1)}, u32[]{:S(2)}, u32[]{:S(2)}) collective-permute-start(f32[64,128]{1,0:T(8,128)S(1)} %get-tuple-element.13), channel_id=1, source_target_pairs={{0,7},{1,0},{2,1},{3,2},{4,3},{5,4},{6,5},{7,6},{8,15},{9,8},{10,9... | collective-permute-start | bytes 98312 | tf_op jit(solution)/shard_map/ppermute | solution.py:913
  10.7 13.3 %collective-permute-start = (f32[64,128]{1,0:T(8,128)S(1)}, f32[64,128]{1,0:T(8,128)S(1)}, u32[]{:S(2)}, u32[]{:S(2)}) collective-permute-start(f32[64,128]{1,0:T(8,128)S(1)} %get-tuple-element.14), channel_id=1, source_target_pairs={{0,1},{1,2},{2,3},{3,4},{4,5},{5,6},{6,7},{7,0},{8,9},{9,10},{10,1... | collective-permute-start | bytes 98312 | tf_op jit(solution)/shard_map/ppermute | solution.py:912
  24.0 0.6 copy-start
  24.0 0.6 copy-start.1

commit v3 on v2

--- a/solution.py
+++ b/solution.py
@@ -200,29 +200,23 @@
     def lane_block(matrix):
         return np.concatenate([matrix.real, -matrix.imag], axis=1)
 
-    def drive_table(from_x):
-        table = np.zeros((NX, SLABS, ROWS), complex)
-        table[:, :, :8] = from_x.reshape(NX, SLABS, 8)
-        return table
-
-    def point_tables():
+    tables["tg"] = side_table(np.concatenate([lane_block(from_own), lane_block(from_partner)], axis=1))
+
+    def point_rows(waves, shifts):
         out = []
         for m in range(2):
-            table = np.zeros((NX, SLABS, ROWS), complex)
-            table[:, :, 8 + 2 * m] = np.exp(-1j * np.outer(theta, firsts + WIDE))
-            table[:, :, 9 + 2 * m] = np.exp(-1j * np.outer(theta, firsts - 1))
-            out.append(table)
-        for m in range(2):
-            table = np.zeros((8, SLABS, ROWS), complex)
-            table[:, :, 9 + 2 * m] = np.exp(-1j * np.outer(theta[:8], firsts))
-            out.append(table)
+            table = np.zeros((len(waves), 4, SLABS), complex)
+            for field, shift in shifts:
+                table[:, 2 * m + field] = np.exp(-1j * np.outer(waves, firsts + shift))
+            out.append(table.reshape(len(waves), 4 * SLABS))
         return out
 
-    def flat(pieces):
-        return lane_block(np.concatenate(pieces, axis=0).reshape(-1, SLABS * ROWS))
-
-    tables["tg"] = np.stack(
-        [side_table(flat([drive_table(k)] + point_tables())) for k in (from_own, from_partner)]
+    tables["td"] = side_table(
+        lane_block(
+            np.concatenate(
+                point_rows(theta, ((0, WIDE), (1, -1))) + point_rows(theta[:8], ((1, 0),)), axis=0
+            )
+        )
     )
     back = np.exp(1j * np.outer(cells, theta)) * (1 + 1j * np.exp(8j * theta))[None, :] / NX
     tables["tw"] = side_table(lane_block(back))
@@ -602,61 +596,52 @@
 
 
 def mode_kernel(
-    remote, velocity_ref, own_ref, wave_ref, tg_ref, tw_ref, tb_ref, sent_ref,
+    remote, velocity_ref, own_ref, wave_ref, tg_ref, td_ref, tw_ref, tb_ref, sent_ref,
     returned_ref,
     got_ref, back_ref, damp_ref, ratio_ref, last_ref, drive_ref, kept_ref, turn_ref,
-    gather_sem, arrive_sem, scatter_sem, return_sem, own_sem,
+    gather_sem, arrive_sem, swap_out_sem, swap_in_sem, scatter_sem, return_sem, own_sem,
 ):
-    count = STEPS * SLABS
     tm, space = remote.place()
-    is_owner = tm % 2 == 1
+    core = tm % 2
     owner = (tm // 2) * SLABS + space
-    me = tm * SLABS + space
 
     def rows_of(index, number=1):
         return pl.ds(pl.multiple_of(index * ROWS, 4), number * ROWS)
 
-    @pl.loop(0, OWNERS)
+    @pl.loop(1, OWNERS)
     def _(k):
         pair = (tm // 2 + STEPS // 2 - k // SLABS) % (STEPS // 2)
         to_space = ((space // 2 + (k % SLABS) // 2) % (SLABS // 2)) * 2 + (space + k) % 2
-        target = pair * SLABS + to_space
-
-        @pl.when(jnp.logical_not(is_owner) | (k > 0))
-        def _():
-            remote.start(
-                sent_ref.at[rows_of(target), :], got_ref.at[rows_of(me), :],
-                gather_sem, arrive_sem.at[tm], (2 * pair + 1, to_space),
-            )
-
-    @pl.when(is_owner)
-    def _():
-        got_ref[rows_of(me), :] = sent_ref[rows_of(owner), :]
-        solve_modes(
-            remote, owner, tm, me, rows_of,
-            velocity_ref, own_ref, wave_ref, tg_ref, tw_ref, tb_ref,
-            sent_ref, returned_ref,
-            got_ref, back_ref, damp_ref, ratio_ref, last_ref, drive_ref, kept_ref, turn_ref,
-            arrive_sem, scatter_sem, return_sem, own_sem,
+        remote.start(
+            sent_ref.at[rows_of(pair * SLABS + to_space), :],
+            got_ref.at[rows_of((tm // 2) * SLABS + space), :],
+            gather_sem, arrive_sem.at[tm // 2], (2 * pair + core, to_space),
         )
-        remote.wait_sent(sent_ref.at[rows_of(0, OWNERS - 1), :], gather_sem)
-        remote.wait_sent(back_ref.at[rows_of(0, count - 1), :], scatter_sem)
-        remote.local(back_ref.at[rows_of(me), :], returned_ref.at[rows_of(owner), :], own_sem).wait()
-        remote.wait_got(returned_ref.at[rows_of(0, OWNERS - 1), :], return_sem)
-
-    @pl.when(jnp.logical_not(is_owner))
-    def _():
-        remote.wait_sent(sent_ref.at[rows_of(0, OWNERS), :], gather_sem)
-        remote.wait_got(returned_ref.at[rows_of(0, OWNERS), :], return_sem)
+
+    got_ref[rows_of(owner), :] = sent_ref[rows_of(owner), :]
+    solve_modes(
+        remote, 2, owner, tm, space, rows_of,
+        velocity_ref, own_ref, wave_ref, tg_ref, td_ref, tw_ref, tb_ref, returned_ref,
+        got_ref, back_ref, damp_ref, ratio_ref, last_ref, drive_ref, kept_ref, turn_ref,
+        arrive_sem, swap_out_sem, swap_in_sem, scatter_sem, return_sem, own_sem,
+    )
+    remote.wait_sent(sent_ref.at[rows_of(0, OWNERS - 1), :], gather_sem)
+    remote.wait_sent(back_ref.at[rows_of(0, OWNERS - 1), :], scatter_sem)
+    remote.local(back_ref.at[rows_of(owner), :], returned_ref.at[rows_of(owner), :], own_sem).wait()
+    remote.wait_got(returned_ref.at[rows_of(0, OWNERS - 1), :], return_sem)
+
+
+GROUP = 4
 
 
 def solve_modes(
-    remote, owner, tm, me, rows_of,
-    velocity_ref, own_ref, wave_ref, tg_ref, tw_ref, tb_ref,
-    sent_ref, returned_ref,
+    remote, share, owner, tm, space, rows_of,
+    velocity_ref, own_ref, wave_ref, tg_ref, td_ref, tw_ref, tb_ref, returned_ref,
     got_ref, back_ref, damp_ref, ratio_ref, last_ref, drive_ref, kept_ref, turn_ref,
-    arrive_sem, scatter_sem, return_sem, own_sem,
+    arrive_sem, swap_out_sem, swap_in_sem, scatter_sem, return_sem, own_sem,
 ):
+    rounds = STEPS // share // GROUP
+    core = tm % share
     v0, v1, v2 = velocity_ref[0], velocity_ref[1], velocity_ref[2]
     own = own_ref[owner]
     line = [own[k : k + 1, :] for k in range(8)]
@@ -673,10 +658,12 @@
     def times_lanes(v, table):
         return v * table[0] + pltpu.roll(v, 64, 1) * table[1]
 
+    def repeated(v, count):
+        return jnp.concatenate([v] * count, axis=0)
+
     row = lax.broadcasted_iota(jnp.int32, (128, 128), 0).astype(f32)
-    turn_ref[:, 0:128] = jnp.where(row == line[7], line[6], 0.0).astype(bf16)
-    turn_ref[:, 128:256] = jnp.where(row == line[4], line[6], 0.0).astype(bf16)
-    turn_ref[:, 256:384] = jnp.where(row == line[5], -1.0, 0.0).astype(bf16)
+    turn_ref[:, 0:128] = jnp.where(row == line[4], line[6], 0.0).astype(bf16)
+    turn_ref[:, 128:256] = jnp.where(row == line[5], -1.0, 0.0).astype(bf16)
 
     @pl.loop(0, 16)
     def _(at):
@@ -704,100 +691,164 @@
         closing = inverse_of((1.0 - circulant_alpha * power[0], -circulant_alpha * power[1]))
         for k, value in enumerate(crossed(closing)):
             ratio_ref[2 + k, rows, :] = value
-        last_ref[rows, :] = jnp.zeros((8, 128), f32)
 
     first_step = tm - tm % 2
     roots = [crossed(found[m][0]) for m in range(4)]
+    flip = repeated(sign, 12)
+
+    def step_of(i):
+        return (first_step + share * i + core) % STEPS
+
+    def swap(i):
+        remote.start(
+            drive_ref.at[step_of(i)], drive_ref.at[step_of(i)],
+            swap_out_sem, swap_in_sem, (tm + 1 - 2 * core, space),
+        )
+
+    @pl.loop(0, rounds)
+    def _(round_at):
+        values, crossings = [], []
+        for k in range(GROUP):
+            s = step_of(round_at * GROUP + k)
+            slot = s // share
+            top = slot * (SLABS * ROWS)
+
+            @pl.when(s == tm)
+            def _():
+                remote.wait_got(got_ref.at[rows_of(0, SLABS - 1), :], arrive_sem.at[slot])
+
+            @pl.when(s != tm)
+            def _():
+                remote.wait_got(got_ref.at[rows_of(0, SLABS), :], arrive_sem.at[slot])
+
+            pieces = [got_ref[pl.ds(top + x * ROWS, 8), :] for x in range(SLABS)]
+            pieces += [got_ref[pl.ds(top + 8 + f, SLABS, stride=ROWS), :] for f in range(4)]
+            v = jnp.concatenate(pieces, axis=0)
+            values.append(halves(v))
+            crossings.append(halves(flip * pltpu.roll(v, 64, 1)))
+        stacked = jnp.concatenate([half for pair in values for half in pair], axis=0)
+        turned = jnp.dot(stacked, turn_ref[...], preferred_element_type=f32).astype(bf16)
+        columns, own_points, other_points = [], [], []
+        for k in range(GROUP):
+            parts = []
+            for half in range(2):
+                rows = slice(96 * (2 * k + half), 96 * (2 * k + half) + 96)
+                parts.append((values[k][half], crossings[k][half], turned[rows, :128], turned[rows, 128:]))
+            order = (parts[0], parts[1], parts[0])
+            columns.append(jnp.concatenate([piece[:64] for part in order for piece in part], axis=0))
+            own_points.append(jnp.concatenate([piece[64:] for part in order for piece in part[:2]], axis=0))
+            other_points.append(jnp.concatenate([piece[64:] for part in order for piece in part[2:]], axis=0))
+        drive = jnp.dot(tg_ref[...], jnp.concatenate(columns, axis=1), preferred_element_type=f32)
+        points = jnp.dot(
+            td_ref[...], jnp.concatenate(own_points + other_points, axis=1), preferred_element_type=f32
+        )
+        for k in range(GROUP):
+            s = step_of(round_at * GROUP + k)
+            total = drive[:, 128 * k : 128 * k + 128]
+            for m in range(4):
+                at = 128 * (k + GROUP * (m // 2))
+                j = m % 2
+                point = times_lanes(points[256 + 8 * j : 264 + 8 * j, at : at + 128], roots[m])
+                d = points[128 * j : 128 * j + 128, at : at + 128] - repeated(point, 16)
+                y = times_lanes(d, (damp_ref[m, 0], damp_ref[m, 1]))
+                if m < 2:
+                    kept_ref[s // share, m] = y
+                total = total + y
+            drive_ref[s] = total
+        if share > 1:
+            @pl.when(round_at > 0)
+            def _():
+                for k in range(GROUP):
+                    swap((round_at - 1) * GROUP + k)
+
+    if share > 1:
+        for k in range(GROUP):
+            swap((rounds - 1) * GROUP + k)
+        remote.wait_got(drive_ref.at[pl.ds(0, STEPS // 2)], swap_in_sem)
+
+    def wrapped(s, v):
+        return jnp.where(s == 0, circulant_alpha, 1.0).astype(f32) * v
+
+    def following(s, v):
+        return drive_ref[s] + times_lanes(v, (ratio_ref[0], ratio_ref[1]))
+
+    last_ref[...] = jnp.zeros((128, 128), f32)
 
     @pl.loop(0, STEPS)
     def _(i):
         s = (first_step + i) % STEPS
-        block = pl.ds(pl.multiple_of(s * (SLABS * ROWS), 8), SLABS * ROWS)
-
-        @pl.when(s == tm)
-        def _():
-            remote.wait_got(got_ref.at[rows_of(0, SLABS - 1), :], arrive_sem.at[s])
-
-        @pl.when(s != tm)
-        def _():
-            remote.wait_got(got_ref.at[rows_of(0, SLABS), :], arrive_sem.at[s])
-
-        high, low = halves(got_ref[block, :])
-        both = jnp.concatenate([high, low], axis=0)
-        turned = jnp.dot(both, turn_ref[...], preferred_element_type=f32).astype(bf16)
-        cut = SLABS * ROWS
-        pieces = [high, turned[:cut, :128], low, turned[cut:, :128], high, turned[:cut, :128]]
-        mine = jnp.dot(tg_ref[0], jnp.concatenate(pieces, axis=0), preferred_element_type=f32)
-        pieces = [
-            turned[:cut, 128:256], turned[:cut, 256:], turned[cut:, 128:256], turned[cut:, 256:],
-            turned[:cut, 128:256], turned[:cut, 256:],
-        ]
-        theirs = jnp.dot(tg_ref[1], jnp.concatenate(pieces, axis=0), preferred_element_type=f32)
-        total = mine[:128] + theirs[:128]
-        for m in range(4):
-            out = mine if m < 2 else theirs
-            k = m % 2
-            point = times_lanes(out[384 + 8 * k : 392 + 8 * k], roots[m])
-            d = out[128 + 128 * k : 256 + 128 * k] - jnp.concatenate([point] * 16, axis=0)
-            y = times_lanes(d, (damp_ref[m, 0], damp_ref[m, 1]))
-            if m < 2:
-                kept_ref[s, m] = y
-            total = total + y
-        drive_ref[s] = total
-        wrap = jnp.where(s == 0, circulant_alpha, 1.0).astype(f32)
-        last_ref[...] = total + times_lanes(wrap * last_ref[...], (ratio_ref[0], ratio_ref[1]))
+        last_ref[...] = following(s, wrapped(s, last_ref[...]))
 
     last_ref[...] = times_lanes(last_ref[...], (ratio_ref[2], ratio_ref[3]))
     kappas = [crossed(found[m][2]) for m in range(2)]
     ups = [crossed(found[m][1]) for m in range(2)]
-    flip = jnp.concatenate([sign] * 16, axis=0)
+    flip_all = repeated(sign, 16)
 
     def both_parts(v):
-        return jnp.concatenate([v, flip * pltpu.roll(v, 64, 1)], axis=0)
-
-    def send(s):
+        return jnp.concatenate([v, flip_all * pltpu.roll(v, 64, 1)], axis=0)
+
+    def send(i):
+        s = step_of(i)
         for x in range(SLABS):
-            target = s * SLABS + x
-
-            @pl.when(target != me)
+            index = (s // share) * SLABS + x
+
+            @pl.when((s != tm) | (space != x))
             def _():
                 remote.start(
-                    back_ref.at[rows_of(target), :], returned_ref.at[rows_of(owner), :],
+                    back_ref.at[rows_of(index), :], returned_ref.at[rows_of(owner), :],
                     scatter_sem, return_sem, (s, x),
                 )
 
-            @pl.when(target == me)
+            @pl.when((s == tm) & (space == x))
             def _():
                 remote.local(
-                    back_ref.at[rows_of(me), :], returned_ref.at[rows_of(owner), :], own_sem
+                    back_ref.at[rows_of(owner), :], returned_ref.at[rows_of(owner), :], own_sem
                 ).start()
 
-    @pl.loop(0, STEPS)
-    def _(i):
-        s = (first_step + i) % STEPS
-        top = pl.multiple_of(s * (SLABS * ROWS), 8)
-        wrap = jnp.where(s == 0, circulant_alpha, 1.0).astype(f32)
-        last = wrap * last_ref[...]
-        packed = left_dot(tw_ref[...], both_parts(last))
-        for x in range(SLABS):
-            back_ref[pl.ds(top + x * ROWS, 8), :] = packed[8 * x : 8 * x + 8]
+    @pl.loop(0, rounds)
+    def _(round_at):
+        inputs = []
+        last = last_ref[...]
+        for k in range(GROUP):
+            mine = None
+            for c in range(share):
+                s = (first_step + share * (round_at * GROUP + k) + c) % STEPS
+                last = wrapped(s, last)
+                mine = last if mine is None else jnp.where(core == c, last, mine)
+                last = following(s, last)
+            inputs.append(mine)
+        last_ref[...] = last
+        packed = left_dot(tw_ref[...], jnp.concatenate([both_parts(v) for v in inputs], axis=1))
         lines = []
-        for m in range(2):
-            y = times_lanes(last, (damp_ref[4 + m, 0], damp_ref[4 + m, 1])) + kept_ref[s, m]
-            lines.append(both_parts(y))
+        for k in range(GROUP):
+            slot = step_of(round_at * GROUP + k) // share
+            for m in range(2):
+                y = times_lanes(inputs[k], (damp_ref[4 + m, 0], damp_ref[4 + m, 1])) + kept_ref[slot, m]
+                lines.append(both_parts(y))
         ends = left_dot(tb_ref[...], jnp.concatenate(lines, axis=1))
-        for m in range(2):
-            part = [ends[8 * k : 8 * k + 8, 128 * m : 128 * m + 128] for k in range(3)]
-            u = times_lanes(part[0] - times_lanes(part[1], ups[m]), kappas[m])
-            back_ref[pl.ds(top + 8 + m * 2, SLABS, stride=ROWS), :] = u
-            back_ref[pl.ds(top + 9 + m * 2, SLABS, stride=ROWS), :] = part[2]
-        last_ref[...] = drive_ref[s] + times_lanes(last, (ratio_ref[0], ratio_ref[1]))
-
-        @pl.when(i > 0)
+        for k in range(GROUP):
+            top = (step_of(round_at * GROUP + k) // share) * (SLABS * ROWS)
+            for x in range(SLABS):
+                back_ref[pl.ds(top + x * ROWS, 8), :] = packed[8 * x : 8 * x + 8, 128 * k : 128 * k + 128]
+            for m in range(2):
+                at = 128 * (2 * k + m)
+                part = [ends[8 * j : 8 * j + 8, at : at + 128] for j in range(3)]
+                u = times_lanes(part[0] - times_lanes(part[1], ups[m]), kappas[m])
+                back_ref[pl.ds(top + 8 + m * 2, SLABS, stride=ROWS), :] = u
+                back_ref[pl.ds(top + 9 + m * 2, SLABS, stride=ROWS), :] = part[2]
+
+        @pl.when(round_at > 0)
         def _():
-            send((s + STEPS - 1) % STEPS)
-
-    send((first_step + STEPS - 1) % STEPS)
+            @pl.loop(0, GROUP)
+            def _(k):
+                send((round_at - 1) * GROUP + k)
+
+    @pl.loop(0, GROUP)
+    def _(k):
+        send((rounds - 1) * GROUP + k)
+
+    if share > 1:
+        remote.wait_sent(drive_ref.at[pl.ds(0, STEPS // 2)], swap_out_sem)
 
 
 class Remote:
@@ -874,21 +925,20 @@
     return pl.pallas_call(
         functools.partial(mode_kernel, remote),
         out_shape=shape(OWNERS * ROWS, 128),
-        in_specs=[spec(SMEM)] + [spec(VMEM)] * 6,
+        in_specs=[spec(SMEM)] + [spec(VMEM)] * 7,
         out_specs=spec(ANY),
         scratch_shapes=[
-            VMEM((STEPS * SLABS * ROWS, 128), f32), VMEM((STEPS * SLABS * ROWS, 128), f32),
+            VMEM((OWNERS * ROWS, 128), f32), VMEM((OWNERS * ROWS, 128), f32),
             VMEM((6, 2, 128, 128), f32), VMEM((4, 128, 128), f32), VMEM((128, 128), f32),
-            VMEM((STEPS, 128, 128), f32), VMEM((STEPS, 2, 128, 128), f32), VMEM((128, 384), bf16),
-            pltpu.SemaphoreType.DMA, pltpu.SemaphoreType.DMA((STEPS,)),
-            pltpu.SemaphoreType.DMA, pltpu.SemaphoreType.DMA, pltpu.SemaphoreType.DMA,
-        ],
+            VMEM((STEPS, 128, 128), f32), VMEM((STEPS // 2, 2, 128, 128), f32), VMEM((128, 256), bf16),
+            pltpu.SemaphoreType.DMA, pltpu.SemaphoreType.DMA((STEPS // 2,)),
+        ] + [pltpu.SemaphoreType.DMA] * 5,
         compiler_params=pltpu.CompilerParams(
             vmem_limit_bytes=60 * 1024 * 1024, has_side_effects=True
         ),
         interpret=interpret,
         name="modes",
-    )(velocity, TABLES["own"], TABLES["wave_x"], TABLES["tg"], TABLES["tw"], TABLES["tb"], sent)
+    )(velocity, TABLES["own"], TABLES["wave_x"], TABLES["tg"], TABLES["td"], TABLES["tw"], TABLES["tb"], sent)
 
 
 def backward(velocity, iterate, u, got, interpret=False):

time: 117 us -> 110 us (0.940)
  Pallas kernels: 105 us -> 97.9 us
    pallas_call x1, Pallas kernels: 76.7 us -> 69.5 us  [modes(): pl.pallas_call(functools.partial(mode_kernel, remote), out_shape=shape(OW...]
  transfers between devices with their start and end apart: 2 -> 2, of which waited for: 0 -> 0; matrix products, arithmetic and copies ran while one was open for 0% -> 0% of each run, Pallas kernels for 11% -> 12%
where the time goes in v3:
time: 110 us; the launch traced here: 109 us
  Pallas kernels  97.9 us (89%)
  starting transfers between devices  9.92 us (9%)
  local copies, waits for them, and re-layouts  1.4 us (1%)
    pallas_call x1, Pallas kernels, modes(): pl.pallas_call(functools.partial(mode_kernel, remote), out_shape=shape(OW...  69.5 us
    pallas_call x1, Pallas kernels, sources(): pl.pallas_call(source_kernel, out_shape=(shape(40, 128, 128), shape(8, 64...  13.3 us
    ppermute x1, starting transfers between devices, shards(): above = lax.ppermute(diffusivity[0], 'space', down)  9.92 us
    pallas_call x1, Pallas kernels, backward(): pl.pallas_call(backward_kernel, out_shape=shape(4, WIDE, NZ, NY), in_spec...  9.57 us
    pallas_call x1, Pallas kernels, slab(): pl.pallas_call(slab_kernel, out_shape=(shape(32, 128, 128), shape(OWNERS...  5.61 us
  transfers between devices with their start and end apart: 2, of which 0 were waited for; matrix products, arithmetic and copies ran while one was open for 0% of the time, Pallas kernels for 12%

profile of v3, /device:TPU:1, one launch (start us, length us, event | category | flops | bytes accessed | tf_op | source)
XLA Modules:
  0.0 109.3 jit_solution(17429842293888105552)
XLA Ops:
  0.0 0.8 slice_bitcast_fusion
  0.8 9.9 %collective-permute-start.1 = (f32[64,128]{1,0:T(8,128)S(1)}, f32[64,128]{1,0:T(8,128)S(1)}, u32[]{:S(2)}, u32[]{:S(2)}) collective-permute-start(f32[64,128]{1,0:T(8,128)S(1)} %get-tuple-element.13), channel_id=1, source_target_pairs={{0,7},{1,0},{2,1},{3,2},{4,3},{5,4},{6,5},{7,6},{8,15},{9,8},{10,9... | collective-permute-start | bytes 98312 | tf_op jit(solution)/shard_map/ppermute | solution.py:963
  10.7 0.0 collective-permute-start
  10.7 13.3 %sources.1 = (f32[40,128,128]{2,1,0:T(8,128)}, f32[8,64,128]{2,1,0:T(8,128)}) custom-call(f32[3]{0:T(128)} %velocity_ref.7, s32[1]{0:T(128)} %bitcast.1.step_ref, f32[4,16,64,128]{3,2,1,0:T(8,128)} %bitcast.8, f32[4,16,64,128]{3,2,1,0:T(8,128)} %bitcast.10, f32[16,64,128]{2,1,0:T(8,128)} %kappa_ref.1, bf16[2,256,256]{2,1,0:T(8,128)(2,1)} %constant.30.clone.ty_ref, ...), custom_call_target="tpu_custom_call" | custom-call | flops 4000000000 | bytes 8000000 | tf_op jit(solution)/shard_map/sources/pallas_call | solution.py:895
  24.0 0.0 collective-permute-done.1.above_ref
  24.0 0.0 copy-start
  24.0 0.0 collective-permute-done.below_ref
  24.0 0.0 copy-start.1
  24.0 0.6 copy-done
  24.6 0.0 copy-done.1
  24.7 5.6 %slab.1 = (f32[32,128,128]{2,1,0:T(8,128)}, f32[1536,128]{1,0:T(8,128)}) custom-call(f32[3]{0:T(128)} %velocity_ref.7, f32[40,128,128]{2,1,0:T(8,128)} %get-tuple-element.9.spec_ref, f32[8,64,128]{2,1,0:T(8,128)} %get-tuple-element.10.mixed_ref, f32[64,128]{1,0:T(8,128)} %copy-done.1, f32[64,128]{1,0:T(8,128)} %copy-done, ...), custom_call_target="tpu_custom_call" | custom-call | tf_op jit(solution)/shard_map/slab/pallas_call | solution.py:909
  30.3 69.5 %modes.1.got_ref = f32[1536,128]{1,0:T(8,128)} custom-call(f32[3]{0:T(128)} %velocity_ref.7, f32[128,8,128]{2,1,0:T(8,128)} %constant.34.clone.own_ref, f32[2,128,128]{2,1,0:T(8,128)} %constant.35.clone.wave_ref, bf16[128,768]{1,0:T(8,128)(2,1)} %constant.36.clone.tg_ref, bf16[272,192]{1,0:T(8,128)(2,1)} %constant.37.clone.td_ref, ...), custom_call_target="tpu_custom_call" | custom-call | tf_op jit(solution)/shard_map/modes/pallas_call | solution.py:925
  99.7 9.6 %backward.1 = f32[4,16,64,128]{3,2,1,0:T(8,128)} custom-call(f32[3]{0:T(128)} %velocity_ref.7, f32[4,16,64,128]{3,2,1,0:T(8,128)} %bitcast.9, f32[32,128,128]{2,1,0:T(8,128)} %get-tuple-element.11.u_ref, f32[1536,128]{1,0:T(8,128)} %modes.1.got_ref, bf16[2,256,256]{2,1,0:T(8,128)(2,1)} %constant.40.clone.uy_ref, bf16[128,384]{1,0:T(8,128)(2,1)} %constant.41.clone.uz_ref, ...), custom_call_target="tpu_custom_call" | custom-call | tf_op jit(solution)/shard_map/backward/pallas_call | solution.py:945
Async XLA Ops:
  0.8 23.2 %collective-permute-start.1 = (f32[64,128]{1,0:T(8,128)S(1)}, f32[64,128]{1,0:T(8,128)S(1)}, u32[]{:S(2)}, u32[]{:S(2)}) collective-permute-start(f32[64,128]{1,0:T(8,128)S(1)} %get-tuple-element.13), channel_id=1, source_target_pairs={{0,7},{1,0},{2,1},{3,2},{4,3},{5,4},{6,5},{7,6},{8,15},{9,8},{10,9... | collective-permute-start | bytes 98312 | tf_op jit(solution)/shard_map/ppermute | solution.py:963
  10.7 13.3 %collective-permute-start = (f32[64,128]{1,0:T(8,128)S(1)}, f32[64,128]{1,0:T(8,128)S(1)}, u32[]{:S(2)}, u32[]{:S(2)}) collective-permute-start(f32[64,128]{1,0:T(8,128)S(1)} %get-tuple-element.14), channel_id=1, source_target_pairs={{0,1},{1,2},{2,3},{3,4},{4,5},{5,6},{6,7},{7,0},{8,9},{9,10},{10,1... | collective-permute-start | bytes 98312 | tf_op jit(solution)/shard_map/ppermute | solution.py:962
  24.0 0.6 copy-start
  24.0 0.6 copy-start.1

commit v4 on v3

--- a/solution.py
+++ b/solution.py
@@ -371,33 +371,31 @@
     return left_dot(tz_ref[...], stacked)
 
 
-def source_kernel(
-    velocity_ref, step_ref, iterate_ref, right_ref, kappa_ref, ty_ref, tz_ref,
-    spec_ref, mixed_ref,
-    high_ref, low_ref,
+def put_rows(slot, at, real, imag):
+    for k, part in enumerate((real, imag)):
+        for ref, value in zip(slot, halves(part)):
+            ref[64 * at : 64 * at + 64, k * 128 : (k + 1) * 128] = value
+
+
+def mixture(m, groups):
+    real = imag = None
+    for scale, values in groups:
+        for n in range(4):
+            factor = scale * ROW[m][n]
+            a, b = factor.real * values[n], factor.imag * values[n]
+            real = a if real is None else real + a
+            imag = b if imag is None else imag + b
+    return real, imag
+
+
+def source_stage(
+    keep, middle, velocity_ref, iterate_ref, right_ref, kappa_ref, ty_ref, tz_ref, spec_ref, mixed_ref, slots,
 ):
     v0, v1, v2 = velocity_ref[0], velocity_ref[1], velocity_ref[2]
 
-    def put(at, real, imag):
-        rows = pl.ds(pl.multiple_of(at * 64, 64), 64)
-        for k, part in enumerate((real, imag)):
-            high, low = halves(part)
-            high_ref[rows, k * 128 : (k + 1) * 128] = high
-            low_ref[rows, k * 128 : (k + 1) * 128] = low
-
-    def mixture(m, groups):
-        real = imag = None
-        for scale, values in groups:
-            for n in range(4):
-                factor = scale * ROW[m][n]
-                a, b = factor.real * values[n], factor.imag * values[n]
-                real = a if real is None else real + a
-                imag = b if imag is None else imag + b
-        return real, imag
-
-    def inner(x, below, above):
+    def stencil(x, slot, at, below, above):
         plain, applied = [], []
-        kappa = kappa_ref[x]
+        kappa = diffusion_number * kappa_ref[x]
         for n in range(4):
             f = iterate_ref[n, x]
             up_z, down_z = pltpu.roll(f, NZ - 1, 0), pltpu.roll(f, 1, 0)
@@ -410,42 +408,53 @@
             if below:
                 down_x = iterate_ref[n, x - 1]
                 total, moved = total + down_x, moved - v0 * down_x
-            applied.append((diffusion_number * kappa) * total - 0.5 * moved)
+            applied.append(kappa * total - 0.5 * moved)
             plain.append(right_ref[n, x] - f)
         for m in range(2):
-            real, imag = mixture(m, [(1.0, plain), (MU[m], applied)])
-            put(m * 16 + x, real, imag)
+            put_rows(slot, 2 * m + at, *mixture(m, [(1.0, plain), (MU[m], applied)]))
+
+    def produce(block, slot, first=False, final=False):
+        stencil(2 * block, slot, 0, not first, True)
+        stencil(2 * block + 1, slot, 1, True, not final)
+
+    def last_node(block, slot):
+        for k in range(4):
+            x = 4 * block + k
+            put_rows(slot, k, keep * iterate_ref[3, x], keep * iterate_ref[3, x + 8])
+
+    def transformed(block, slot):
+        out = dft_block(slot[0][...], slot[1][...], ty_ref, tz_ref)
+        for k in range(4):
+            spec_ref[block * 4 + k] = out[:, 128 * k : 128 * k + 128]
 
     for side, x in enumerate((0, WIDE - 1)):
         for m in range(2):
             real, imag = mixture(m, [(MU[m], [iterate_ref[n, x] for n in range(4)])])
             mixed_ref[side * 4 + m * 2] = real
             mixed_ref[side * 4 + m * 2 + 1] = imag
-    inner(0, False, True)
-    inner(WIDE - 1, True, False)
-
-    @pl.loop(1, WIDE - 1)
-    def _(x):
-        inner(x, True, True)
-
-    keep = jnp.where(step_ref[0] < STEPS - 1, 1.0, 0.0).astype(f32)
-
-    @pl.loop(0, 8)
-    def _(x):
-        put(32 + x, keep * iterate_ref[3, x], keep * iterate_ref[3, x + 8])
-
-    @pl.loop(0, 10)
-    def _(block):
-        rows = pl.ds(pl.multiple_of(block * 256, 256), 256)
-        out = dft_block(high_ref[rows, :], low_ref[rows, :], ty_ref, tz_ref)
-        for k in range(4):
-            spec_ref[block * 4 + k] = out[:, 128 * k : 128 * k + 128]
-
-
-def slab_kernel(
+    first, second = slots
+    produce(0, first, first=True)
+
+    @pl.loop(0, 3)
+    def _(i):
+        transformed(2 * i, first)
+        produce(2 * i + 1, second)
+        transformed(2 * i + 1, second)
+        produce(2 * i + 2, first)
+
+    middle()
+    transformed(6, first)
+    produce(7, second, final=True)
+    transformed(7, second)
+    last_node(0, first)
+    transformed(8, first)
+    last_node(1, second)
+    transformed(9, second)
+
+
+def slab_stage(
     velocity_ref, spec_ref, mixed_ref, below_ref, above_ref, ty_ref, tz_ref, lane_ref, row_ref,
     u_ref, send_ref,
-    edge_ref,
 ):
     v0 = velocity_ref[0]
     outer = [diffusion_number * below_ref[...] - 0.5 * v0, diffusion_number * above_ref[...] + 0.5 * v0]
@@ -457,7 +466,7 @@
     high, low = halves(jnp.concatenate(edges, axis=0))
     out = dft_block(high, low, ty_ref, tz_ref)
     for k in range(4):
-        edge_ref[k] = out[:, 128 * k : 128 * k + 128]
+        spec_ref[40 + k] = out[:, 128 * k : 128 * k + 128]
 
     lane = lax.broadcasted_iota(jnp.int32, (8, 128), 1)
     sub = lax.broadcasted_iota(jnp.int32, (8, 128), 0)
@@ -469,8 +478,11 @@
         found = chunk_factors(t, lane_ref, row_ref, velocity_ref, MU)
         bases = [pl.multiple_of(base + 8 * t, 8) for base in (0, 32)]
 
-        def plane(at, base, ref=spec_ref):
-            return ref[at, pl.ds(base, 8), :], ref[at, pl.ds(base + 64, 8), :]
+        def plane(at, base):
+            return spec_ref[at, pl.ds(base, 8), :], spec_ref[at, pl.ds(base + 64, 8), :]
+
+        def field(m, x, base):
+            return plane(4 * (x // 2) + 2 * m + x % 2, base)
 
         def send(value, low, high):
             for h, packed in enumerate(packed_for(low, high, block)):
@@ -482,11 +494,11 @@
             for half in range(2):
                 base = bases[half]
                 p, q, kappa, inv = found[half][m]
-                under, over = plane(m * 2, base, edge_ref), plane(m * 2 + 1, base, edge_ref)
-                u = plus(plane(m * 16, base), times(p, under))
+                under, over = plane(40 + 2 * m, base), plane(41 + 2 * m, base)
+                u = plus(field(m, 0, base), times(p, under))
                 us = [u]
                 for x in range(1, WIDE):
-                    u = plus(plane(m * 16 + x, base), times(p, u))
+                    u = plus(field(m, x, base), times(p, u))
                     us.append(u)
                 for x in range(WIDE):
                     u_ref[m * 16 + x, pl.ds(base, 8), :] = us[x][0]
@@ -595,10 +607,13 @@
                 out_ref[n, x] = total
 
 
-def mode_kernel(
-    remote, velocity_ref, own_ref, wave_ref, tg_ref, td_ref, tw_ref, tb_ref, sent_ref,
-    returned_ref,
+def whole_kernel(
+    remote, velocity_ref, iterate_ref, right_ref, kappa_ref,
+    ty_ref, tz_ref, lane_ref, row_ref, own_ref, wave_ref, tg_ref, td_ref, tw_ref, tb_ref,
+    u_ref, returned_ref,
+    high_a, low_a, high_b, low_b, spec_ref, mixed_ref, below_ref, above_ref, sent_ref,
     got_ref, back_ref, damp_ref, ratio_ref, last_ref, drive_ref, kept_ref, turn_ref,
+    edge_out_sem, below_sem, above_sem,
     gather_sem, arrive_sem, swap_out_sem, swap_in_sem, scatter_sem, return_sem, own_sem,
 ):
     tm, space = remote.place()
@@ -608,10 +623,38 @@
     def rows_of(index, number=1):
         return pl.ds(pl.multiple_of(index * ROWS, 4), number * ROWS)
 
+    def other(k):
+        pair = (tm // 2 + STEPS // 2 - k // SLABS) % (STEPS // 2)
+        to_space = ((space // 2 + (k % SLABS) // 2) % (SLABS // 2)) * 2 + (space + k) % 2
+        return pair, to_space
+
+    remote.greet((tm + 1 - 2 * core, space))
+
     @pl.loop(1, OWNERS)
     def _(k):
-        pair = (tm // 2 + STEPS // 2 - k // SLABS) % (STEPS // 2)
-        to_space = ((space // 2 + (k % SLABS) // 2) % (SLABS // 2)) * 2 + (space + k) % 2
+        pair, to_space = other(k)
+        remote.greet((2 * pair + core, to_space))
+
+    def middle():
+        remote.all_here(OWNERS)
+        remote.start(kappa_ref.at[WIDE - 1], below_ref, edge_out_sem, below_sem, (tm, (space + 1) % SLABS))
+        remote.start(kappa_ref.at[0], above_ref, edge_out_sem, above_sem, (tm, (space + SLABS - 1) % SLABS))
+
+    keep = jnp.where(tm < STEPS - 1, 1.0, 0.0).astype(f32)
+    source_stage(
+        keep, middle, velocity_ref, iterate_ref, right_ref, kappa_ref, ty_ref, tz_ref, spec_ref, mixed_ref,
+        ((high_a, low_a), (high_b, low_b)),
+    )
+    remote.wait_got(below_ref, below_sem)
+    remote.wait_got(above_ref, above_sem)
+    slab_stage(
+        velocity_ref, spec_ref, mixed_ref, below_ref, above_ref, ty_ref, tz_ref, lane_ref, row_ref,
+        u_ref, sent_ref,
+    )
+
+    @pl.loop(1, OWNERS)
+    def _(k):
+        pair, to_space = other(k)
         remote.start(
             sent_ref.at[rows_of(pair * SLABS + to_space), :],
             got_ref.at[rows_of((tm // 2) * SLABS + space), :],
@@ -625,6 +668,7 @@
         got_ref, back_ref, damp_ref, ratio_ref, last_ref, drive_ref, kept_ref, turn_ref,
         arrive_sem, swap_out_sem, swap_in_sem, scatter_sem, return_sem, own_sem,
     )
+    remote.wait_sent(kappa_ref.at[pl.ds(0, 2)], edge_out_sem)
     remote.wait_sent(sent_ref.at[rows_of(0, OWNERS - 1), :], gather_sem)
     remote.wait_sent(back_ref.at[rows_of(0, OWNERS - 1), :], scatter_sem)
     remote.local(back_ref.at[rows_of(owner), :], returned_ref.at[rows_of(owner), :], own_sem).wait()
@@ -855,6 +899,14 @@
     def place(self):
         return lax.axis_index("tm"), lax.axis_index("space")
 
+    def greet(self, device):
+        pl.semaphore_signal(
+            pltpu.get_barrier_semaphore(), inc=1, device_id=device, device_id_type=MESH
+        )
+
+    def all_here(self, count):
+        pl.semaphore_wait(pltpu.get_barrier_semaphore(), count)
+
     def start(self, source, target, send_sem, recv_sem, device):
         pltpu.make_async_remote_copy(
             src_ref=source, dst_ref=target, send_sem=send_sem, recv_sem=recv_sem,
@@ -891,54 +943,32 @@
 PARAMS = pltpu.CompilerParams(vmem_limit_bytes=60 * 1024 * 1024)
 
 
-def sources(velocity, step, iterate, right_side, kappa, interpret=False):
+def whole(velocity, iterate, right_side, kappa, remote=Remote(), interpret=False):
+    dma = pltpu.SemaphoreType.DMA
     return pl.pallas_call(
-        source_kernel,
-        out_shape=(shape(40, 128, 128), shape(8, 64, 128)),
-        in_specs=[spec(SMEM)] * 2 + [spec(VMEM)] * 5,
-        out_specs=(spec(VMEM), spec(VMEM)),
-        scratch_shapes=[VMEM((2560, 256), bf16), VMEM((2560, 256), bf16)],
-        compiler_params=PARAMS,
-        cost_estimate=pl.CostEstimate(flops=4_000_000_000, bytes_accessed=8_000_000, transcendentals=0),
-        interpret=interpret,
-        name="sources",
-    )(velocity, step, iterate, right_side, kappa, TABLES["ty"], TABLES["tz"])
-
-
-def slab(velocity, spectra, mixed, below, above, interpret=False):
-    return pl.pallas_call(
-        slab_kernel,
+        functools.partial(whole_kernel, remote),
         out_shape=(shape(32, 128, 128), shape(OWNERS * ROWS, 128)),
-        in_specs=[spec(SMEM)] + [spec(VMEM)] * 8,
-        out_specs=(spec(VMEM), spec(VMEM)),
-        scratch_shapes=[VMEM((4, 128, 128), f32)],
-        compiler_params=PARAMS,
-        interpret=interpret,
-        name="slab",
-    )(
-        velocity, spectra, mixed, below, above,
-        TABLES["ty"], TABLES["tz"], TABLES["lane"], TABLES["row"],
-    )
-
-
-def modes(velocity, sent, remote=Remote(), interpret=False):
-    return pl.pallas_call(
-        functools.partial(mode_kernel, remote),
-        out_shape=shape(OWNERS * ROWS, 128),
-        in_specs=[spec(SMEM)] + [spec(VMEM)] * 7,
-        out_specs=spec(ANY),
-        scratch_shapes=[
+        in_specs=[spec(SMEM)] + [spec(VMEM)] * 13,
+        out_specs=(spec(VMEM), spec(ANY)),
+        scratch_shapes=[VMEM((256, 256), bf16)] * 4
+        + [
+            VMEM((44, 128, 128), f32), VMEM((8, NZ, NY), f32), VMEM((NZ, NY), f32), VMEM((NZ, NY), f32),
+            VMEM((OWNERS * ROWS, 128), f32),
             VMEM((OWNERS * ROWS, 128), f32), VMEM((OWNERS * ROWS, 128), f32),
             VMEM((6, 2, 128, 128), f32), VMEM((4, 128, 128), f32), VMEM((128, 128), f32),
             VMEM((STEPS, 128, 128), f32), VMEM((STEPS // 2, 2, 128, 128), f32), VMEM((128, 256), bf16),
-            pltpu.SemaphoreType.DMA, pltpu.SemaphoreType.DMA((STEPS // 2,)),
-        ] + [pltpu.SemaphoreType.DMA] * 5,
+            dma, dma, dma, dma, dma((STEPS // 2,)), dma, dma, dma, dma, dma,
+        ],
         compiler_params=pltpu.CompilerParams(
-            vmem_limit_bytes=60 * 1024 * 1024, has_side_effects=True
+            vmem_limit_bytes=60 * 1024 * 1024, has_side_effects=True, collective_id=0
         ),
         interpret=interpret,
-        name="modes",
-    )(velocity, TABLES["own"], TABLES["wave_x"], TABLES["tg"], TABLES["td"], TABLES["tw"], TABLES["tb"], sent)
+        name="whole",
+    )(
+        velocity, iterate, right_side, kappa,
+        TABLES["ty"], TABLES["tz"], TABLES["lane"], TABLES["row"], TABLES["own"], TABLES["wave_x"],
+        TABLES["tg"], TABLES["td"], TABLES["tw"], TABLES["tb"],
+    )
 
 
 def backward(velocity, iterate, u, got, interpret=False):
@@ -956,15 +986,7 @@
 
 def shards(iterate, right_side, diffusivity, velocity):
     iterate, right_side = iterate[0], right_side[0]
-    tm = lax.axis_index("tm")
-    up = [(i, (i + 1) % SLABS) for i in range(SLABS)]
-    down = [(i, (i - 1) % SLABS) for i in range(SLABS)]
-    below = lax.ppermute(diffusivity[WIDE - 1], "space", up)
-    above = lax.ppermute(diffusivity[0], "space", down)
-    step = tm.astype(jnp.int32)[None]
-    spectra, mixed = sources(velocity, step, iterate, right_side, diffusivity)
-    u, sent = slab(velocity, spectra, mixed, below, above)
-    returned = modes(velocity, sent)
+    u, returned = whole(velocity, iterate, right_side, diffusivity)
     return backward(velocity, iterate, u, returned)[None]
 
 

time: 110 us -> 88.3 us (0.80)
  Pallas kernels: 97.9 us -> 86.9 us
  starting transfers between devices: 9.92 us -> 0 us
  local copies, waits for them, and re-layouts: 1.4 us -> 0 us
    pallas_call x3 -> x1, Pallas kernels: 88.4 us -> 77.3 us  [whole(): pl.pallas_call(functools.partial(whole_kernel, remote), out_shape=(shape(...]
    ppermute x2 -> x0, starting transfers between devices: 9.92 us -> none  [the longest x1 9.92 us: shards(): above = lax.ppermute(diffusivity[0], 'space', down)]
  transfers between devices with their start and end apart: 2 -> 0, of which waited for: 0 -> 0; matrix products, arithmetic and copies ran while one was open for 0% -> 0% of each run, Pallas kernels for 12% -> 0%
where the time goes in v4:
time: 88.3 us; the launch traced here: 86.9 us
  Pallas kernels  86.9 us (98%)
    pallas_call x1, Pallas kernels, whole(): pl.pallas_call(functools.partial(whole_kernel, remote), out_shape=(shape(...  77.3 us
    pallas_call x1, Pallas kernels, backward(): pl.pallas_call(backward_kernel, out_shape=shape(4, WIDE, NZ, NY), in_spec...  9.57 us

profile of v4, /device:TPU:1, one launch (start us, length us, event | category | flops | bytes accessed | tf_op | source)
XLA Modules:
  0.0 86.9 jit_solution(11707660442256675762)
XLA Ops:
  0.0 77.3 %whole.1 = (f32[32,128,128]{2,1,0:T(8,128)}, f32[1536,128]{1,0:T(8,128)}) custom-call(f32[3]{0:T(128)} %velocity_ref.3, f32[4,16,64,128]{3,2,1,0:T(8,128)} %bitcast.3, f32[4,16,64,128]{3,2,1,0:T(8,128)} %bitcast.5, f32[16,64,128]{2,1,0:T(8,128)} %kappa_ref.1, bf16[2,256,256]{2,1,0:T(8,128)(2,1)} %constant.24.clone.ty_ref, ...), custom_call_target="tpu_custom_call" | custom-call | tf_op jit(solution)/shard_map/whole/pallas_call | solution.py:948
  77.3 9.6 %backward.1 = f32[4,16,64,128]{3,2,1,0:T(8,128)} custom-call(f32[3]{0:T(128)} %velocity_ref.3, f32[4,16,64,128]{3,2,1,0:T(8,128)} %bitcast.4, f32[32,128,128]{2,1,0:T(8,128)} %get-tuple-element.7.u_ref, f32[1536,128]{1,0:T(8,128)} %get-tuple-element.8.got_ref, bf16[2,256,256]{2,1,0:T(8,128)(2,1)} %constant.34.clone.uy_ref, ...), custom_call_target="tpu_custom_call" | custom-call | tf_op jit(solution)/shard_map/backward/pallas_call | solution.py:975

commit v5 on v4

--- a/solution.py
+++ b/solution.py
@@ -389,7 +389,7 @@
 
 
 def source_stage(
-    keep, middle, velocity_ref, iterate_ref, right_ref, kappa_ref, ty_ref, tz_ref, spec_ref, mixed_ref, slots,
+    keep, ready, middle, velocity_ref, iterate_ref, right_ref, kappa_ref, ty_ref, tz_ref, spec_ref, mixed_ref, slots,
 ):
     v0, v1, v2 = velocity_ref[0], velocity_ref[1], velocity_ref[2]
 
@@ -427,22 +427,26 @@
         for k in range(4):
             spec_ref[block * 4 + k] = out[:, 128 * k : 128 * k + 128]
 
+    first, second = slots
+    ready(0)
+    ready(1)
+    produce(0, first, first=True)
+
+    @pl.loop(0, 3)
+    def _(i):
+        ready(2 * i + 2)
+        transformed(2 * i, first)
+        produce(2 * i + 1, second)
+        ready(2 * i + 3)
+        transformed(2 * i + 1, second)
+        produce(2 * i + 2, first)
+
+    middle()
     for side, x in enumerate((0, WIDE - 1)):
         for m in range(2):
             real, imag = mixture(m, [(MU[m], [iterate_ref[n, x] for n in range(4)])])
             mixed_ref[side * 4 + m * 2] = real
             mixed_ref[side * 4 + m * 2 + 1] = imag
-    first, second = slots
-    produce(0, first, first=True)
-
-    @pl.loop(0, 3)
-    def _(i):
-        transformed(2 * i, first)
-        produce(2 * i + 1, second)
-        transformed(2 * i + 1, second)
-        produce(2 * i + 2, first)
-
-    middle()
     transformed(6, first)
     produce(7, second, final=True)
     transformed(7, second)
@@ -527,10 +531,12 @@
 
 
 def backward_kernel(
-    velocity_ref, iterate_ref, u_ref, got_ref, uy_ref, uz_ref, lane_ref, row_ref,
-    out_ref,
-    spec_ref,
+    velocity_ref, iterate_hbm, u_ref, got_ref, uy_ref, uz_ref, lane_ref, row_ref,
+    out_hbm,
+    spec_ref, iterate_ref, out_ref, load_sem, store_sem,
 ):
+    load = pltpu.make_async_copy(iterate_hbm, iterate_ref, load_sem)
+    load.start()
     lane = lax.broadcasted_iota(jnp.int32, (8, 128), 1)
     sub = lax.broadcasted_iota(jnp.int32, (8, 128), 0)
     block = lane // 32
@@ -579,8 +585,9 @@
                     spec_ref[m * 16 + x, pl.ds(base, 8), :] = y[0]
                     spec_ref[m * 16 + x, pl.ds(base + 64, 8), :] = y[1]
 
-    @pl.loop(0, 8)
-    def _(block):
+    load.wait()
+
+    def finished(block):
         planes = [2 * block, 2 * block + 1, 16 + 2 * block, 17 + 2 * block]
         stacked = jnp.concatenate([spec_ref[at] for at in planes], axis=1)
         mid = left_dot(uz_ref[...], stacked)
@@ -592,7 +599,13 @@
             axis=0,
         )
         high, low = halves(rows)
-        out = right_dot(high, low, uy_ref[0], uy_ref[1])
+        return right_dot(high, low, uy_ref[0], uy_ref[1])
+
+    def store(block):
+        planes = pl.ds(2 * block, 2)
+        return pltpu.make_async_copy(out_ref.at[:, planes], out_hbm.at[:, planes], store_sem.at[block])
+
+    def added(block, out):
         for k in range(2):
             x = 2 * block + k
             parts = []
@@ -606,44 +619,92 @@
                     total = total + (2.0 * c.real) * parts[m][0] - (2.0 * c.imag) * parts[m][1]
                 out_ref[n, x] = total
 
+    @pl.loop(0, 4)
+    def _(i):
+        blocks = (2 * i, 2 * i + 1)
+        outs = [finished(block) for block in blocks]
+        for block, out in zip(blocks, outs):
+            added(block, out)
+
+        @pl.when(i > 0)
+        def _():
+            store(2 * i - 2).start()
+            store(2 * i - 1).start()
+
+    store(6).start()
+    store(7).start()
+
+    @pl.loop(0, 8)
+    def _(block):
+        store(block).wait()
+
+
+def other_places(tm, space, work):
+    pair = lax.div(tm, 2)
+    x, side = lax.div(space, 2), lax.rem(space, 2)
+    places = [
+        lax.rem(x + k // 2, SLABS // 2) * 2 + lax.rem(side + k, 2) for k in range(SLABS)
+    ]
+    for k in range(1, SLABS):
+        work(pair, places[k])
+
+    @pl.loop(1, STEPS // 2)
+    def _(i):
+        other = lax.rem(pair + STEPS // 2 - i, STEPS // 2)
+        for k in range(SLABS):
+            work(other, places[k])
+
 
 def whole_kernel(
-    remote, velocity_ref, iterate_ref, right_ref, kappa_ref,
+    remote, velocity_ref, iterate_hbm, right_hbm, kappa_hbm,
     ty_ref, tz_ref, lane_ref, row_ref, own_ref, wave_ref, tg_ref, td_ref, tw_ref, tb_ref,
-    u_ref, returned_ref,
+    u_hbm, returned_ref,
+    iterate_ref, right_ref, kappa_ref, u_ref,
     high_a, low_a, high_b, low_b, spec_ref, mixed_ref, below_ref, above_ref, sent_ref,
-    got_ref, back_ref, damp_ref, ratio_ref, last_ref, drive_ref, kept_ref, turn_ref,
-    edge_out_sem, below_sem, above_sem,
-    gather_sem, arrive_sem, swap_out_sem, swap_in_sem, scatter_sem, return_sem, own_sem,
+    got_ref, back_ref, damp_ref, ratio_ref, last_ref, mate_ref, drive_ref, kept_ref, turn_ref,
+    load_sem, u_sem, edge_out_sem, below_sem, above_sem,
+    gather_sem, arrive_sem, swap_out_sem, swap_in_sem, mate_out_sem, mate_in_sem,
+    scatter_sem, return_sem, own_sem,
 ):
     tm, space = remote.place()
-    core = tm % 2
-    owner = (tm // 2) * SLABS + space
+    core = lax.rem(tm, 2)
+    owner = lax.div(tm, 2) * SLABS + space
 
     def rows_of(index, number=1):
         return pl.ds(pl.multiple_of(index * ROWS, 4), number * ROWS)
 
-    def other(k):
-        pair = (tm // 2 + STEPS // 2 - k // SLABS) % (STEPS // 2)
-        to_space = ((space // 2 + (k % SLABS) // 2) % (SLABS // 2)) * 2 + (space + k) % 2
-        return pair, to_space
+    def loads(piece):
+        planes = pl.ds(2 * piece, 2)
+        return [
+            remote.local(iterate_hbm.at[:, planes], iterate_ref.at[:, planes], load_sem.at[0, piece]),
+            remote.local(right_hbm.at[:, planes], right_ref.at[:, planes], load_sem.at[1, piece]),
+            remote.local(kappa_hbm.at[planes], kappa_ref.at[planes], load_sem.at[2, piece]),
+        ]
+
+    for piece in range(8):
+        for copy in loads(piece):
+            copy.start()
+
+    def ready(piece):
+        for copy in loads(piece):
+            copy.wait()
 
     remote.greet((tm + 1 - 2 * core, space))
-
-    @pl.loop(1, OWNERS)
-    def _(k):
-        pair, to_space = other(k)
-        remote.greet((2 * pair + core, to_space))
+    other_places(tm, space, lambda pair, place: remote.greet((2 * pair + core, place)))
 
     def middle():
         remote.all_here(OWNERS)
-        remote.start(kappa_ref.at[WIDE - 1], below_ref, edge_out_sem, below_sem, (tm, (space + 1) % SLABS))
-        remote.start(kappa_ref.at[0], above_ref, edge_out_sem, above_sem, (tm, (space + SLABS - 1) % SLABS))
+        remote.start(
+            kappa_ref.at[WIDE - 1], below_ref, edge_out_sem, below_sem, (tm, lax.rem(space + 1, SLABS))
+        )
+        remote.start(
+            kappa_ref.at[0], above_ref, edge_out_sem, above_sem, (tm, lax.rem(space + SLABS - 1, SLABS))
+        )
 
     keep = jnp.where(tm < STEPS - 1, 1.0, 0.0).astype(f32)
     source_stage(
-        keep, middle, velocity_ref, iterate_ref, right_ref, kappa_ref, ty_ref, tz_ref, spec_ref, mixed_ref,
-        ((high_a, low_a), (high_b, low_b)),
+        keep, ready, middle, velocity_ref, iterate_ref, right_ref, kappa_ref, ty_ref, tz_ref,
+        spec_ref, mixed_ref, ((high_a, low_a), (high_b, low_b)),
     )
     remote.wait_got(below_ref, below_sem)
     remote.wait_got(above_ref, above_sem)
@@ -652,40 +713,43 @@
         u_ref, sent_ref,
     )
 
-    @pl.loop(1, OWNERS)
-    def _(k):
-        pair, to_space = other(k)
+    here = rows_of(owner)
+
+    def send(pair, place):
         remote.start(
-            sent_ref.at[rows_of(pair * SLABS + to_space), :],
-            got_ref.at[rows_of((tm // 2) * SLABS + space), :],
-            gather_sem, arrive_sem.at[tm // 2], (2 * pair + core, to_space),
-        )
-
-    got_ref[rows_of(owner), :] = sent_ref[rows_of(owner), :]
+            sent_ref.at[rows_of(pair * SLABS + place), :], got_ref.at[here, :],
+            gather_sem, arrive_sem.at[lax.div(tm, 2)], (2 * pair + core, place),
+        )
+
+    other_places(tm, space, send)
+    keep_u = remote.local(u_ref, u_hbm, u_sem)
+    keep_u.start()
+    got_ref[here, :] = sent_ref[here, :]
     solve_modes(
         remote, 2, owner, tm, space, rows_of,
         velocity_ref, own_ref, wave_ref, tg_ref, td_ref, tw_ref, tb_ref, returned_ref,
-        got_ref, back_ref, damp_ref, ratio_ref, last_ref, drive_ref, kept_ref, turn_ref,
-        arrive_sem, swap_out_sem, swap_in_sem, scatter_sem, return_sem, own_sem,
-    )
+        got_ref, back_ref, damp_ref, ratio_ref, last_ref, mate_ref, drive_ref, kept_ref, turn_ref,
+        arrive_sem, swap_out_sem, swap_in_sem, mate_out_sem, mate_in_sem, scatter_sem, return_sem, own_sem,
+    )
+    keep_u.wait()
     remote.wait_sent(kappa_ref.at[pl.ds(0, 2)], edge_out_sem)
     remote.wait_sent(sent_ref.at[rows_of(0, OWNERS - 1), :], gather_sem)
     remote.wait_sent(back_ref.at[rows_of(0, OWNERS - 1), :], scatter_sem)
-    remote.local(back_ref.at[rows_of(owner), :], returned_ref.at[rows_of(owner), :], own_sem).wait()
+    remote.local(back_ref.at[here, :], returned_ref.at[here, :], own_sem).wait()
     remote.wait_got(returned_ref.at[rows_of(0, OWNERS - 1), :], return_sem)
 
 
-GROUP = 4
+GROUP = 2
 
 
 def solve_modes(
     remote, share, owner, tm, space, rows_of,
     velocity_ref, own_ref, wave_ref, tg_ref, td_ref, tw_ref, tb_ref, returned_ref,
-    got_ref, back_ref, damp_ref, ratio_ref, last_ref, drive_ref, kept_ref, turn_ref,
-    arrive_sem, swap_out_sem, swap_in_sem, scatter_sem, return_sem, own_sem,
+    got_ref, back_ref, damp_ref, ratio_ref, last_ref, mate_ref, drive_ref, kept_ref, turn_ref,
+    arrive_sem, swap_out_sem, swap_in_sem, mate_out_sem, mate_in_sem, scatter_sem, return_sem, own_sem,
 ):
     rounds = STEPS // share // GROUP
-    core = tm % share
+    core = lax.rem(tm, share)
     v0, v1, v2 = velocity_ref[0], velocity_ref[1], velocity_ref[2]
     own = own_ref[owner]
     line = [own[k : k + 1, :] for k in range(8)]
@@ -729,41 +793,51 @@
             total = term if total is None else plus(total, term)
         for k, value in enumerate(crossed(total)):
             ratio_ref[k, rows, :] = value
-        power = total
-        for k in range(5):
+        power = times(total, total)
+        for k, value in enumerate(crossed(power if share == 2 else total)):
+            ratio_ref[4 + k, rows, :] = value
+        for k in range(4):
             power = times(power, power)
         closing = inverse_of((1.0 - circulant_alpha * power[0], -circulant_alpha * power[1]))
         for k, value in enumerate(crossed(closing)):
             ratio_ref[2 + k, rows, :] = value
 
-    first_step = tm - tm % 2
+    first_step = tm - lax.rem(tm, 2)
     roots = [crossed(found[m][0]) for m in range(4)]
     flip = repeated(sign, 12)
 
     def step_of(i):
-        return (first_step + share * i + core) % STEPS
+        return lax.rem(first_step + share * i + core, STEPS)
+
+    def wrapped(s, v):
+        return jnp.where(s == 0, circulant_alpha, 1.0).astype(f32) * v
 
     def swap(i):
         remote.start(
             drive_ref.at[step_of(i)], drive_ref.at[step_of(i)],
             swap_out_sem, swap_in_sem, (tm + 1 - 2 * core, space),
         )
+
+    last_ref[...] = jnp.zeros((128, 128), f32)
 
     @pl.loop(0, rounds)
     def _(round_at):
         values, crossings = [], []
         for k in range(GROUP):
             s = step_of(round_at * GROUP + k)
-            slot = s // share
+            slot = lax.div(s, share)
             top = slot * (SLABS * ROWS)
-
-            @pl.when(s == tm)
-            def _():
-                remote.wait_got(got_ref.at[rows_of(0, SLABS - 1), :], arrive_sem.at[slot])
-
-            @pl.when(s != tm)
-            def _():
+            if k > 0:
                 remote.wait_got(got_ref.at[rows_of(0, SLABS), :], arrive_sem.at[slot])
+            else:
+
+                @pl.when(round_at == 0)
+                def _():
+                    remote.wait_got(got_ref.at[rows_of(0, SLABS - 1), :], arrive_sem.at[slot])
+
+                @pl.when(round_at > 0)
+                def _():
+                    remote.wait_got(got_ref.at[rows_of(0, SLABS), :], arrive_sem.at[slot])
 
             pieces = [got_ref[pl.ds(top + x * ROWS, 8), :] for x in range(SLABS)]
             pieces += [got_ref[pl.ds(top + 8 + f, SLABS, stride=ROWS), :] for f in range(4)]
@@ -796,9 +870,11 @@
                 d = points[128 * j : 128 * j + 128, at : at + 128] - repeated(point, 16)
                 y = times_lanes(d, (damp_ref[m, 0], damp_ref[m, 1]))
                 if m < 2:
-                    kept_ref[s // share, m] = y
+                    kept_ref[lax.div(s, share), m] = y
                 total = total + y
             drive_ref[s] = total
+            summed = wrapped(s - core, last_ref[...])
+            last_ref[...] = total + times_lanes(summed, (ratio_ref[4], ratio_ref[5]))
         if share > 1:
             @pl.when(round_at > 0)
             def _():
@@ -806,22 +882,20 @@
                     swap((round_at - 1) * GROUP + k)
 
     if share > 1:
+        mate = (tm + 1 - 2 * core, space)
         for k in range(GROUP):
             swap((rounds - 1) * GROUP + k)
+        remote.start(last_ref, mate_ref, mate_out_sem, mate_in_sem, mate)
+        remote.wait_got(mate_ref, mate_in_sem)
+        remote.wait_sent(last_ref, mate_out_sem)
+        mine, theirs = last_ref[...], mate_ref[...]
+        last_ref[...] = jnp.where(core == 0, theirs, mine) + times_lanes(
+            jnp.where(core == 0, mine, theirs), (ratio_ref[0], ratio_ref[1])
+        )
         remote.wait_got(drive_ref.at[pl.ds(0, STEPS // 2)], swap_in_sem)
-
-    def wrapped(s, v):
-        return jnp.where(s == 0, circulant_alpha, 1.0).astype(f32) * v
 
     def following(s, v):
         return drive_ref[s] + times_lanes(v, (ratio_ref[0], ratio_ref[1]))
-
-    last_ref[...] = jnp.zeros((128, 128), f32)
-
-    @pl.loop(0, STEPS)
-    def _(i):
-        s = (first_step + i) % STEPS
-        last_ref[...] = following(s, wrapped(s, last_ref[...]))
 
     last_ref[...] = times_lanes(last_ref[...], (ratio_ref[2], ratio_ref[3]))
     kappas = [crossed(found[m][2]) for m in range(2)]
@@ -831,23 +905,30 @@
     def both_parts(v):
         return jnp.concatenate([v, flip_all * pltpu.roll(v, 64, 1)], axis=0)
 
+    x_at, side = lax.div(space, 2), lax.rem(space, 2)
+    places = [lax.rem(x_at + k // 2, SLABS // 2) * 2 + lax.rem(side + k, 2) for k in range(SLABS)]
+    here = rows_of(owner)
+
     def send(i):
         s = step_of(i)
-        for x in range(SLABS):
-            index = (s // share) * SLABS + x
-
-            @pl.when((s != tm) | (space != x))
-            def _():
-                remote.start(
-                    back_ref.at[rows_of(index), :], returned_ref.at[rows_of(owner), :],
-                    scatter_sem, return_sem, (s, x),
-                )
-
-            @pl.when((s == tm) & (space == x))
-            def _():
-                remote.local(
-                    back_ref.at[rows_of(owner), :], returned_ref.at[rows_of(owner), :], own_sem
-                ).start()
+        top = lax.div(s, share) * SLABS
+
+        def put(place):
+            remote.start(
+                back_ref.at[rows_of(top + place), :], returned_ref.at[here, :],
+                scatter_sem, return_sem, (s, place),
+            )
+
+        @pl.when(i == 0)
+        def _():
+            remote.local(back_ref.at[here, :], returned_ref.at[here, :], own_sem).start()
+
+        @pl.when(i > 0)
+        def _():
+            put(places[0])
+
+        for place in places[1:]:
+            put(place)
 
     @pl.loop(0, rounds)
     def _(round_at):
@@ -856,7 +937,7 @@
         for k in range(GROUP):
             mine = None
             for c in range(share):
-                s = (first_step + share * (round_at * GROUP + k) + c) % STEPS
+                s = lax.rem(first_step + share * (round_at * GROUP + k) + c, STEPS)
                 last = wrapped(s, last)
                 mine = last if mine is None else jnp.where(core == c, last, mine)
                 last = following(s, last)
@@ -865,13 +946,13 @@
         packed = left_dot(tw_ref[...], jnp.concatenate([both_parts(v) for v in inputs], axis=1))
         lines = []
         for k in range(GROUP):
-            slot = step_of(round_at * GROUP + k) // share
+            slot = lax.div(step_of(round_at * GROUP + k), share)
             for m in range(2):
                 y = times_lanes(inputs[k], (damp_ref[4 + m, 0], damp_ref[4 + m, 1])) + kept_ref[slot, m]
                 lines.append(both_parts(y))
         ends = left_dot(tb_ref[...], jnp.concatenate(lines, axis=1))
         for k in range(GROUP):
-            top = (step_of(round_at * GROUP + k) // share) * (SLABS * ROWS)
+            top = lax.div(step_of(round_at * GROUP + k), share) * (SLABS * ROWS)
             for x in range(SLABS):
                 back_ref[pl.ds(top + x * ROWS, 8), :] = packed[8 * x : 8 * x + 8, 128 * k : 128 * k + 128]
             for m in range(2):
@@ -948,16 +1029,20 @@
     return pl.pallas_call(
         functools.partial(whole_kernel, remote),
         out_shape=(shape(32, 128, 128), shape(OWNERS * ROWS, 128)),
-        in_specs=[spec(SMEM)] + [spec(VMEM)] * 13,
-        out_specs=(spec(VMEM), spec(ANY)),
-        scratch_shapes=[VMEM((256, 256), bf16)] * 4
+        in_specs=[spec(SMEM)] + [spec(ANY)] * 3 + [spec(VMEM)] * 10,
+        out_specs=(spec(ANY), spec(ANY)),
+        scratch_shapes=[
+            VMEM((4, WIDE, NZ, NY), f32), VMEM((4, WIDE, NZ, NY), f32), VMEM((WIDE, NZ, NY), f32),
+            VMEM((32, 128, 128), f32),
+        ]
+        + [VMEM((256, 256), bf16)] * 4
         + [
             VMEM((44, 128, 128), f32), VMEM((8, NZ, NY), f32), VMEM((NZ, NY), f32), VMEM((NZ, NY), f32),
             VMEM((OWNERS * ROWS, 128), f32),
             VMEM((OWNERS * ROWS, 128), f32), VMEM((OWNERS * ROWS, 128), f32),
-            VMEM((6, 2, 128, 128), f32), VMEM((4, 128, 128), f32), VMEM((128, 128), f32),
+            VMEM((6, 2, 128, 128), f32), VMEM((6, 128, 128), f32), VMEM((128, 128), f32), VMEM((128, 128), f32),
             VMEM((STEPS, 128, 128), f32), VMEM((STEPS // 2, 2, 128, 128), f32), VMEM((128, 256), bf16),
-            dma, dma, dma, dma, dma((STEPS // 2,)), dma, dma, dma, dma, dma,
+            dma((3, 8)), dma, dma, dma, dma, dma, dma((STEPS // 2,)), dma, dma, dma, dma, dma, dma, dma,
         ],
         compiler_params=pltpu.CompilerParams(
             vmem_limit_bytes=60 * 1024 * 1024, has_side_effects=True, collective_id=0
@@ -975,9 +1060,12 @@
     return pl.pallas_call(
         backward_kernel,
         out_shape=shape(4, WIDE, NZ, NY),
-        in_specs=[spec(SMEM)] + [spec(VMEM)] * 7,
-        out_specs=spec(VMEM),
-        scratch_shapes=[VMEM((32, 128, 128), f32)],
+        in_specs=[spec(SMEM), spec(ANY)] + [spec(VMEM)] * 6,
+        out_specs=spec(ANY),
+        scratch_shapes=[
+            VMEM((32, 128, 128), f32), VMEM((4, WIDE, NZ, NY), f32), VMEM((4, WIDE, NZ, NY), f32),
+            pltpu.SemaphoreType.DMA, pltpu.SemaphoreType.DMA((8,)),
+        ],
         compiler_params=PARAMS,
         interpret=interpret,
         name="backward",

time: 88.3 us -> 76.9 us (0.87)
  Pallas kernels: 86.9 us -> 75.7 us
    pallas_call x1, Pallas kernels: 77.3 us -> 68.5 us  [whole(): pl.pallas_call(functools.partial(whole_kernel, remote), out_shape=(shape(...]
    pallas_call x1, Pallas kernels: 9.57 us -> 7.26 us  [backward(): pl.pallas_call(backward_kernel, out_shape=shape(4, WIDE, NZ, NY), in_spec...]
where the time goes in v5:
time: 76.9 us; the launch traced here: 75.7 us
  Pallas kernels  75.7 us (98%)
    pallas_call x1, Pallas kernels, whole(): pl.pallas_call(functools.partial(whole_kernel, remote), out_shape=(shape(...  68.5 us
    pallas_call x1, Pallas kernels, backward(): pl.pallas_call(backward_kernel, out_shape=shape(4, WIDE, NZ, NY), in_spec...  7.26 us

profile of v5, /device:TPU:1, one launch (start us, length us, event | category | flops | bytes accessed | tf_op | source)
XLA Modules:
  0.0 75.7 jit_solution(9952773870031518235)
XLA Ops:
  0.0 68.5 %whole.1 = (f32[32,128,128]{2,1,0:T(8,128)}, f32[1536,128]{1,0:T(8,128)}) custom-call(f32[3]{0:T(128)} %velocity_ref.3, f32[4,16,64,128]{3,2,1,0:T(8,128)} %bitcast.3, f32[4,16,64,128]{3,2,1,0:T(8,128)} %bitcast.5, f32[16,64,128]{2,1,0:T(8,128)} %kappa_hbm.1, bf16[2,256,256]{2,1,0:T(8,128)(2,1)} %constant.24.clone.ty_ref, ...), custom_call_target="tpu_custom_call" | custom-call | tf_op jit(solution)/shard_map/whole/pallas_call | solution.py:1029
  68.5 7.3 %backward.1 = f32[4,16,64,128]{3,2,1,0:T(8,128)} custom-call(f32[3]{0:T(128)} %velocity_ref.3, f32[4,16,64,128]{3,2,1,0:T(8,128)} %bitcast.4, f32[32,128,128]{2,1,0:T(8,128)} %get-tuple-element.7.u_ref, f32[1536,128]{1,0:T(8,128)} %get-tuple-element.8.got_ref, bf16[2,256,256]{2,1,0:T(8,128)(2,1)} %constant.34.clone.uy_ref, ...), custom_call_target="tpu_custom_call" | custom-call | tf_op jit(solution)/shard_map/backward/pallas_call | solution.py:1060

commit v6 on v5

--- a/solution.py
+++ b/solution.py
@@ -13,6 +13,7 @@
 SLABS, WIDE = 8, 16
 OWNERS = 128
 ROWS = 12
+LINES = 16
 MESH = pl.DeviceIdType.MESH
 f32, bf16 = jnp.float32, jnp.bfloat16
 
@@ -456,10 +457,39 @@
     transformed(9, second)
 
 
-def slab_stage(
-    velocity_ref, spec_ref, mixed_ref, below_ref, above_ref, ty_ref, tz_ref, lane_ref, row_ref,
-    u_ref, send_ref,
-):
+def put_chunk(ref, t, x, low, high):
+    for k, value in enumerate((low[0], high[0], low[1], high[1])):
+        ref[pl.ds(pl.multiple_of(256 * t + 32 * x + 8 * k, 8), 8), :] = value
+
+
+def get_chunk(ref, t, x):
+    parts = [ref[pl.ds(pl.multiple_of(256 * t + 32 * x + 8 * k, 8), 8), :] for k in range(4)]
+    return (parts[0], parts[2]), (parts[1], parts[3])
+
+
+def packed_planes(sums, x, lane, first_row):
+    own, other = [], []
+    for half in range(2):
+        first, second = sums[x][half], sums[x + 8][half]
+        own.append((first[0] - second[1], first[1] + second[0]))
+        other.append((first[0] + second[1], first[1] - second[0]))
+    partners = plane_partner(other[0], other[1], lane, first_row)
+    return [plus(own[half], partners[half]) for half in range(2)]
+
+
+def unpacked_planes(fetch, lane, first_row):
+    last = [[None, None] for x in range(WIDE)]
+    for x in range(8):
+        packed = fetch(x)
+        partners = plane_partner(packed[0], packed[1], lane, first_row)
+        for half in range(2):
+            both, apart = plus(packed[half], partners[half]), minus(packed[half], partners[half])
+            last[x][half] = (0.5 * both[0], 0.5 * both[1])
+            last[x + 8][half] = (0.5 * apart[1], -0.5 * apart[0])
+    return last
+
+
+def edge_stage(velocity_ref, spec_ref, mixed_ref, below_ref, above_ref, ty_ref, tz_ref):
     v0 = velocity_ref[0]
     outer = [diffusion_number * below_ref[...] - 0.5 * v0, diffusion_number * above_ref[...] + 0.5 * v0]
     edges = [
@@ -472,21 +502,27 @@
     for k in range(4):
         spec_ref[40 + k] = out[:, 128 * k : 128 * k + 128]
 
+
+def slab_stage(odd, begin, velocity_ref, spec_ref, lane_ref, row_ref, y_ref, send_ref, chunk_ref):
     lane = lax.broadcasted_iota(jnp.int32, (8, 128), 1)
     sub = lax.broadcasted_iota(jnp.int32, (8, 128), 0)
     block = lane // 32
 
     @pl.loop(0, 4)
     def _(t):
+        begin(t)
         first_row = (sub + t) == 0
         found = chunk_factors(t, lane_ref, row_ref, velocity_ref, MU)
         bases = [pl.multiple_of(base + 8 * t, 8) for base in (0, 32)]
+        if odd:
+            last = unpacked_planes(lambda x: get_chunk(chunk_ref, t, x), lane, first_row)
 
         def plane(at, base):
             return spec_ref[at, pl.ds(base, 8), :], spec_ref[at, pl.ds(base + 64, 8), :]
 
-        def field(m, x, base):
-            return plane(4 * (x // 2) + 2 * m + x % 2, base)
+        def field(m, x, half):
+            value = plane(4 * (x // 2) + 2 * m + x % 2, bases[half])
+            return plus(value, scaled(EPS[m], last[x][half])) if odd else value
 
         def send(value, low, high):
             for h, packed in enumerate(packed_for(low, high, block)):
@@ -499,50 +535,40 @@
                 base = bases[half]
                 p, q, kappa, inv = found[half][m]
                 under, over = plane(40 + 2 * m, base), plane(41 + 2 * m, base)
-                u = plus(field(m, 0, base), times(p, under))
+                u = plus(field(m, 0, half), times(p, under))
                 us = [u]
                 for x in range(1, WIDE):
-                    u = plus(field(m, x, base), times(p, u))
+                    u = plus(field(m, x, half), times(p, u))
                     us.append(u)
-                for x in range(WIDE):
-                    u_ref[m * 16 + x, pl.ds(base, 8), :] = us[x][0]
-                    u_ref[m * 16 + x, pl.ds(base + 64, 8), :] = us[x][1]
                 outflow = plus(times(p, us[-1]), over)
                 y = us[-1]
                 for x in range(WIDE - 1, -1, -1):
                     if x < WIDE - 1:
                         y = plus(us[x], times(q, y))
                     z = times(inv, y)
+                    y_ref[m * 16 + x, pl.ds(base, 8), :] = z[0]
+                    y_ref[m * 16 + x, pl.ds(base + 64, 8), :] = z[1]
                     sums[x][half] = z if m == 0 else plus(sums[x][half], z)
                 carries.append((outflow, plus(times(q, y), under)))
             for k in range(2):
                 send(8 + m * 2 + k, carries[0][k], carries[1][k])
         for x in range(8):
-            own, other = [], []
-            for half in range(2):
-                first, second = sums[x][half], sums[x + 8][half]
-                own.append((first[0] - second[1], first[1] + second[0]))
-                other.append((first[0] + second[1], first[1] - second[0]))
-            partners = plane_partner(other[0], other[1], lane, first_row)
-            packed = [
-                plus(plus(own[half], partners[half]), plane(32 + x, bases[half])) for half in range(2)
-            ]
-            send(x, packed[0], packed[1])
-
-
-def backward_kernel(
-    velocity_ref, iterate_hbm, u_ref, got_ref, uy_ref, uz_ref, lane_ref, row_ref,
-    out_hbm,
-    spec_ref, iterate_ref, out_ref, load_sem, store_sem,
-):
-    load = pltpu.make_async_copy(iterate_hbm, iterate_ref, load_sem)
-    load.start()
+            packed = packed_planes(sums, x, lane, first_row)
+            packed = [plus(packed[half], plane(32 + x, bases[half])) for half in range(2)]
+            if odd:
+                send(x, packed[0], packed[1])
+            else:
+                put_chunk(chunk_ref, t, x, packed[0], packed[1])
+
+
+def finish_stage(odd, begin, velocity_ref, lane_ref, row_ref, y_ref, got_ref, chunk_ref):
     lane = lax.broadcasted_iota(jnp.int32, (8, 128), 1)
     sub = lax.broadcasted_iota(jnp.int32, (8, 128), 0)
     block = lane // 32
 
     @pl.loop(0, 4)
     def _(t):
+        begin(t)
         first_row = (sub + t) == 0
         found = chunk_factors(t, lane_ref, row_ref, velocity_ref, MU)
         bases = [pl.multiple_of(base + 8 * t, 8) for base in (0, 32)]
@@ -553,38 +579,40 @@
             ]
             return unpacked_from(values, block)
 
-        last = [[None, None] for x in range(WIDE)]
-        for x in range(8):
-            packed = take(x)
-            partners = plane_partner(packed[0], packed[1], lane, first_row)
-            for half in range(2):
-                both, apart = plus(packed[half], partners[half]), minus(packed[half], partners[half])
-                last[x][half] = (0.5 * both[0], 0.5 * both[1])
-                last[x + 8][half] = (0.5 * apart[1], -0.5 * apart[0])
+        last = unpacked_planes(
+            (lambda x: get_chunk(chunk_ref, t, x)) if odd else take, lane, first_row
+        )
+        sums = [[None, None] for x in range(WIDE)]
         for m in range(2):
             start, end = take(8 + m * 2), take(9 + m * 2)
             for half in range(2):
                 base = bases[half]
                 p, q, kappa, inv = found[half][m]
-
-                def old(x):
-                    return (
-                        u_ref[m * 16 + x, pl.ds(base, 8), :],
-                        u_ref[m * 16 + x, pl.ds(base + 64, 8), :],
-                    )
-
                 u = start[half]
-                totals = [plus(u, old(0))]
+                us = [u]
                 for x in range(1, WIDE - 1):
                     u = plus(scaled(EPS[m], last[x][half]), times(p, u))
-                    totals.append(plus(u, old(x)))
-                y = plus(times(inv, old(WIDE - 1)), end[half])
+                    us.append(u)
+                y = end[half]
                 for x in range(WIDE - 1, -1, -1):
                     if x < WIDE - 1:
-                        y = plus(times(inv, totals[x]), times(q, y))
-                    spec_ref[m * 16 + x, pl.ds(base, 8), :] = y[0]
-                    spec_ref[m * 16 + x, pl.ds(base + 64, 8), :] = y[1]
-
+                        y = plus(times(inv, us[x]), times(q, y))
+                    for k in range(2):
+                        rows = pl.ds(base + 64 * k, 8)
+                        y_ref[m * 16 + x, rows, :] = y_ref[m * 16 + x, rows, :] + y[k]
+                    if not odd:
+                        sums[x][half] = y if m == 0 else plus(sums[x][half], y)
+        if not odd:
+            for x in range(8):
+                packed = packed_planes(sums, x, lane, first_row)
+                put_chunk(chunk_ref, t, x, packed[0], packed[1])
+
+
+def backward_kernel(
+    iterate_hbm, spec_ref, uy_ref, uz_ref, out_hbm, iterate_ref, out_ref, load_sem, store_sem
+):
+    load = pltpu.make_async_copy(iterate_hbm, iterate_ref, load_sem)
+    load.start()
     load.wait()
 
     def finished(block):
@@ -658,11 +686,12 @@
 def whole_kernel(
     remote, velocity_ref, iterate_hbm, right_hbm, kappa_hbm,
     ty_ref, tz_ref, lane_ref, row_ref, own_ref, wave_ref, tg_ref, td_ref, tw_ref, tb_ref,
-    u_hbm, returned_ref,
-    iterate_ref, right_ref, kappa_ref, u_ref,
+    y_hbm,
+    iterate_ref, right_ref, kappa_ref, y_ref,
     high_a, low_a, high_b, low_b, spec_ref, mixed_ref, below_ref, above_ref, sent_ref,
+    chunk_out, chunk_in, chunk_back_out, chunk_back_in, returned_ref,
     got_ref, back_ref, damp_ref, ratio_ref, last_ref, mate_ref, drive_ref, kept_ref, turn_ref,
-    load_sem, u_sem, edge_out_sem, below_sem, above_sem,
+    load_sem, y_sem, chunk_out_sem, chunk_in_sem, edge_out_sem, below_sem, above_sem,
     gather_sem, arrive_sem, swap_out_sem, swap_in_sem, mate_out_sem, mate_in_sem,
     scatter_sem, return_sem, own_sem,
 ):
@@ -689,11 +718,17 @@
         for copy in loads(piece):
             copy.wait()
 
-    remote.greet((tm + 1 - 2 * core, space))
-    other_places(tm, space, lambda pair, place: remote.greet((2 * pair + core, place)))
+    mate = (tm + 1 - 2 * core, space)
+
+    def greet(pair, place):
+        remote.greet((2 * pair, place))
+        remote.greet((2 * pair + 1, place))
+
+    remote.greet(mate)
+    other_places(tm, space, greet)
 
     def middle():
-        remote.all_here(OWNERS)
+        remote.all_here(2 * OWNERS - 1)
         remote.start(
             kappa_ref.at[WIDE - 1], below_ref, edge_out_sem, below_sem, (tm, lax.rem(space + 1, SLABS))
         )
@@ -708,35 +743,130 @@
     )
     remote.wait_got(below_ref, below_sem)
     remote.wait_got(above_ref, above_sem)
-    slab_stage(
-        velocity_ref, spec_ref, mixed_ref, below_ref, above_ref, ty_ref, tz_ref, lane_ref, row_ref,
-        u_ref, sent_ref,
+    edge_stage(velocity_ref, spec_ref, mixed_ref, below_ref, above_ref, ty_ref, tz_ref)
+    is_odd = core == 1
+
+    def chunk_at(ref, t):
+        return ref.at[pl.ds(pl.multiple_of(256 * t, 256), 256), :]
+
+    def hand_over(source, target, t, base):
+        remote.start(
+            chunk_at(source, t), chunk_at(target, t), chunk_out_sem.at[base // 4],
+            chunk_in_sem.at[base + t], mate,
+        )
+
+    def stage(work, source, target, base):
+        @pl.when(jnp.logical_not(is_odd))
+        def _():
+            def begin(t):
+                @pl.when(t > 0)
+                def _():
+                    hand_over(source, target, t - 1, base)
+
+            work(False, begin, source)
+            hand_over(source, target, 3, base)
+
+        @pl.when(is_odd)
+        def _():
+            work(True, lambda t: remote.wait_got(chunk_at(target, t), chunk_in_sem.at[base + t]), target)
+
+    stage(
+        lambda odd, begin, ref: slab_stage(
+            odd, begin, velocity_ref, spec_ref, lane_ref, row_ref, y_ref, sent_ref, ref
+        ),
+        chunk_out, chunk_in, 0,
     )
 
-    here = rows_of(owner)
-
-    def send(pair, place):
+    pair = lax.div(tm, 2)
+    side = lax.rem(pair, 2)
+    at_home = side == core
+    slot = lax.div(pair, 2) * SLABS + space
+
+    def even_rows(index):
+        return pl.ds(pl.multiple_of(index * ROWS + 8, 4), 4)
+
+    def send_even(other, place):
         remote.start(
-            sent_ref.at[rows_of(pair * SLABS + place), :], got_ref.at[here, :],
-            gather_sem, arrive_sem.at[lax.div(tm, 2)], (2 * pair + core, place),
-        )
-
-    other_places(tm, space, send)
-    keep_u = remote.local(u_ref, u_hbm, u_sem)
-    keep_u.start()
-    got_ref[here, :] = sent_ref[here, :]
+            sent_ref.at[even_rows(other * SLABS + place), :],
+            got_ref.at[pl.ds(pl.multiple_of(slot * LINES + ROWS, 4), 4), :],
+            gather_sem, arrive_sem.at[lax.div(pair, 2)], (2 * other + side, place),
+        )
+
+    def send_odd(other, place):
+        remote.start(
+            sent_ref.at[rows_of(other * SLABS + place), :],
+            got_ref.at[pl.ds(pl.multiple_of(slot * LINES, 4), ROWS), :],
+            gather_sem, arrive_sem.at[lax.div(pair, 2)], (2 * other + side, place),
+        )
+
+    @pl.when(is_odd)
+    def _():
+        other_places(tm, space, send_odd)
+
+        @pl.when(at_home)
+        def _():
+            got_ref[pl.ds(pl.multiple_of(slot * LINES, 4), ROWS), :] = sent_ref[rows_of(owner), :]
+
+        @pl.when(jnp.logical_not(at_home))
+        def _():
+            send_odd(pair, space)
+
+    @pl.when(jnp.logical_not(is_odd))
+    def _():
+        other_places(tm, space, send_even)
+
+        @pl.when(at_home)
+        def _():
+            got_ref[pl.ds(pl.multiple_of(slot * LINES + ROWS, 4), 4), :] = sent_ref[even_rows(owner), :]
+
+        @pl.when(jnp.logical_not(at_home))
+        def _():
+            send_even(pair, space)
+
     solve_modes(
         remote, 2, owner, tm, space, rows_of,
         velocity_ref, own_ref, wave_ref, tg_ref, td_ref, tw_ref, tb_ref, returned_ref,
         got_ref, back_ref, damp_ref, ratio_ref, last_ref, mate_ref, drive_ref, kept_ref, turn_ref,
         arrive_sem, swap_out_sem, swap_in_sem, mate_out_sem, mate_in_sem, scatter_sem, return_sem, own_sem,
     )
-    keep_u.wait()
+
+    def settle(rows):
+        @pl.when(at_home)
+        def _():
+            remote.wait_got(returned_ref.at[pl.ds(0, (OWNERS - 1) * rows), :], return_sem)
+            remote.wait_sent(sent_ref.at[pl.ds(0, (OWNERS - 1) * (LINES - rows)), :], gather_sem)
+            remote.wait_sent(back_ref.at[pl.ds(0, (OWNERS // 2) * LINES - rows), :], scatter_sem)
+
+        @pl.when(jnp.logical_not(at_home))
+        def _():
+            remote.wait_got(returned_ref.at[pl.ds(0, OWNERS * rows), :], return_sem)
+            remote.wait_sent(sent_ref.at[pl.ds(0, OWNERS * (LINES - rows)), :], gather_sem)
+            remote.wait_sent(back_ref.at[pl.ds(0, (OWNERS // 2) * LINES), :], scatter_sem)
+
+    @pl.when(jnp.logical_not(is_odd))
+    def _():
+        settle(ROWS)
+
+    @pl.when(is_odd)
+    def _():
+        settle(4)
+
+    stage(
+        lambda odd, begin, ref: finish_stage(
+            odd, begin, velocity_ref, lane_ref, row_ref, y_ref, returned_ref, ref
+        ),
+        chunk_back_out, chunk_back_in, 4,
+    )
+    keep_y = remote.local(y_ref, y_hbm, y_sem)
+    keep_y.start()
+
+    @pl.when(jnp.logical_not(is_odd))
+    def _():
+        remote.wait_sent(chunk_out, chunk_out_sem.at[0])
+        remote.wait_sent(chunk_back_out, chunk_out_sem.at[1])
+
     remote.wait_sent(kappa_ref.at[pl.ds(0, 2)], edge_out_sem)
-    remote.wait_sent(sent_ref.at[rows_of(0, OWNERS - 1), :], gather_sem)
-    remote.wait_sent(back_ref.at[rows_of(0, OWNERS - 1), :], scatter_sem)
-    remote.local(back_ref.at[here, :], returned_ref.at[here, :], own_sem).wait()
-    remote.wait_got(returned_ref.at[rows_of(0, OWNERS - 1), :], return_sem)
+    keep_y.wait()
 
 
 GROUP = 2
@@ -748,8 +878,11 @@
     got_ref, back_ref, damp_ref, ratio_ref, last_ref, mate_ref, drive_ref, kept_ref, turn_ref,
     arrive_sem, swap_out_sem, swap_in_sem, mate_out_sem, mate_in_sem, scatter_sem, return_sem, own_sem,
 ):
-    rounds = STEPS // share // GROUP
+    pairs = STEPS // 2
+    rounds = pairs // share // GROUP
     core = lax.rem(tm, share)
+    pair = lax.div(tm, 2)
+    at_home = lax.rem(pair, share) == core
     v0, v1, v2 = velocity_ref[0], velocity_ref[1], velocity_ref[2]
     own = own_ref[owner]
     line = [own[k : k + 1, :] for k in range(8)]
@@ -794,27 +927,36 @@
         for k, value in enumerate(crossed(total)):
             ratio_ref[k, rows, :] = value
         power = times(total, total)
-        for k, value in enumerate(crossed(power if share == 2 else total)):
+        for k, value in enumerate(crossed(power)):
             ratio_ref[4 + k, rows, :] = value
-        for k in range(4):
+        fourth = times(power, power)
+        for k, value in enumerate(crossed(fourth if share == 2 else power)):
+            ratio_ref[6 + k, rows, :] = value
+        power = fourth
+        for k in range(3):
             power = times(power, power)
         closing = inverse_of((1.0 - circulant_alpha * power[0], -circulant_alpha * power[1]))
         for k, value in enumerate(crossed(closing)):
             ratio_ref[2 + k, rows, :] = value
 
-    first_step = tm - lax.rem(tm, 2)
+    first_pair = pair - lax.rem(pair, 2)
     roots = [crossed(found[m][0]) for m in range(4)]
-    flip = repeated(sign, 12)
-
-    def step_of(i):
-        return lax.rem(first_step + share * i + core, STEPS)
-
-    def wrapped(s, v):
-        return jnp.where(s == 0, circulant_alpha, 1.0).astype(f32) * v
+    flip = repeated(sign, 16)
+    ratio = (ratio_ref.at[0], ratio_ref.at[1])
+    square = (ratio_ref.at[4], ratio_ref.at[5])
+
+    def times_refs(v, table):
+        return times_lanes(v, (table[0][...], table[1][...]))
+
+    def pair_of(i):
+        return lax.rem(first_pair + share * i + core, pairs)
+
+    def wrapped(at, v):
+        return jnp.where(at == 0, circulant_alpha, 1.0).astype(f32) * v
 
     def swap(i):
         remote.start(
-            drive_ref.at[step_of(i)], drive_ref.at[step_of(i)],
+            drive_ref.at[pair_of(i)], drive_ref.at[pair_of(i)],
             swap_out_sem, swap_in_sem, (tm + 1 - 2 * core, space),
         )
 
@@ -824,57 +966,82 @@
     def _(round_at):
         values, crossings = [], []
         for k in range(GROUP):
-            s = step_of(round_at * GROUP + k)
-            slot = lax.div(s, share)
-            top = slot * (SLABS * ROWS)
+            at = pair_of(round_at * GROUP + k)
+            slot = lax.div(at, share)
+            top = slot * (SLABS * LINES)
+
+            def arrived(rows):
+                remote.wait_got(got_ref.at[pl.ds(0, rows), :], arrive_sem.at[slot])
+
             if k > 0:
-                remote.wait_got(got_ref.at[rows_of(0, SLABS), :], arrive_sem.at[slot])
+                arrived(SLABS * LINES)
             else:
-
-                @pl.when(round_at == 0)
+                home = (round_at == 0) & at_home
+
+                @pl.when(home & (core == 0))
                 def _():
-                    remote.wait_got(got_ref.at[rows_of(0, SLABS - 1), :], arrive_sem.at[slot])
-
-                @pl.when(round_at > 0)
+                    arrived(SLABS * LINES - 4)
+
+                @pl.when(home & (core == 1))
                 def _():
-                    remote.wait_got(got_ref.at[rows_of(0, SLABS), :], arrive_sem.at[slot])
-
-            pieces = [got_ref[pl.ds(top + x * ROWS, 8), :] for x in range(SLABS)]
-            pieces += [got_ref[pl.ds(top + 8 + f, SLABS, stride=ROWS), :] for f in range(4)]
+                    arrived(SLABS * LINES - ROWS)
+
+                @pl.when(jnp.logical_not(home))
+                def _():
+                    arrived(SLABS * LINES)
+
+            pieces = [got_ref[pl.ds(top + x * LINES, 8), :] for x in range(SLABS)]
+            pieces += [got_ref[pl.ds(top + 8 + f, SLABS, stride=LINES), :] for f in range(8)]
             v = jnp.concatenate(pieces, axis=0)
             values.append(halves(v))
             crossings.append(halves(flip * pltpu.roll(v, 64, 1)))
-        stacked = jnp.concatenate([half for pair in values for half in pair], axis=0)
+        stacked = jnp.concatenate([half for pieces in values for half in pieces], axis=0)
         turned = jnp.dot(stacked, turn_ref[...], preferred_element_type=f32).astype(bf16)
         columns, own_points, other_points = [], [], []
         for k in range(GROUP):
             parts = []
             for half in range(2):
-                rows = slice(96 * (2 * k + half), 96 * (2 * k + half) + 96)
+                rows = slice(128 * (2 * k + half), 128 * (2 * k + half) + 128)
                 parts.append((values[k][half], crossings[k][half], turned[rows, :128], turned[rows, 128:]))
             order = (parts[0], parts[1], parts[0])
             columns.append(jnp.concatenate([piece[:64] for part in order for piece in part], axis=0))
-            own_points.append(jnp.concatenate([piece[64:] for part in order for piece in part[:2]], axis=0))
-            other_points.append(jnp.concatenate([piece[64:] for part in order for piece in part[2:]], axis=0))
+            for step in range(2):
+                lines = slice(64 + 32 * step, 96 + 32 * step)
+                own_points.append(
+                    jnp.concatenate([piece[lines] for part in order for piece in part[:2]], axis=0)
+                )
+                other_points.append(
+                    jnp.concatenate([piece[lines] for part in order for piece in part[2:]], axis=0)
+                )
         drive = jnp.dot(tg_ref[...], jnp.concatenate(columns, axis=1), preferred_element_type=f32)
         points = jnp.dot(
             td_ref[...], jnp.concatenate(own_points + other_points, axis=1), preferred_element_type=f32
         )
         for k in range(GROUP):
-            s = step_of(round_at * GROUP + k)
+            at = pair_of(round_at * GROUP + k)
+            slot = lax.div(at, share)
             total = drive[:, 128 * k : 128 * k + 128]
-            for m in range(4):
-                at = 128 * (k + GROUP * (m // 2))
-                j = m % 2
-                point = times_lanes(points[256 + 8 * j : 264 + 8 * j, at : at + 128], roots[m])
-                d = points[128 * j : 128 * j + 128, at : at + 128] - repeated(point, 16)
-                y = times_lanes(d, (damp_ref[m, 0], damp_ref[m, 1]))
-                if m < 2:
-                    kept_ref[lax.div(s, share), m] = y
-                total = total + y
-            drive_ref[s] = total
-            summed = wrapped(s - core, last_ref[...])
-            last_ref[...] = total + times_lanes(summed, (ratio_ref[4], ratio_ref[5]))
+            for step, store in ((1, 0), (0, 1)):
+                summed = None
+                for m in range(4):
+                    where = 128 * (2 * k + step + 2 * GROUP * (m // 2))
+                    j = m % 2
+                    point = times_lanes(points[256 + 8 * j : 264 + 8 * j, where : where + 128], roots[m])
+                    d = points[128 * j : 128 * j + 128, where : where + 128] - repeated(point, 16)
+                    y = times_lanes(d, (damp_ref[m, 0], damp_ref[m, 1]))
+                    summed = y if summed is None else summed + y
+                    if m < 2:
+                        if store == 1:
+                            y = y + times_lanes(early, (damp_ref[4 + m, 0], damp_ref[4 + m, 1]))
+                        kept_ref[slot, 2 * store + m] = y
+                if store == 0:
+                    early = summed
+                    total = total + times_refs(summed, ratio)
+                else:
+                    total = total + summed
+            drive_ref[at] = total
+            before = wrapped(at - core, last_ref[...])
+            last_ref[...] = total + times_lanes(before, (ratio_ref[6], ratio_ref[7]))
         if share > 1:
             @pl.when(round_at > 0)
             def _():
@@ -889,18 +1056,18 @@
         remote.wait_got(mate_ref, mate_in_sem)
         remote.wait_sent(last_ref, mate_out_sem)
         mine, theirs = last_ref[...], mate_ref[...]
-        last_ref[...] = jnp.where(core == 0, theirs, mine) + times_lanes(
-            jnp.where(core == 0, mine, theirs), (ratio_ref[0], ratio_ref[1])
-        )
-        remote.wait_got(drive_ref.at[pl.ds(0, STEPS // 2)], swap_in_sem)
-
-    def following(s, v):
-        return drive_ref[s] + times_lanes(v, (ratio_ref[0], ratio_ref[1]))
+        last_ref[...] = jnp.where(core == 0, theirs, mine) + times_refs(
+            jnp.where(core == 0, mine, theirs), square
+        )
+        remote.wait_got(drive_ref.at[pl.ds(0, pairs // 2)], swap_in_sem)
+
+    def following(at, v):
+        return drive_ref[at] + times_refs(v, square)
 
     last_ref[...] = times_lanes(last_ref[...], (ratio_ref[2], ratio_ref[3]))
     kappas = [crossed(found[m][2]) for m in range(2)]
     ups = [crossed(found[m][1]) for m in range(2)]
-    flip_all = repeated(sign, 16)
+    flip_all = flip
 
     def both_parts(v):
         return jnp.concatenate([v, flip_all * pltpu.roll(v, 64, 1)], axis=0)
@@ -910,25 +1077,42 @@
     here = rows_of(owner)
 
     def send(i):
-        s = step_of(i)
-        top = lax.div(s, share) * SLABS
-
-        def put(place):
-            remote.start(
-                back_ref.at[rows_of(top + place), :], returned_ref.at[here, :],
-                scatter_sem, return_sem, (s, place),
-            )
-
-        @pl.when(i == 0)
+        at = pair_of(i)
+        top = lax.div(at, share) * SLABS
+
+        def put(place, even, odd):
+            lines = (top + place) * LINES
+            if even is not None:
+                even(
+                    back_ref.at[pl.ds(pl.multiple_of(lines, 4), ROWS), :], returned_ref.at[here, :],
+                    scatter_sem, return_sem, (2 * at, place),
+                )
+            if odd is not None:
+                odd(
+                    back_ref.at[pl.ds(pl.multiple_of(lines + ROWS, 4), 4), :],
+                    returned_ref.at[pl.ds(pl.multiple_of(owner * ROWS + 8, 4), 4), :],
+                    scatter_sem, return_sem, (2 * at + 1, place),
+                )
+
+        def stay(source, target, *others):
+            target[...] = source[...]
+
+        home = (i == 0) & at_home
+
+        @pl.when(jnp.logical_not(home))
         def _():
-            remote.local(back_ref.at[here, :], returned_ref.at[here, :], own_sem).start()
-
-        @pl.when(i > 0)
+            put(places[0], remote.start, remote.start)
+
+        @pl.when(home & (core == 0))
         def _():
-            put(places[0])
+            put(places[0], stay, remote.start)
+
+        @pl.when(home & (core == 1))
+        def _():
+            put(places[0], remote.start, stay)
 
         for place in places[1:]:
-            put(place)
+            put(place, remote.start, remote.start)
 
     @pl.loop(0, rounds)
     def _(round_at):
@@ -937,30 +1121,33 @@
         for k in range(GROUP):
             mine = None
             for c in range(share):
-                s = lax.rem(first_step + share * (round_at * GROUP + k) + c, STEPS)
-                last = wrapped(s, last)
+                at = lax.rem(first_pair + share * (round_at * GROUP + k) + c, pairs)
+                last = wrapped(at, last)
                 mine = last if mine is None else jnp.where(core == c, last, mine)
-                last = following(s, last)
+                last = following(at, last)
             inputs.append(mine)
         last_ref[...] = last
         packed = left_dot(tw_ref[...], jnp.concatenate([both_parts(v) for v in inputs], axis=1))
         lines = []
         for k in range(GROUP):
-            slot = lax.div(step_of(round_at * GROUP + k), share)
-            for m in range(2):
-                y = times_lanes(inputs[k], (damp_ref[4 + m, 0], damp_ref[4 + m, 1])) + kept_ref[slot, m]
-                lines.append(both_parts(y))
+            slot = lax.div(pair_of(round_at * GROUP + k), share)
+            for step, v in enumerate((inputs[k], times_refs(inputs[k], ratio))):
+                for m in range(2):
+                    y = times_lanes(v, (damp_ref[4 + m, 0], damp_ref[4 + m, 1]))
+                    lines.append(both_parts(y + kept_ref[slot, 2 * step + m]))
         ends = left_dot(tb_ref[...], jnp.concatenate(lines, axis=1))
         for k in range(GROUP):
-            top = lax.div(step_of(round_at * GROUP + k), share) * (SLABS * ROWS)
+            top = lax.div(pair_of(round_at * GROUP + k), share) * (SLABS * LINES)
             for x in range(SLABS):
-                back_ref[pl.ds(top + x * ROWS, 8), :] = packed[8 * x : 8 * x + 8, 128 * k : 128 * k + 128]
-            for m in range(2):
-                at = 128 * (2 * k + m)
-                part = [ends[8 * j : 8 * j + 8, at : at + 128] for j in range(3)]
-                u = times_lanes(part[0] - times_lanes(part[1], ups[m]), kappas[m])
-                back_ref[pl.ds(top + 8 + m * 2, SLABS, stride=ROWS), :] = u
-                back_ref[pl.ds(top + 9 + m * 2, SLABS, stride=ROWS), :] = part[2]
+                back_ref[pl.ds(top + x * LINES, 8), :] = packed[8 * x : 8 * x + 8, 128 * k : 128 * k + 128]
+            for step in range(2):
+                for m in range(2):
+                    where = 128 * (4 * k + 2 * step + m)
+                    part = [ends[8 * j : 8 * j + 8, where : where + 128] for j in range(3)]
+                    u = times_lanes(part[0] - times_lanes(part[1], ups[m]), kappas[m])
+                    line = top + 8 + 4 * step + 2 * m
+                    back_ref[pl.ds(line, SLABS, stride=LINES), :] = u
+                    back_ref[pl.ds(line + 1, SLABS, stride=LINES), :] = part[2]
 
         @pl.when(round_at > 0)
         def _():
@@ -973,7 +1160,7 @@
         send((rounds - 1) * GROUP + k)
 
     if share > 1:
-        remote.wait_sent(drive_ref.at[pl.ds(0, STEPS // 2)], swap_out_sem)
+        remote.wait_sent(drive_ref.at[pl.ds(0, pairs // 2)], swap_out_sem)
 
 
 class Remote:
@@ -1028,9 +1215,9 @@
     dma = pltpu.SemaphoreType.DMA
     return pl.pallas_call(
         functools.partial(whole_kernel, remote),
-        out_shape=(shape(32, 128, 128), shape(OWNERS * ROWS, 128)),
+        out_shape=shape(32, 128, 128),
         in_specs=[spec(SMEM)] + [spec(ANY)] * 3 + [spec(VMEM)] * 10,
-        out_specs=(spec(ANY), spec(ANY)),
+        out_specs=spec(ANY),
         scratch_shapes=[
             VMEM((4, WIDE, NZ, NY), f32), VMEM((4, WIDE, NZ, NY), f32), VMEM((WIDE, NZ, NY), f32),
             VMEM((32, 128, 128), f32),
@@ -1039,10 +1226,13 @@
         + [
             VMEM((44, 128, 128), f32), VMEM((8, NZ, NY), f32), VMEM((NZ, NY), f32), VMEM((NZ, NY), f32),
             VMEM((OWNERS * ROWS, 128), f32),
-            VMEM((OWNERS * ROWS, 128), f32), VMEM((OWNERS * ROWS, 128), f32),
-            VMEM((6, 2, 128, 128), f32), VMEM((6, 128, 128), f32), VMEM((128, 128), f32), VMEM((128, 128), f32),
-            VMEM((STEPS, 128, 128), f32), VMEM((STEPS // 2, 2, 128, 128), f32), VMEM((128, 256), bf16),
-            dma((3, 8)), dma, dma, dma, dma, dma, dma((STEPS // 2,)), dma, dma, dma, dma, dma, dma, dma,
+            VMEM((1024, 128), f32), VMEM((1024, 128), f32), VMEM((1024, 128), f32), VMEM((1024, 128), f32),
+            VMEM((OWNERS * ROWS, 128), f32),
+            VMEM((OWNERS // 2 * LINES, 128), f32), VMEM((OWNERS // 2 * LINES, 128), f32),
+            VMEM((6, 2, 128, 128), f32), VMEM((8, 128, 128), f32), VMEM((128, 128), f32), VMEM((128, 128), f32),
+            VMEM((STEPS // 2, 128, 128), f32), VMEM((STEPS // 4, 4, 128, 128), f32), VMEM((128, 256), bf16),
+            dma((3, 8)), dma, dma((2,)), dma((8,)), dma, dma, dma,
+            dma, dma((STEPS // 4,)), dma, dma, dma, dma, dma, dma, dma,
         ],
         compiler_params=pltpu.CompilerParams(
             vmem_limit_bytes=60 * 1024 * 1024, has_side_effects=True, collective_id=0
@@ -1056,26 +1246,26 @@
     )
 
 
-def backward(velocity, iterate, u, got, interpret=False):
+def backward(iterate, y, interpret=False):
     return pl.pallas_call(
         backward_kernel,
         out_shape=shape(4, WIDE, NZ, NY),
-        in_specs=[spec(SMEM), spec(ANY)] + [spec(VMEM)] * 6,
+        in_specs=[spec(ANY)] + [spec(VMEM)] * 3,
         out_specs=spec(ANY),
         scratch_shapes=[
-            VMEM((32, 128, 128), f32), VMEM((4, WIDE, NZ, NY), f32), VMEM((4, WIDE, NZ, NY), f32),
+            VMEM((4, WIDE, NZ, NY), f32), VMEM((4, WIDE, NZ, NY), f32),
             pltpu.SemaphoreType.DMA, pltpu.SemaphoreType.DMA((8,)),
         ],
         compiler_params=PARAMS,
         interpret=interpret,
         name="backward",
-    )(velocity, iterate, u, got, TABLES["uy"], TABLES["uz"], TABLES["lane"], TABLES["row"])
+    )(iterate, y, TABLES["uy"], TABLES["uz"])
 
 
 def shards(iterate, right_side, diffusivity, velocity):
     iterate, right_side = iterate[0], right_side[0]
-    u, returned = whole(velocity, iterate, right_side, diffusivity)
-    return backward(velocity, iterate, u, returned)[None]
+    y = whole(velocity, iterate, right_side, diffusivity)
+    return backward(iterate, y)[None]
 
 
 def solution(mesh):

time: 76.9 us -> 79.5 us (1.034); the launches traced: 75.7 us -> 79.3 us
  Pallas kernels: 75.7 us -> 79.3 us
    pallas_call x1, Pallas kernels: 68.5 us -> 72.4 us  [whole(): pl.pallas_call(functools.partial(whole_kernel, remote), out_shape=shape(3...]
where the time goes in v6:
time: 79.5 us; the launch traced here: 79.3 us
  Pallas kernels  79.3 us (100%)
    pallas_call x1, Pallas kernels, whole(): pl.pallas_call(functools.partial(whole_kernel, remote), out_shape=shape(3...  72.4 us
    pallas_call x1, Pallas kernels, backward(): pl.pallas_call(backward_kernel, out_shape=shape(4, WIDE, NZ, NY), in_spec...  6.87 us

profile of v6, /device:TPU:1, one launch (start us, length us, event | category | flops | bytes accessed | tf_op | source)
XLA Modules:
  0.0 79.3 jit_solution(3406268397649330593)
XLA Ops:
  0.0 72.4 %whole.1.spec_ref = f32[32,128,128]{2,1,0:T(8,128)} custom-call(f32[3]{0:T(128)} %velocity_ref.1, f32[4,16,64,128]{3,2,1,0:T(8,128)} %bitcast.3, f32[4,16,64,128]{3,2,1,0:T(8,128)} %bitcast.5, f32[16,64,128]{2,1,0:T(8,128)} %kappa_hbm.1, bf16[2,256,256]{2,1,0:T(8,128)(2,1)} %constant.24.clone.ty_ref, bf16[128,384]{1,0:T(8,128)(2,1)} %constant.25.clone.tz_ref, ...), custom_call_target="tpu_custom_call" | custom-call | tf_op jit(solution)/shard_map/whole/pallas_call | solution.py:1216
  72.4 6.9 %backward.1 = f32[4,16,64,128]{3,2,1,0:T(8,128)} custom-call(f32[4,16,64,128]{3,2,1,0:T(8,128)} %bitcast.4, f32[32,128,128]{2,1,0:T(8,128)} %whole.1.spec_ref, bf16[2,256,256]{2,1,0:T(8,128)(2,1)} %constant.34.clone.uy_ref, bf16[128,384]{1,0:T(8,128)(2,1)} %constant.35.clone.uz_ref), custom_call_target="tpu_custom_call" | custom-call | tf_op jit(solution)/shard_map/backward/pallas_call | solution.py:1250

commit v7 on v6

--- a/solution.py
+++ b/solution.py
@@ -609,11 +609,22 @@
 
 
 def backward_kernel(
-    iterate_hbm, spec_ref, uy_ref, uz_ref, out_hbm, iterate_ref, out_ref, load_sem, store_sem
+    iterate_hbm, spec_hbm, uy_ref, uz_ref, out_hbm, spec_ref, iterate_ref, out_ref, load_sem, store_sem
 ):
-    load = pltpu.make_async_copy(iterate_hbm, iterate_ref, load_sem)
-    load.start()
-    load.wait()
+    def loads(group):
+        planes = pl.ds(4 * group, 4)
+        upper = pl.ds(16 + 4 * group, 4)
+        return [
+            pltpu.make_async_copy(spec_hbm.at[planes], spec_ref.at[planes], load_sem.at[0, group]),
+            pltpu.make_async_copy(spec_hbm.at[upper], spec_ref.at[upper], load_sem.at[1, group]),
+            pltpu.make_async_copy(
+                iterate_hbm.at[:, planes], iterate_ref.at[:, planes], load_sem.at[2, group]
+            ),
+        ]
+
+    for group in range(4):
+        for copy in loads(group):
+            copy.start()
 
     def finished(block):
         planes = [2 * block, 2 * block + 1, 16 + 2 * block, 17 + 2 * block]
@@ -647,23 +658,24 @@
                     total = total + (2.0 * c.real) * parts[m][0] - (2.0 * c.imag) * parts[m][1]
                 out_ref[n, x] = total
 
-    @pl.loop(0, 4)
-    def _(i):
-        blocks = (2 * i, 2 * i + 1)
+    pending = None
+    for group in range(4):
+        for copy in loads(group):
+            copy.wait()
+        blocks = (2 * group, 2 * group + 1)
         outs = [finished(block) for block in blocks]
-        for block, out in zip(blocks, outs):
-            added(block, out)
-
-        @pl.when(i > 0)
-        def _():
-            store(2 * i - 2).start()
-            store(2 * i - 1).start()
-
-    store(6).start()
-    store(7).start()
-
-    @pl.loop(0, 8)
-    def _(block):
+        if pending is not None:
+            for block, out in pending:
+                added(block, out)
+        pending = list(zip(blocks, outs))
+        if group > 1:
+            store(2 * group - 4).start()
+            store(2 * group - 3).start()
+    for block, out in pending:
+        added(block, out)
+    for block in range(4, 8):
+        store(block).start()
+    for block in range(8):
         store(block).wait()
 
 
@@ -691,7 +703,7 @@
     high_a, low_a, high_b, low_b, spec_ref, mixed_ref, below_ref, above_ref, sent_ref,
     chunk_out, chunk_in, chunk_back_out, chunk_back_in, returned_ref,
     got_ref, back_ref, damp_ref, ratio_ref, last_ref, mate_ref, drive_ref, kept_ref, turn_ref,
-    load_sem, y_sem, chunk_out_sem, chunk_in_sem, edge_out_sem, below_sem, above_sem,
+    vouch_sem, load_sem, y_sem, chunk_out_sem, chunk_in_sem, edge_out_sem, below_sem, above_sem,
     gather_sem, arrive_sem, swap_out_sem, swap_in_sem, mate_out_sem, mate_in_sem,
     scatter_sem, return_sem, own_sem,
 ):
@@ -720,15 +732,17 @@
 
     mate = (tm + 1 - 2 * core, space)
 
-    def greet(pair, place):
-        remote.greet((2 * pair, place))
-        remote.greet((2 * pair + 1, place))
-
-    remote.greet(mate)
-    other_places(tm, space, greet)
+    for k in range(1, SLABS):
+        remote.greet((tm, lax.rem(space + k, SLABS)))
+
+    @pl.loop(1, STEPS)
+    def _(k):
+        remote.greet((lax.rem(tm + k, STEPS), space))
 
     def middle():
-        remote.all_here(2 * OWNERS - 1)
+        remote.all_here(SLABS + STEPS - 2)
+        for k in range(1, SLABS):
+            remote.vouch(vouch_sem, (tm, lax.rem(space + k, SLABS)))
         remote.start(
             kappa_ref.at[WIDE - 1], below_ref, edge_out_sem, below_sem, (tm, lax.rem(space + 1, SLABS))
         )
@@ -755,10 +769,12 @@
             chunk_in_sem.at[base + t], mate,
         )
 
-    def stage(work, source, target, base):
+    def stage(work, source, target, base, done):
         @pl.when(jnp.logical_not(is_odd))
         def _():
             def begin(t):
+                done(t)
+
                 @pl.when(t > 0)
                 def _():
                     hand_over(source, target, t - 1, base)
@@ -768,14 +784,20 @@
 
         @pl.when(is_odd)
         def _():
-            work(True, lambda t: remote.wait_got(chunk_at(target, t), chunk_in_sem.at[base + t]), target)
+            def begin(t):
+                done(t)
+                remote.wait_got(chunk_at(target, t), chunk_in_sem.at[base + t])
+
+            work(True, begin, target)
 
     stage(
         lambda odd, begin, ref: slab_stage(
             odd, begin, velocity_ref, spec_ref, lane_ref, row_ref, y_ref, sent_ref, ref
         ),
-        chunk_out, chunk_in, 0,
+        chunk_out, chunk_in, 0, lambda t: None,
     )
+
+    remote.vouched(vouch_sem, SLABS - 1)
 
     pair = lax.div(tm, 2)
     side = lax.rem(pair, 2)
@@ -851,14 +873,23 @@
     def _():
         settle(4)
 
+    def store_chunk(t):
+        for base in (0, 32, 64, 96):
+            rows = pl.ds(pl.multiple_of(base + 8 * t, 8), 8)
+            remote.local(y_ref.at[:, rows, :], y_hbm.at[:, rows, :], y_sem).start()
+
+    def store_before(t):
+        @pl.when(t > 0)
+        def _():
+            store_chunk(t - 1)
+
     stage(
         lambda odd, begin, ref: finish_stage(
             odd, begin, velocity_ref, lane_ref, row_ref, y_ref, returned_ref, ref
         ),
-        chunk_back_out, chunk_back_in, 4,
+        chunk_back_out, chunk_back_in, 4, store_before,
     )
-    keep_y = remote.local(y_ref, y_hbm, y_sem)
-    keep_y.start()
+    store_chunk(3)
 
     @pl.when(jnp.logical_not(is_odd))
     def _():
@@ -866,7 +897,7 @@
         remote.wait_sent(chunk_back_out, chunk_out_sem.at[1])
 
     remote.wait_sent(kappa_ref.at[pl.ds(0, 2)], edge_out_sem)
-    keep_y.wait()
+    remote.local(y_ref, y_hbm, y_sem).wait()
 
 
 GROUP = 2
@@ -1175,6 +1206,12 @@
     def all_here(self, count):
         pl.semaphore_wait(pltpu.get_barrier_semaphore(), count)
 
+    def vouch(self, sem, device):
+        pl.semaphore_signal(sem, inc=1, device_id=device, device_id_type=MESH)
+
+    def vouched(self, sem, count):
+        pl.semaphore_wait(sem, count)
+
     def start(self, source, target, send_sem, recv_sem, device):
         pltpu.make_async_remote_copy(
             src_ref=source, dst_ref=target, send_sem=send_sem, recv_sem=recv_sem,
@@ -1231,7 +1268,7 @@
             VMEM((OWNERS // 2 * LINES, 128), f32), VMEM((OWNERS // 2 * LINES, 128), f32),
             VMEM((6, 2, 128, 128), f32), VMEM((8, 128, 128), f32), VMEM((128, 128), f32), VMEM((128, 128), f32),
             VMEM((STEPS // 2, 128, 128), f32), VMEM((STEPS // 4, 4, 128, 128), f32), VMEM((128, 256), bf16),
-            dma((3, 8)), dma, dma((2,)), dma((8,)), dma, dma, dma,
+            pltpu.SemaphoreType.REGULAR, dma((3, 8)), dma, dma((2,)), dma((8,)), dma, dma, dma,
             dma, dma((STEPS // 4,)), dma, dma, dma, dma, dma, dma, dma,
         ],
         compiler_params=pltpu.CompilerParams(
@@ -1250,11 +1287,11 @@
     return pl.pallas_call(
         backward_kernel,
         out_shape=shape(4, WIDE, NZ, NY),
-        in_specs=[spec(ANY)] + [spec(VMEM)] * 3,
+        in_specs=[spec(ANY)] * 2 + [spec(VMEM)] * 2,
         out_specs=spec(ANY),
         scratch_shapes=[
-            VMEM((4, WIDE, NZ, NY), f32), VMEM((4, WIDE, NZ, NY), f32),
-            pltpu.SemaphoreType.DMA, pltpu.SemaphoreType.DMA((8,)),
+            VMEM((32, 128, 128), f32), VMEM((4, WIDE, NZ, NY), f32), VMEM((4, WIDE, NZ, NY), f32),
+            pltpu.SemaphoreType.DMA((3, 4)), pltpu.SemaphoreType.DMA((8,)),
         ],
         compiler_params=PARAMS,
         interpret=interpret,

time: 79.5 us -> 75.9 us (0.955)
  Pallas kernels: 79.3 us -> 75.8 us
    pallas_call x1, Pallas kernels: 72.4 us -> 69.5 us  [whole(): pl.pallas_call(functools.partial(whole_kernel, remote), out_shape=shape(3...]
where the time goes in v7:
time: 75.9 us; the launch traced here: 75.8 us
  Pallas kernels  75.8 us (100%)
    pallas_call x1, Pallas kernels, whole(): pl.pallas_call(functools.partial(whole_kernel, remote), out_shape=shape(3...  69.5 us
    pallas_call x1, Pallas kernels, backward(): pl.pallas_call(backward_kernel, out_shape=shape(4, WIDE, NZ, NY), in_spec...  6.31 us

profile of v7, /device:TPU:1, one launch (start us, length us, event | category | flops | bytes accessed | tf_op | source)
XLA Modules:
  0.0 75.8 jit_solution(580404415813624545)
XLA Ops:
  0.0 69.5 %whole.1.spec_hbm = f32[32,128,128]{2,1,0:T(8,128)} custom-call(f32[3]{0:T(128)} %velocity_ref.1, f32[4,16,64,128]{3,2,1,0:T(8,128)} %bitcast.3, f32[4,16,64,128]{3,2,1,0:T(8,128)} %bitcast.5, f32[16,64,128]{2,1,0:T(8,128)} %kappa_hbm.1, bf16[2,256,256]{2,1,0:T(8,128)(2,1)} %constant.24.clone.ty_ref, bf16[128,384]{1,0:T(8,128)(2,1)} %constant.25.clone.tz_ref, ...), custom_call_target="tpu_custom_call" | custom-call | tf_op jit(solution)/shard_map/whole/pallas_call | solution.py:1253
  69.5 6.3 %backward.1 = f32[4,16,64,128]{3,2,1,0:T(8,128)} custom-call(f32[4,16,64,128]{3,2,1,0:T(8,128)} %bitcast.4, f32[32,128,128]{2,1,0:T(8,128)} %whole.1.spec_hbm, bf16[2,256,256]{2,1,0:T(8,128)(2,1)} %constant.34.clone.uy_ref, bf16[128,384]{1,0:T(8,128)(2,1)} %constant.35.clone.uz_ref), custom_call_target="tpu_custom_call" | custom-call | tf_op jit(solution)/shard_map/backward/pallas_call | solution.py:1287

commit v8 on v7

--- a/solution.py
+++ b/solution.py
@@ -697,13 +697,13 @@
 
 def whole_kernel(
     remote, velocity_ref, iterate_hbm, right_hbm, kappa_hbm,
-    ty_ref, tz_ref, lane_ref, row_ref, own_ref, wave_ref, tg_ref, td_ref, tw_ref, tb_ref,
+    own_hbm, ty_ref, tz_ref, lane_ref, row_ref, wave_ref, tg_ref, td_ref, tw_ref, tb_ref,
     y_hbm,
     iterate_ref, right_ref, kappa_ref, y_ref,
     high_a, low_a, high_b, low_b, spec_ref, mixed_ref, below_ref, above_ref, sent_ref,
     chunk_out, chunk_in, chunk_back_out, chunk_back_in, returned_ref,
     got_ref, back_ref, damp_ref, ratio_ref, last_ref, mate_ref, drive_ref, kept_ref, turn_ref,
-    vouch_sem, load_sem, y_sem, chunk_out_sem, chunk_in_sem, edge_out_sem, below_sem, above_sem,
+    line_ref, line_sem, vouch_sem, load_sem, y_sem, chunk_out_sem, chunk_in_sem, edge_out_sem, below_sem, above_sem,
     gather_sem, arrive_sem, swap_out_sem, swap_in_sem, mate_out_sem, mate_in_sem,
     scatter_sem, return_sem, own_sem,
 ):
@@ -725,6 +725,9 @@
     for piece in range(8):
         for copy in loads(piece):
             copy.start()
+
+    line_load = remote.local(own_hbm.at[owner], line_ref, line_sem)
+    line_load.start()
 
     def ready(piece):
         for copy in loads(piece):
@@ -845,9 +848,10 @@
         def _():
             send_even(pair, space)
 
+    line_load.wait()
     solve_modes(
         remote, 2, owner, tm, space, rows_of,
-        velocity_ref, own_ref, wave_ref, tg_ref, td_ref, tw_ref, tb_ref, returned_ref,
+        velocity_ref, line_ref, wave_ref, tg_ref, td_ref, tw_ref, tb_ref, returned_ref,
         got_ref, back_ref, damp_ref, ratio_ref, last_ref, mate_ref, drive_ref, kept_ref, turn_ref,
         arrive_sem, swap_out_sem, swap_in_sem, mate_out_sem, mate_in_sem, scatter_sem, return_sem, own_sem,
     )
@@ -900,7 +904,8 @@
     remote.local(y_ref, y_hbm, y_sem).wait()
 
 
-GROUP = 2
+GROUP = 4
+TAIL = 2
 
 
 def solve_modes(
@@ -915,7 +920,7 @@
     pair = lax.div(tm, 2)
     at_home = lax.rem(pair, share) == core
     v0, v1, v2 = velocity_ref[0], velocity_ref[1], velocity_ref[2]
-    own = own_ref[owner]
+    own = own_ref[...]
     line = [own[k : k + 1, :] for k in range(8)]
     wide = [jnp.broadcast_to(v, (8, 128)) for v in line]
     sign = wide[6]
@@ -995,6 +1000,13 @@
 
     @pl.loop(0, rounds)
     def _(round_at):
+        if share > 1:
+
+            @pl.when(round_at > 0)
+            def _():
+                for k in range(GROUP):
+                    swap((round_at - 1) * GROUP + k)
+
         values, crossings = [], []
         for k in range(GROUP):
             at = pair_of(round_at * GROUP + k)
@@ -1073,11 +1085,6 @@
             drive_ref[at] = total
             before = wrapped(at - core, last_ref[...])
             last_ref[...] = total + times_lanes(before, (ratio_ref[6], ratio_ref[7]))
-        if share > 1:
-            @pl.when(round_at > 0)
-            def _():
-                for k in range(GROUP):
-                    swap((round_at - 1) * GROUP + k)
 
     if share > 1:
         mate = (tm + 1 - 2 * core, space)
@@ -1145,14 +1152,22 @@
         for place in places[1:]:
             put(place, remote.start, remote.start)
 
-    @pl.loop(0, rounds)
+    tail_rounds = pairs // share // TAIL
+
+    @pl.loop(0, tail_rounds)
     def _(round_at):
+        @pl.when(round_at > 0)
+        def _():
+            @pl.loop(0, TAIL)
+            def _(k):
+                send((round_at - 1) * TAIL + k)
+
         inputs = []
         last = last_ref[...]
-        for k in range(GROUP):
+        for k in range(TAIL):
             mine = None
             for c in range(share):
-                at = lax.rem(first_pair + share * (round_at * GROUP + k) + c, pairs)
+                at = lax.rem(first_pair + share * (round_at * TAIL + k) + c, pairs)
                 last = wrapped(at, last)
                 mine = last if mine is None else jnp.where(core == c, last, mine)
                 last = following(at, last)
@@ -1160,15 +1175,15 @@
         last_ref[...] = last
         packed = left_dot(tw_ref[...], jnp.concatenate([both_parts(v) for v in inputs], axis=1))
         lines = []
-        for k in range(GROUP):
-            slot = lax.div(pair_of(round_at * GROUP + k), share)
+        for k in range(TAIL):
+            slot = lax.div(pair_of(round_at * TAIL + k), share)
             for step, v in enumerate((inputs[k], times_refs(inputs[k], ratio))):
                 for m in range(2):
                     y = times_lanes(v, (damp_ref[4 + m, 0], damp_ref[4 + m, 1]))
                     lines.append(both_parts(y + kept_ref[slot, 2 * step + m]))
         ends = left_dot(tb_ref[...], jnp.concatenate(lines, axis=1))
-        for k in range(GROUP):
-            top = lax.div(pair_of(round_at * GROUP + k), share) * (SLABS * LINES)
+        for k in range(TAIL):
+            top = lax.div(pair_of(round_at * TAIL + k), share) * (SLABS * LINES)
             for x in range(SLABS):
                 back_ref[pl.ds(top + x * LINES, 8), :] = packed[8 * x : 8 * x + 8, 128 * k : 128 * k + 128]
             for step in range(2):
@@ -1180,15 +1195,9 @@
                     back_ref[pl.ds(line, SLABS, stride=LINES), :] = u
                     back_ref[pl.ds(line + 1, SLABS, stride=LINES), :] = part[2]
 
-        @pl.when(round_at > 0)
-        def _():
-            @pl.loop(0, GROUP)
-            def _(k):
-                send((round_at - 1) * GROUP + k)
-
-    @pl.loop(0, GROUP)
+    @pl.loop(0, TAIL)
     def _(k):
-        send((rounds - 1) * GROUP + k)
+        send((tail_rounds - 1) * TAIL + k)
 
     if share > 1:
         remote.wait_sent(drive_ref.at[pl.ds(0, pairs // 2)], swap_out_sem)
@@ -1253,7 +1262,7 @@
     return pl.pallas_call(
         functools.partial(whole_kernel, remote),
         out_shape=shape(32, 128, 128),
-        in_specs=[spec(SMEM)] + [spec(ANY)] * 3 + [spec(VMEM)] * 10,
+        in_specs=[spec(SMEM)] + [spec(ANY)] * 4 + [spec(VMEM)] * 9,
         out_specs=spec(ANY),
         scratch_shapes=[
             VMEM((4, WIDE, NZ, NY), f32), VMEM((4, WIDE, NZ, NY), f32), VMEM((WIDE, NZ, NY), f32),
@@ -1268,7 +1277,7 @@
             VMEM((OWNERS // 2 * LINES, 128), f32), VMEM((OWNERS // 2 * LINES, 128), f32),
             VMEM((6, 2, 128, 128), f32), VMEM((8, 128, 128), f32), VMEM((128, 128), f32), VMEM((128, 128), f32),
             VMEM((STEPS // 2, 128, 128), f32), VMEM((STEPS // 4, 4, 128, 128), f32), VMEM((128, 256), bf16),
-            pltpu.SemaphoreType.REGULAR, dma((3, 8)), dma, dma((2,)), dma((8,)), dma, dma, dma,
+            VMEM((8, 128), f32), dma, pltpu.SemaphoreType.REGULAR, dma((3, 8)), dma, dma((2,)), dma((8,)), dma, dma, dma,
             dma, dma((STEPS // 4,)), dma, dma, dma, dma, dma, dma, dma,
         ],
         compiler_params=pltpu.CompilerParams(
@@ -1278,7 +1287,7 @@
         name="whole",
     )(
         velocity, iterate, right_side, kappa,
-        TABLES["ty"], TABLES["tz"], TABLES["lane"], TABLES["row"], TABLES["own"], TABLES["wave_x"],
+        TABLES["own"], TABLES["ty"], TABLES["tz"], TABLES["lane"], TABLES["row"], TABLES["wave_x"],
         TABLES["tg"], TABLES["td"], TABLES["tw"], TABLES["tb"],
     )
 

time: 75.9 us -> 74.2 us (0.978)
  Pallas kernels: 75.8 us -> 74.1 us
    pallas_call x1, Pallas kernels: 69.5 us -> 67.7 us  [whole(): pl.pallas_call(functools.partial(whole_kernel, remote), out_shape=shape(3...]
where the time goes in v8:
time: 74.2 us; the launch traced here: 74.1 us
  Pallas kernels  74.1 us (100%)
    pallas_call x1, Pallas kernels, whole(): pl.pallas_call(functools.partial(whole_kernel, remote), out_shape=shape(3...  67.7 us
    pallas_call x1, Pallas kernels, backward(): pl.pallas_call(backward_kernel, out_shape=shape(4, WIDE, NZ, NY), in_spec...  6.32 us

profile of v8, /device:TPU:1, one launch (start us, length us, event | category | flops | bytes accessed | tf_op | source)
XLA Modules:
  0.0 74.1 jit_solution(3338146906097382503)
XLA Ops:
  0.0 67.7 %whole.1.spec_hbm = f32[32,128,128]{2,1,0:T(8,128)} custom-call(f32[3]{0:T(128)} %velocity_ref.1, f32[4,16,64,128]{3,2,1,0:T(8,128)} %bitcast.3, f32[4,16,64,128]{3,2,1,0:T(8,128)} %bitcast.5, f32[16,64,128]{2,1,0:T(8,128)} %kappa_hbm.1, f32[128,8,128]{2,1,0:T(8,128)} %constant.24.clone.own_hbm, bf16[2,256,256]{2,1,0:T(8,128)(2,1)} %constant.25.clone.ty_ref, ...), custom_call_target="tpu_custom_call" | custom-call | tf_op jit(solution)/shard_map/whole/pallas_call | solution.py:1262
  67.8 6.3 %backward.1 = f32[4,16,64,128]{3,2,1,0:T(8,128)} custom-call(f32[4,16,64,128]{3,2,1,0:T(8,128)} %bitcast.4, f32[32,128,128]{2,1,0:T(8,128)} %whole.1.spec_hbm, bf16[2,256,256]{2,1,0:T(8,128)(2,1)} %constant.34.clone.uy_ref, bf16[128,384]{1,0:T(8,128)(2,1)} %constant.35.clone.uz_ref), custom_call_target="tpu_custom_call" | custom-call | tf_op jit(solution)/shard_map/backward/pallas_call | solution.py:1296

commit v9 on v8

--- a/solution.py
+++ b/solution.py
@@ -503,7 +503,7 @@
         spec_ref[40 + k] = out[:, 128 * k : 128 * k + 128]
 
 
-def slab_stage(odd, begin, velocity_ref, spec_ref, lane_ref, row_ref, y_ref, send_ref, chunk_ref):
+def slab_stage(odd, begin, velocity_ref, spec_ref, lane_ref, row_ref, y_ref, send_ref, chunk_ref, factor_ref):
     lane = lax.broadcasted_iota(jnp.int32, (8, 128), 1)
     sub = lax.broadcasted_iota(jnp.int32, (8, 128), 0)
     block = lane // 32
@@ -514,6 +514,11 @@
         first_row = (sub + t) == 0
         found = chunk_factors(t, lane_ref, row_ref, velocity_ref, MU)
         bases = [pl.multiple_of(base + 8 * t, 8) for base in (0, 32)]
+        for half in range(2):
+            for m in range(2):
+                for k, j in enumerate((0, 1, 3)):
+                    for part in range(2):
+                        factor_ref[m * 6 + 2 * k + part, pl.ds(bases[half], 8), :] = found[half][m][j][part]
         if odd:
             last = unpacked_planes(lambda x: get_chunk(chunk_ref, t, x), lane, first_row)
 
@@ -561,7 +566,7 @@
                 put_chunk(chunk_ref, t, x, packed[0], packed[1])
 
 
-def finish_stage(odd, begin, velocity_ref, lane_ref, row_ref, y_ref, got_ref, chunk_ref):
+def finish_stage(odd, begin, y_ref, got_ref, chunk_ref, factor_ref):
     lane = lax.broadcasted_iota(jnp.int32, (8, 128), 1)
     sub = lax.broadcasted_iota(jnp.int32, (8, 128), 0)
     block = lane // 32
@@ -570,7 +575,6 @@
     def _(t):
         begin(t)
         first_row = (sub + t) == 0
-        found = chunk_factors(t, lane_ref, row_ref, velocity_ref, MU)
         bases = [pl.multiple_of(base + 8 * t, 8) for base in (0, 32)]
 
         def take(value):
@@ -587,7 +591,10 @@
             start, end = take(8 + m * 2), take(9 + m * 2)
             for half in range(2):
                 base = bases[half]
-                p, q, kappa, inv = found[half][m]
+                p, q, inv = [
+                    tuple(factor_ref[m * 6 + 2 * k + part, pl.ds(base, 8), :] for part in range(2))
+                    for k in range(3)
+                ]
                 u = start[half]
                 us = [u]
                 for x in range(1, WIDE - 1):
@@ -660,8 +667,9 @@
 
     pending = None
     for group in range(4):
-        for copy in loads(group):
-            copy.wait()
+        if group % 2 == 0:
+            for copy in loads(group) + loads(group + 1):
+                copy.wait()
         blocks = (2 * group, 2 * group + 1)
         outs = [finished(block) for block in blocks]
         if pending is not None:
@@ -703,7 +711,7 @@
     high_a, low_a, high_b, low_b, spec_ref, mixed_ref, below_ref, above_ref, sent_ref,
     chunk_out, chunk_in, chunk_back_out, chunk_back_in, returned_ref,
     got_ref, back_ref, damp_ref, ratio_ref, last_ref, mate_ref, drive_ref, kept_ref, turn_ref,
-    line_ref, line_sem, vouch_sem, load_sem, y_sem, chunk_out_sem, chunk_in_sem, edge_out_sem, below_sem, above_sem,
+    line_ref, factor_ref, line_sem, vouch_sem, load_sem, y_sem, chunk_out_sem, chunk_in_sem, edge_out_sem, below_sem, above_sem,
     gather_sem, arrive_sem, swap_out_sem, swap_in_sem, mate_out_sem, mate_in_sem,
     scatter_sem, return_sem, own_sem,
 ):
@@ -795,7 +803,7 @@
 
     stage(
         lambda odd, begin, ref: slab_stage(
-            odd, begin, velocity_ref, spec_ref, lane_ref, row_ref, y_ref, sent_ref, ref
+            odd, begin, velocity_ref, spec_ref, lane_ref, row_ref, y_ref, sent_ref, ref, factor_ref
         ),
         chunk_out, chunk_in, 0, lambda t: None,
     )
@@ -889,7 +897,7 @@
 
     stage(
         lambda odd, begin, ref: finish_stage(
-            odd, begin, velocity_ref, lane_ref, row_ref, y_ref, returned_ref, ref
+            odd, begin, y_ref, returned_ref, ref, factor_ref
         ),
         chunk_back_out, chunk_back_in, 4, store_before,
     )
@@ -1277,7 +1285,7 @@
             VMEM((OWNERS // 2 * LINES, 128), f32), VMEM((OWNERS // 2 * LINES, 128), f32),
             VMEM((6, 2, 128, 128), f32), VMEM((8, 128, 128), f32), VMEM((128, 128), f32), VMEM((128, 128), f32),
             VMEM((STEPS // 2, 128, 128), f32), VMEM((STEPS // 4, 4, 128, 128), f32), VMEM((128, 256), bf16),
-            VMEM((8, 128), f32), dma, pltpu.SemaphoreType.REGULAR, dma((3, 8)), dma, dma((2,)), dma((8,)), dma, dma, dma,
+            VMEM((8, 128), f32), VMEM((12, NZ, NY), f32), dma, pltpu.SemaphoreType.REGULAR, dma((3, 8)), dma, dma((2,)), dma((8,)), dma, dma, dma,
             dma, dma((STEPS // 4,)), dma, dma, dma, dma, dma, dma, dma,
         ],
         compiler_params=pltpu.CompilerParams(

time: 74.2 us -> 73.9 us (level)
  no operation moved by 1% of the time
where the time goes in v9:
time: 73.9 us; the launch traced here: 73.8 us
  Pallas kernels  73.8 us (100%)
    pallas_call x1, Pallas kernels, whole(): pl.pallas_call(functools.partial(whole_kernel, remote), out_shape=shape(3...  67.8 us
    pallas_call x1, Pallas kernels, backward(): pl.pallas_call(backward_kernel, out_shape=shape(4, WIDE, NZ, NY), in_spec...  6.03 us

profile of v9, /device:TPU:1, one launch (start us, length us, event | category | flops | bytes accessed | tf_op | source)
XLA Modules:
  0.0 73.8 jit_solution(17480237562351164076)
XLA Ops:
  0.0 67.8 %whole.1.spec_hbm = f32[32,128,128]{2,1,0:T(8,128)} custom-call(f32[3]{0:T(128)} %velocity_ref.1, f32[4,16,64,128]{3,2,1,0:T(8,128)} %bitcast.3, f32[4,16,64,128]{3,2,1,0:T(8,128)} %bitcast.5, f32[16,64,128]{2,1,0:T(8,128)} %kappa_hbm.1, f32[128,8,128]{2,1,0:T(8,128)} %constant.24.clone.own_hbm, bf16[2,256,256]{2,1,0:T(8,128)(2,1)} %constant.25.clone.ty_ref, ...), custom_call_target="tpu_custom_call" | custom-call | tf_op jit(solution)/shard_map/whole/pallas_call | solution.py:1270
  67.8 6.0 %backward.1 = f32[4,16,64,128]{3,2,1,0:T(8,128)} custom-call(f32[4,16,64,128]{3,2,1,0:T(8,128)} %bitcast.4, f32[32,128,128]{2,1,0:T(8,128)} %whole.1.spec_hbm, bf16[2,256,256]{2,1,0:T(8,128)(2,1)} %constant.34.clone.uy_ref, bf16[128,384]{1,0:T(8,128)(2,1)} %constant.35.clone.uz_ref), custom_call_target="tpu_custom_call" | custom-call | tf_op jit(solution)/shard_map/backward/pallas_call | solution.py:1304
